TPU v7x, 32 devices: a whole 2x2x4 slice. The times are simulated.
32 devices in a mesh: gx: 4 (over y, core), gy: 8 (over z, x).
Axes of the slice: x: 2, y: 2, z: 4, core: 2. Of those that a mesh axis runs over, the one named last changes fastest.
Arguments:
- q_now: float32 [5, 64, 128, 256], P(None, 'gx', 'gy'), may hold values from -6 to 6
- q_prev: float32 [5, 64, 128, 256], P(None, 'gx', 'gy'), may hold values from -6 to 6
- jacobian: float32 [64, 128, 256], P('gx', 'gy'), may hold values from 0.5 to 2
- flux_split: float32 [3, 2, 5, 5], replicated, may hold values from -2 to 2
- donor_base: int32 [32768], P(('gx', 'gy')), may hold values from 0 to 57374
- donor_frac: float32 [3, 32768], P(None, ('gx', 'gy')), may hold values from 0 to 1
- fringe_dest: int32 [32768, 1], P(('gx', 'gy')), may hold values from 0 to 31; in each aligned block of 1024 rows (0 to 1023, 1024 to 2047, ...) at most 64 rows name the same one
- receptor_cell: int32 [32768], P(('gx', 'gy')), may hold values from 0 to 65535
- fringe_count: int32 [32], P(('gx', 'gy')), may hold values from 1 to 1024, 24576 in all
Outputs:
- q_next: float32 [5, 64, 128, 256], P(None, 'gx', 'gy')
Inputs may be any that keep to these rules, and one draw needn't show every extreme that they name: `fringe_dest`: among the 1024 rows of one block, at most 64 name the same destination block; some block sends exactly 64 to one destination. A block's live rows are its first fringe_count rows; the counts sum to 24576 and some block has 1024. `receptor_cell`: several rows may share a receptor cell.
All inputs are finite; a program needn't handle non-finite values.
Results may differ from a plain program's by a relative error of at most 0.0003.
Values sent between devices are 32-bit elements; how exact they have to be, the bound alone decides.
No kernel may reach another device: no remote copies, remote signals or barrier semaphores. Data moves between devices by JAX's collectives and lax.ppermute only.
A program may use at most 192 MiB of HBM per device.

v0:
```python
import functools

import jax
import jax.numpy as jnp
from jax import lax
from jax.experimental import pallas as pl
from jax.experimental.pallas import tpu as pltpu
from jax.sharding import PartitionSpec as P

step_tau = 0.2
step_phys = 0.5
penalty = 2.0

AXES = ("gx", "gy")
LANES = 256
CHANNELS = 16
MIB = 1 << 20


def iota(shape, dim):
    return lax.broadcasted_iota(jnp.int32, shape, dim)


def dot(a, b, dims):
    return lax.dot_general(a, b, (dims, ((), ())), preferred_element_type=jnp.float32)


def halves(x):
    high = x.astype(jnp.bfloat16)
    return high, (x - high.astype(jnp.float32)).astype(jnp.bfloat16)


def ranks(dest, devices):
    rows = dest.shape[1]
    blocks = rows // LANES
    hot = (iota((devices, rows), 0) == dest).astype(jnp.float32)
    stacked = jnp.concatenate([hot[:, b * LANES : (b + 1) * LANES] for b in range(blocks)], axis=0)
    before = (iota((LANES, LANES), 0) < iota((LANES, LANES), 1)).astype(jnp.float32)
    local = dot(stacked.astype(jnp.bfloat16), before.astype(jnp.bfloat16), ((1,), (0,)))
    carried = jnp.zeros((devices, 1), jnp.float32)
    pieces = []
    for b in range(blocks):
        part = local[b * devices : (b + 1) * devices]
        own = hot[:, b * LANES : (b + 1) * LANES]
        pieces.append(jnp.sum((part + carried) * own, axis=0, keepdims=True))
        carried = carried + jnp.sum(own, axis=1, keepdims=True)
    return jnp.concatenate(pieces, axis=1)


def donor_kernel(count, q_prev, q_now, base, frac, dest, cell, out, planes, lhs, spread, corner, place, values, sems, *, size, devices, capacity):
    nvars, size_x, size_y, size_z = size
    columns = size_x * size_y
    rows = base.shape[1]
    copies = []
    for k, ref in enumerate((q_prev, q_now)):
        copies.append(pltpu.make_async_copy(ref, planes.at[k], sems.at[k]))
        copies[-1].start()
    start = base[...].astype(jnp.float32)
    in_y = jnp.floor((start + 0.5) * (1.0 / (size_z - 1)))
    base_z = start - in_y * (size_z - 1)
    base_x = jnp.floor((in_y + 0.5) * (1.0 / (size_y - 1)))
    base_y = in_y - base_x * (size_y - 1)
    frac_x, frac_y, frac_z = frac[0:1, :], frac[1:2, :], frac[2:3, :]

    def weights(first, part, shape):
        at = iota(shape, 0).astype(jnp.float32) - first
        return jnp.where(at == 0.0, 1.0 - part, jnp.where(at == 1.0, part, 0.0))

    along_z = weights(base_z, frac_z, (size_z, rows))
    high, low = halves(along_z)
    spread[0:size_z, :] = high
    spread[size_z : 2 * size_z, :] = low
    spread[2 * size_z : 3 * size_z, :] = high
    along_x = weights(base_x, frac_x, (size_x, rows))
    along_y = weights(base_y, frac_y, (size_y, rows))
    for x in range(size_x):
        corner[x * size_y : (x + 1) * size_y, :] = along_x[x : x + 1, :] * along_y
    alive = iota((1, rows), 1) < count[0]
    slot = ranks(dest[...], devices)
    where_to = jnp.where(alive, dest[...].astype(jnp.float32) * capacity + slot, -1.0)
    place[...] = jnp.transpose(jnp.broadcast_to(where_to, (8, rows)))
    landing = cell[...].astype(jnp.float32)
    land_xy = jnp.floor((landing + 0.5) * (1.0 / size_z))
    values[...] = jnp.zeros(values.shape, jnp.float32)
    values[2 * nvars : 2 * nvars + 1, :] = land_xy + 1.0
    values[2 * nvars + 1 : 2 * nvars + 2, :] = landing - land_xy * size_z
    for k in range(2):
        copies[k].wait()
        for v in range(nvars):
            at = pl.ds((k * nvars + v) * columns, columns)
            high, low = halves(planes[k, v])
            lhs[at, 0:size_z] = high
            lhs[at, size_z : 2 * size_z] = high
            lhs[at, 2 * size_z : 3 * size_z] = low
    for n in range(rows // LANES):
        lanes = slice(n * LANES, (n + 1) * LANES)
        for k in range(2):
            part = dot(lhs[k * nvars * columns : (k + 1) * nvars * columns, :], spread[:, lanes], ((1,), (0,)))
            for v in range(nvars):
                picked = part[v * columns : (v + 1) * columns] * corner[:, lanes]
                values[k * nvars + v : k * nvars + v + 1, lanes] = jnp.sum(picked, axis=0, keepdims=True)
    first = values[...]
    high, rest = first.astype(jnp.bfloat16), None
    rest = first - high.astype(jnp.float32)
    middle = rest.astype(jnp.bfloat16)
    last = (rest - middle.astype(jnp.float32)).astype(jnp.bfloat16)
    three = jnp.concatenate([high, middle, last], axis=0)
    column = jnp.broadcast_to(place[:, 0:1], (rows, LANES))
    for n in range(devices * capacity // LANES):
        chosen = (column == (iota((rows, LANES), 1) + n * LANES).astype(jnp.float32)).astype(jnp.float32).astype(jnp.bfloat16)
        moved = dot(three, chosen, ((1,), (0,)))
        moved = moved[0:CHANNELS] + moved[CHANNELS : 2 * CHANNELS] + moved[2 * CHANNELS : 3 * CHANNELS]
        for d in range(LANES // capacity):
            piece = moved[:, d * capacity : (d + 1) * capacity]
            to = n * (LANES // capacity) + d
            out[to] = jnp.concatenate([piece[0:8], piece[8:16]], axis=1)


def flux_of(coef, centre, neighbours):
    nvars = len(centre)
    total = [None] * nvars
    for d, (behind, ahead) in enumerate(neighbours):
        for side in range(2):
            moved = [c - b for c, b in zip(centre, behind)] if side == 0 else [f - c for c, f in zip(centre, ahead)]
            for a in range(nvars):
                for b in range(nvars):
                    term = coef[((d * 2 + side) * nvars + a) * nvars + b] * moved[b]
                    total[a] = term if total[a] is None else total[a] + term
    return total


def neighbours_at(x, state, x_low, x_high, y_low, y_high, size):
    nvars, size_x, size_y, size_z = size
    rows_at = iota((size_y, size_z), 0)
    z_at = iota((size_y, size_z), 1)
    centre = [state[v, x] for v in range(nvars)]
    back_x = [jnp.where(x == 0, x_low[v], state[v, jnp.maximum(x - 1, 0)]) for v in range(nvars)]
    fore_x = [jnp.where(x == size_x - 1, x_high[v], state[v, jnp.minimum(x + 1, size_x - 1)]) for v in range(nvars)]
    back_y = [jnp.where(rows_at == 0, y_low[v, pl.ds(x, 1), :], pltpu.roll(centre[v], 1, 0)) for v in range(nvars)]
    fore_y = [jnp.where(rows_at == size_y - 1, y_high[v, pl.ds(x, 1), :], pltpu.roll(centre[v], size_y - 1, 0)) for v in range(nvars)]
    back_z = [jnp.where(z_at == 0, 0.0, pltpu.roll(centre[v], 1, 1)) for v in range(nvars)]
    fore_z = [jnp.where(z_at == size_z - 1, 0.0, pltpu.roll(centre[v], size_z - 1, 1)) for v in range(nvars)]
    return centre, [(back_x, fore_x), (back_y, fore_y), (back_z, fore_z)]


def first_kernel(coef, q_now, q_prev, jac, got, x_low, x_high, y_low, y_high, state, target, hits, face_xl, face_xh, face_yl, face_yh, rows, grid, *, size, devices, capacity):
    nvars, size_x, size_y, size_z = size
    columns = size_x * size_y
    for d in range(devices):
        piece = got[d]
        lanes = slice(d * capacity, (d + 1) * capacity)
        rows[0:8, lanes] = piece[:, 0:capacity]
        rows[8:16, lanes] = piece[:, capacity : 2 * capacity]
    grid[...] = jnp.zeros(grid.shape, jnp.float32)
    place_xy = (iota((columns, LANES), 0) + 1).astype(jnp.float32)
    place_z = iota((size_z, LANES), 0).astype(jnp.float32)

    def chunk(n, carry):
        block = rows[:, pl.ds(pl.multiple_of(n * LANES, LANES), LANES)]
        hot_xy = (place_xy == block[2 * nvars : 2 * nvars + 1]).astype(jnp.float32).astype(jnp.bfloat16)
        hot_z = (place_z == block[2 * nvars + 1 : 2 * nvars + 2]).astype(jnp.float32).astype(jnp.bfloat16)
        high, low = halves(block[0 : 2 * nvars])
        pieces = []
        for c in range(2 * nvars):
            pieces += [hot_xy * high[c : c + 1], hot_xy * low[c : c + 1]]
        pieces.append(hot_xy)
        landed = dot(jnp.concatenate(pieces, axis=0), hot_z, ((1,), (1,)))
        for c in range(2 * nvars):
            at = 2 * c * columns
            grid[c] = grid[c] + (landed[at : at + columns] + landed[at + columns : at + 2 * columns])
        grid[2 * nvars] = grid[2 * nvars] + landed[4 * nvars * columns :]
        return carry

    lax.fori_loop(0, devices * capacity // LANES, chunk, 0)
    target[...] = grid[nvars : 2 * nvars]
    hits[...] = grid[2 * nvars]

    def plane(x, carry):
        at = pl.ds(pl.multiple_of(x * size_y, size_y), size_y)
        centre, around = neighbours_at(x, q_now, x_low, x_high, y_low, y_high, size)
        flux = flux_of(coef, centre, around)
        landed = grid[2 * nvars, at, :]
        scale = step_tau * jac[x]
        for v in range(nvars):
            physical = (3.0 * centre[v] - 4.0 * centre[v] + q_prev[v, x]) / (2.0 * step_phys)
            coupling = penalty * (landed * centre[v] - grid[v, at, :])
            new = centre[v] - scale * (flux[v] + physical + coupling)
            state[v, x] = new
            face_yl[v, pl.ds(x, 1), :] = new[0:1]
            face_yh[v, pl.ds(x, 1), :] = new[size_y - 1 : size_y]
        return carry

    lax.fori_loop(0, size_x, plane, 0)
    face_xl[...] = state[:, 0]
    face_xh[...] = state[:, size_x - 1]


def second_kernel(coef, state, q_now, q_prev, jac, target, hits, x_low, x_high, y_low, y_high, out, *, size):
    nvars, size_x, size_y, size_z = size

    def plane(x, carry):
        at = pl.ds(pl.multiple_of(x * size_y, size_y), size_y)
        centre, around = neighbours_at(x, state, x_low, x_high, y_low, y_high, size)
        flux = flux_of(coef, centre, around)
        landed = hits[at, :]
        scale = step_tau * jac[x]
        for v in range(nvars):
            physical = (3.0 * centre[v] - 4.0 * q_now[v, x] + q_prev[v, x]) / (2.0 * step_phys)
            coupling = penalty * (landed * centre[v] - target[v, at, :])
            out[v, x] = centre[v] - scale * (flux[v] + physical + coupling)
        return carry

    lax.fori_loop(0, size_x, plane, 0)


def swap_pairs(axis, odd):
    count = lax.axis_size(axis)
    pairs = []
    for i in range(odd, count - 1, 2):
        pairs += [(i, i + 1), (i + 1, i)]
    return pairs


def exchanged(low_face, high_face, axis):
    here = lax.axis_index(axis)
    even = here % 2 == 0
    inner = lax.ppermute(jnp.where(even, high_face, low_face), axis, swap_pairs(axis, 0))
    outer = lax.ppermute(jnp.where(even, low_face, high_face), axis, swap_pairs(axis, 1))
    return jnp.where(even, outer, inner), jnp.where(even, inner, outer)


def params(limit):
    return pltpu.CompilerParams(vmem_limit_bytes=limit * MIB)


def body(q_now, q_prev, jacobian, flux_split, donor_base, donor_frac, fringe_dest, receptor_cell, fringe_count):
    size = q_now.shape
    nvars, size_x, size_y, size_z = size
    columns = size_x * size_y
    devices = lax.axis_size("gx") * lax.axis_size("gy")
    rows = donor_base.shape[0]
    capacity = 2 * rows // devices
    slots = devices * capacity
    f32, bf16 = jnp.float32, jnp.bfloat16
    smem = pl.BlockSpec(memory_space=pltpu.SMEM)
    hbm = pl.BlockSpec(memory_space=pl.ANY)
    vmem = pl.BlockSpec(memory_space=pltpu.VMEM)
    coef = flux_split.reshape(-1)
    flat = (nvars, columns, size_z)
    sent = pl.pallas_call(
        functools.partial(donor_kernel, size=size, devices=devices, capacity=capacity),
        out_shape=jax.ShapeDtypeStruct((devices, 8, 2 * capacity), f32),
        in_specs=[smem, hbm, hbm, vmem, vmem, vmem, vmem],
        out_specs=vmem,
        scratch_shapes=[
            pltpu.VMEM((2, nvars, columns, size_z), f32),
            pltpu.VMEM((2 * nvars * columns, 3 * size_z), bf16),
            pltpu.VMEM((3 * size_z, rows), bf16),
            pltpu.VMEM((columns, rows), f32),
            pltpu.VMEM((rows, 8), f32),
            pltpu.VMEM((CHANNELS, rows), f32),
            pltpu.SemaphoreType.DMA((2,)),
        ],
        compiler_params=params(48),
        name="donor",
    )(
        fringe_count,
        q_prev.reshape(flat),
        q_now.reshape(flat),
        donor_base.reshape(1, rows),
        donor_frac,
        fringe_dest.reshape(1, rows),
        receptor_cell.reshape(1, rows),
    )
    got = lax.all_to_all(sent, AXES, split_axis=0, concat_axis=0, tiled=True)
    x_halo = exchanged(q_now[:, 0], q_now[:, size_x - 1], "gx")
    y_halo = exchanged(q_now[:, :, 0], q_now[:, :, size_y - 1], "gy")
    face_x = jax.ShapeDtypeStruct((nvars, size_y, size_z), f32)
    face_y = jax.ShapeDtypeStruct((nvars, size_x, size_z), f32)

    def edges(halo, axis):
        here, last = lax.axis_index(axis), lax.axis_size(axis) - 1
        return jnp.where(here == 0, 0.0, halo[0]), jnp.where(here == last, 0.0, halo[1])

    x_halo, y_halo = edges(x_halo, "gx"), edges(y_halo, "gy")
    state, target, hits, *faces = pl.pallas_call(
        functools.partial(first_kernel, size=size, devices=devices, capacity=capacity),
        out_shape=[
            jax.ShapeDtypeStruct(size, f32),
            jax.ShapeDtypeStruct(flat, f32),
            jax.ShapeDtypeStruct((columns, size_z), f32),
            face_x,
            face_x,
            face_y,
            face_y,
        ],
        in_specs=[smem] + [vmem] * 8,
        out_specs=[vmem] * 7,
        scratch_shapes=[pltpu.VMEM((CHANNELS, slots), f32), pltpu.VMEM((2 * nvars + 1, columns, size_z), f32)],
        compiler_params=params(48),
        name="first",
    )(coef, q_now, q_prev, jacobian, got, *x_halo, *y_halo)
    x_halo = edges(exchanged(faces[0], faces[1], "gx"), "gx")
    y_halo = edges(exchanged(faces[2], faces[3], "gy"), "gy")
    return pl.pallas_call(
        functools.partial(second_kernel, size=size),
        out_shape=jax.ShapeDtypeStruct(size, f32),
        in_specs=[smem] + [vmem] * 10,
        out_specs=vmem,
        compiler_params=params(48),
        name="second",
    )(coef, state, q_now, q_prev, jacobian, target, hits, *x_halo, *y_halo)


def solution(mesh):
    return jax.shard_map(
        body,
        mesh=mesh,
        in_specs=(
            P(None, "gx", "gy", None),
            P(None, "gx", "gy", None),
            P("gx", "gy", None),
            P(),
            P(("gx", "gy")),
            P(None, ("gx", "gy")),
            P(("gx", "gy"), None),
            P(("gx", "gy")),
            P(("gx", "gy")),
        ),
        out_specs=P(None, "gx", "gy", None),
        check_vma=False,
    )
```

profile of v0, /device:TPU:9, one launch (start us, length us, event | category | flops | bytes accessed | tf_op | source)
XLA Modules:
  0.0 61.3 jit_solution(5446344263330332406)
XLA Ops:
  0.7 0.0 copy-start
  0.7 1.3 %copy-done = f32[5,16,16,256]{3,2,1,0:T(8,128)S(1)} copy-done((f32[5,16,16,256]{3,2,1,0:T(8,128)S(1)}, f32[5,16,16,256]{3,2,1,0:T(8,128)}, u32[]{:S(2)}) %copy-start) | copy-done | bytes 1310744
  2.0 0.0 copy-start.2
  2.0 1.3 %copy-done.2 = f32[5,16,16,256]{3,2,1,0:T(8,128)S(1)} copy-done((f32[5,16,16,256]{3,2,1,0:T(8,128)S(1)}, f32[5,16,16,256]{3,2,1,0:T(8,128)}, u32[]{:S(2)}) %copy-start.2) | copy-done | bytes 1310744
  3.3 0.0 copy-start.5
  3.3 0.7 %copy-done.5 = f32[3,1024]{1,0:T(4,128)S(1)} copy-done((f32[3,1024]{1,0:T(4,128)S(1)}, f32[3,1024]{1,0:T(4,128)}, u32[]{:S(2)}) %copy-start.5) | copy-done | bytes 12312
  4.0 0.0 copy-start.6
  4.0 0.7 %copy-done.6 = s32[1024]{0:T(1024)S(1)} copy-done((s32[1024]{0:T(1024)S(1)}, s32[1024]{0:T(1024)}, u32[]{:S(2)}) %copy-start.6) | copy-done | bytes 4120
  4.7 0.0 copy-start.7
  4.7 0.7 %copy-done.7 = s32[1024,1]{0,1:T(1,128)S(1)} copy-done((s32[1024,1]{0,1:T(1,128)S(1)}, s32[1024,1]{0,1:T(1,128)}, u32[]{:S(2)}) %copy-start.7) | copy-done | bytes 4120
  5.4 0.0 copy-start.8
  5.4 0.7 %copy-done.8 = s32[1024]{0:T(1024)S(1)} copy-done((s32[1024]{0:T(1024)S(1)}, s32[1024]{0:T(1024)}, u32[]{:S(2)}) %copy-start.8) | copy-done | bytes 4120
  6.1 0.0 copy-start.1
  6.1 6.8 %donor.1 = f32[32,8,128]{2,1,0:T(8,128)} custom-call(s32[1]{0:T(128)S(6)} %copy.27.count, f32[5,256,256]{2,1,0:T(8,128)S(1)} %bitcast.24, f32[5,256,256]{2,1,0:T(8,128)S(1)} %bitcast.23, s32[1,1024]{1,0:T(1,128)S(1)} %bitcast.25, f32[3,1024]{1,0:T(4,128)S(1)} %copy-done.5, s32[1,1024]{1,0:T(1,128)S(1)} %bitcast.26, s32[1,1024]{1,0:T(1,128)S(1)} %bitcast.27), custom_call_target="tpu_custom_call" | custom-call | tf_op jit(solution)/shard_map/donor/pallas_call | solution.py:250
  12.8 0.0 copy-start.9
  12.9 0.0 copy-start.4
  12.9 6.3 %all-to-all-start = ((f32[32,8,128]{2,1,0:T(8,128)}), f32[32,8,128]{2,1,0:T(8,128)S(1)}, u32[]{:S(2)}, u32[]{:S(2)}) async-start(f32[32,8,128]{2,1,0:T(8,128)} %donor.1), calls=%async_computation | async-start | bytes 262144 | tf_op jit(solution)/shard_map/all_to_all | solution.py:275
  19.2 0.0 copy-done.1
  19.3 0.5 collective-permute-start.1
  19.7 3.1 %collective-permute-start = (f32[5,16,256]{2,1,0:T(8,128)S(1)}, f32[5,16,256]{2,1,0:T(8,128)S(1)}, u32[]{:S(2)}, u32[]{:S(2)}) collective-permute-start(f32[5,16,256]{2,1,0:T(8,128)S(1)} %get-tuple-element.22), channel_id=1, source_target_pairs={{8,16},{16,8},{9,17},{17,9},{10,18},{18,10},{11,19},{19,11},{12,20... | collective-permute-start | bytes 245768 | tf_op jit(solution)/shard_map/ppermute | solution.py:228
  22.8 0.1 fusion.2
  23.0 1.2 %collective-permute-start.3 = (f32[5,16,256]{2,1,0:T(8,128)S(1)}, f32[5,16,256]{2,1,0:T(8,128)S(1)}, u32[]{:S(2)}, u32[]{:S(2)}) collective-permute-start(f32[5,16,256]{2,1,0:T(8,128)S(1)} %get-tuple-element.33), channel_id=1, source_target_pairs={{0,1},{1,0},{2,3},{3,2},{4,5},{5,4},{6,7},{7,6},{8,9},{9,8},{10,11... | collective-permute-start | bytes 245768 | tf_op jit(solution)/shard_map/ppermute | solution.py:227
  24.2 2.2 %collective-permute-start.2 = (f32[5,16,256]{2,1,0:T(8,128)S(1)}, f32[5,16,256]{2,1,0:T(8,128)S(1)}, u32[]{:S(2)}, u32[]{:S(2)}) collective-permute-start(f32[5,16,256]{2,1,0:T(8,128)S(1)} %get-tuple-element.34), channel_id=1, source_target_pairs={{1,2},{2,1},{3,4},{4,3},{5,6},{6,5},{9,10},{10,9},{11,12},{12,11},... | collective-permute-start | bytes 245768 | tf_op jit(solution)/shard_map/ppermute | solution.py:228
  26.4 0.0 copy-done.9
  26.4 0.1 reshape.26.coef
  26.5 0.0 collective-permute-done.1
  26.5 0.0 collective-permute-done
  26.6 0.0 collective-permute-done.3
  26.6 3.7 %collective-permute-done.2 = f32[5,16,256]{2,1,0:T(8,128)S(1)} collective-permute-done((f32[5,16,256]{2,1,0:T(8,128)S(1)}, f32[5,16,256]{2,1,0:T(8,128)S(1)}, u32[]{:S(2)}, u32[]{:S(2)}) %collective-permute-start.2) | collective-permute-done | bytes 81952 | tf_op jit(solution)/shard_map/ppermute | solution.py:228
  30.3 0.0 all-to-all-done.got
  30.3 0.0 copy-done.4
  30.3 14.1 %first.1 = (f32[5,16,16,256]{3,2,1,0:T(8,128)S(1)}, f32[5,256,256]{2,1,0:T(8,128)S(1)}, f32[256,256]{1,0:T(8,128)S(1)}, f32[5,16,256]{2,1,0:T(8,128)S(1)}, f32[5...) custom-call(f32[150]{0:T(256)S(1)} %reshape.26.coef, f32[5,16,16,256]{3,2,1,0:T(8,128)S(1)} %copy-done.1, ...), custom_call_target="tpu_custom_call" | custom-call | tf_op jit(solution)/shard_map/first/pallas_call | solution.py:286
  44.4 0.0 copy-start.3
  44.4 0.1 collective-permute-start.5
  44.5 4.0 %collective-permute-start.4 = (f32[5,16,256]{2,1,0:T(8,128)S(1)}, f32[5,16,256]{2,1,0:T(8,128)S(1)}, u32[]{:S(2)}, u32[]{:S(2)}) collective-permute-start(f32[5,16,256]{2,1,0:T(8,128)S(1)} %get-tuple-element.30), channel_id=1, source_target_pairs={{8,16},{16,8},{9,17},{17,9},{10,18},{18,10},{11,19},{19,11},{12,20... | collective-permute-start | bytes 245768 | tf_op jit(solution)/shard_map/ppermute | solution.py:228
  48.6 0.3 collective-permute-start.7
  48.9 1.9 %collective-permute-start.6 = (f32[5,16,256]{2,1,0:T(8,128)S(1)}, f32[5,16,256]{2,1,0:T(8,128)S(1)}, u32[]{:S(2)}, u32[]{:S(2)}) collective-permute-start(f32[5,16,256]{2,1,0:T(8,128)S(1)} %get-tuple-element.26), channel_id=1, source_target_pairs={{1,2},{2,1},{3,4},{4,3},{5,6},{6,5},{9,10},{10,9},{11,12},{12,11},... | collective-permute-start | bytes 245768 | tf_op jit(solution)/shard_map/ppermute | solution.py:228
  50.8 0.0 collective-permute-done.5
  50.8 0.0 collective-permute-done.4
  50.9 1.0 %collective-permute-done.7 = f32[5,16,256]{2,1,0:T(8,128)S(1)} collective-permute-done((f32[5,16,256]{2,1,0:T(8,128)S(1)}, f32[5,16,256]{2,1,0:T(8,128)S(1)}, u32[]{:S(2)}, u32[]{:S(2)}) %collective-permute-start.7) | collective-permute-done | bytes 81952 | tf_op jit(solution)/shard_map/ppermute | solution.py:227
  51.9 3.1 %collective-permute-done.6 = f32[5,16,256]{2,1,0:T(8,128)S(1)} collective-permute-done((f32[5,16,256]{2,1,0:T(8,128)S(1)}, f32[5,16,256]{2,1,0:T(8,128)S(1)}, u32[]{:S(2)}, u32[]{:S(2)}) %collective-permute-start.6) | collective-permute-done | bytes 81952 | tf_op jit(solution)/shard_map/ppermute | solution.py:228
  55.0 0.0 copy-done.3
  55.0 6.3 %second.1 = f32[5,16,16,256]{3,2,1,0:T(8,128)} custom-call(f32[150]{0:T(256)S(1)} %reshape.26.coef, f32[5,16,16,256]{3,2,1,0:T(8,128)S(1)} %get-tuple-element.12.state, f32[5,16,16,256]{3,2,1,0:T(8,128)S(1)} %copy-done.1, f32[5,16,16,256]{3,2,1,0:T(8,128)S(1)} %copy-done.3, f32[16,16,256]{2,1,0:T(8,128)S(1)} %copy-done.4, ...), custom_call_target="tpu_custom_call" | custom-call | tf_op jit(solution)/shard_map/second/pallas_call | solution.py:305
  (9 shorter events, 0.1 us)
Async XLA Ops:
  0.7 1.3 %copy-start = (f32[5,16,16,256]{3,2,1,0:T(8,128)S(1)}, f32[5,16,16,256]{3,2,1,0:T(8,128)}, u32[]{:S(2)}) copy-start(f32[5,16,16,256]{3,2,1,0:T(8,128)} %q_now.3) | copy-start | bytes 3932164
  2.0 1.3 %copy-start.2 = (f32[5,16,16,256]{3,2,1,0:T(8,128)S(1)}, f32[5,16,16,256]{3,2,1,0:T(8,128)}, u32[]{:S(2)}) copy-start(f32[5,16,16,256]{3,2,1,0:T(8,128)} %q_prev.3) | copy-start | bytes 3932164
  3.3 0.7 %copy-start.5 = (f32[3,1024]{1,0:T(4,128)S(1)}, f32[3,1024]{1,0:T(4,128)}, u32[]{:S(2)}) copy-start(f32[3,1024]{1,0:T(4,128)} %frac.1) | copy-start | bytes 36868
  4.0 0.7 %copy-start.6 = (s32[1024]{0:T(1024)S(1)}, s32[1024]{0:T(1024)}, u32[]{:S(2)}) copy-start(s32[1024]{0:T(1024)} %param.13) | copy-start | bytes 12292
  4.7 0.7 %copy-start.7 = (s32[1024,1]{0,1:T(1,128)S(1)}, s32[1024,1]{0,1:T(1,128)}, u32[]{:S(2)}) copy-start(s32[1024,1]{0,1:T(1,128)} %param.15) | copy-start | bytes 12292
  5.4 0.7 %copy-start.8 = (s32[1024]{0:T(1024)S(1)}, s32[1024]{0:T(1024)}, u32[]{:S(2)}) copy-start(s32[1024]{0:T(1024)} %param.16) | copy-start | bytes 12292
  6.1 13.2 %copy-start.1 = (f32[5,16,16,256]{3,2,1,0:T(8,128)S(1)}, f32[5,16,16,256]{3,2,1,0:T(8,128)}, u32[]{:S(2)}) copy-start(f32[5,16,16,256]{3,2,1,0:T(8,128)} %q_now.3) | copy-start | bytes 3932164
  12.8 13.6 %copy-start.9 = (f32[3,2,5,5]{3,1,2,0:T(2,128)S(1)}, f32[3,2,5,5]{3,1,2,0:T(2,128)}, u32[]{:S(2)}) copy-start(f32[3,2,5,5]{3,1,2,0:T(2,128)} %param.12) | copy-start | bytes 1804
  12.9 17.5 %copy-start.4 = (f32[16,16,256]{2,1,0:T(8,128)S(1)}, f32[16,16,256]{2,1,0:T(8,128)}, u32[]{:S(2)}) copy-start(f32[16,16,256]{2,1,0:T(8,128)} %jac.3) | copy-start | bytes 786436
  12.9 17.4 %all-to-all-start = ((f32[32,8,128]{2,1,0:T(8,128)}), f32[32,8,128]{2,1,0:T(8,128)S(1)}, u32[]{:S(2)}, u32[]{:S(2)}) async-start(f32[32,8,128]{2,1,0:T(8,128)} %donor.1), calls=%async_computation | async-start | bytes 262144 | tf_op jit(solution)/shard_map/all_to_all | solution.py:275
  19.3 7.3 %collective-permute-start.1 = (f32[5,16,256]{2,1,0:T(8,128)S(1)}, f32[5,16,256]{2,1,0:T(8,128)S(1)}, u32[]{:S(2)}, u32[]{:S(2)}) collective-permute-start(f32[5,16,256]{2,1,0:T(8,128)S(1)} %get-tuple-element.21), channel_id=1, source_target_pairs={{0,8},{8,0},{16,24},{24,16},{1,9},{9,1},{17,25},{25,17},{2,10},{10... | collective-permute-start | bytes 245768 | tf_op jit(solution)/shard_map/ppermute | solution.py:227
  19.7 6.8 %collective-permute-start = (f32[5,16,256]{2,1,0:T(8,128)S(1)}, f32[5,16,256]{2,1,0:T(8,128)S(1)}, u32[]{:S(2)}, u32[]{:S(2)}) collective-permute-start(f32[5,16,256]{2,1,0:T(8,128)S(1)} %get-tuple-element.22), channel_id=1, source_target_pairs={{8,16},{16,8},{9,17},{17,9},{10,18},{18,10},{11,19},{19,11},{12,20... | collective-permute-start | bytes 245768 | tf_op jit(solution)/shard_map/ppermute | solution.py:228
  23.0 3.6 %collective-permute-start.3 = (f32[5,16,256]{2,1,0:T(8,128)S(1)}, f32[5,16,256]{2,1,0:T(8,128)S(1)}, u32[]{:S(2)}, u32[]{:S(2)}) collective-permute-start(f32[5,16,256]{2,1,0:T(8,128)S(1)} %get-tuple-element.33), channel_id=1, source_target_pairs={{0,1},{1,0},{2,3},{3,2},{4,5},{5,4},{6,7},{7,6},{8,9},{9,8},{10,11... | collective-permute-start | bytes 245768 | tf_op jit(solution)/shard_map/ppermute | solution.py:227
  24.2 6.1 %collective-permute-start.2 = (f32[5,16,256]{2,1,0:T(8,128)S(1)}, f32[5,16,256]{2,1,0:T(8,128)S(1)}, u32[]{:S(2)}, u32[]{:S(2)}) collective-permute-start(f32[5,16,256]{2,1,0:T(8,128)S(1)} %get-tuple-element.34), channel_id=1, source_target_pairs={{1,2},{2,1},{3,4},{4,3},{5,6},{6,5},{9,10},{10,9},{11,12},{12,11},... | collective-permute-start | bytes 245768 | tf_op jit(solution)/shard_map/ppermute | solution.py:228
  44.4 10.6 %copy-start.3 = (f32[5,16,16,256]{3,2,1,0:T(8,128)S(1)}, f32[5,16,16,256]{3,2,1,0:T(8,128)}, u32[]{:S(2)}) copy-start(f32[5,16,16,256]{3,2,1,0:T(8,128)} %q_prev.3) | copy-start | bytes 3932164
  44.4 6.4 %collective-permute-start.5 = (f32[5,16,256]{2,1,0:T(8,128)S(1)}, f32[5,16,256]{2,1,0:T(8,128)S(1)}, u32[]{:S(2)}, u32[]{:S(2)}) collective-permute-start(f32[5,16,256]{2,1,0:T(8,128)S(1)} %get-tuple-element.29), channel_id=1, source_target_pairs={{0,8},{8,0},{16,24},{24,16},{1,9},{9,1},{17,25},{25,17},{2,10},{10... | collective-permute-start | bytes 245768 | tf_op jit(solution)/shard_map/ppermute | solution.py:227
  44.5 6.3 %collective-permute-start.4 = (f32[5,16,256]{2,1,0:T(8,128)S(1)}, f32[5,16,256]{2,1,0:T(8,128)S(1)}, u32[]{:S(2)}, u32[]{:S(2)}) collective-permute-start(f32[5,16,256]{2,1,0:T(8,128)S(1)} %get-tuple-element.30), channel_id=1, source_target_pairs={{8,16},{16,8},{9,17},{17,9},{10,18},{18,10},{11,19},{19,11},{12,20... | collective-permute-start | bytes 245768 | tf_op jit(solution)/shard_map/ppermute | solution.py:228
  48.6 3.4 %collective-permute-start.7 = (f32[5,16,256]{2,1,0:T(8,128)S(1)}, f32[5,16,256]{2,1,0:T(8,128)S(1)}, u32[]{:S(2)}, u32[]{:S(2)}) collective-permute-start(f32[5,16,256]{2,1,0:T(8,128)S(1)} %get-tuple-element.25), channel_id=1, source_target_pairs={{0,1},{1,0},{2,3},{3,2},{4,5},{5,4},{6,7},{7,6},{8,9},{9,8},{10,11... | collective-permute-start | bytes 245768 | tf_op jit(solution)/shard_map/ppermute | solution.py:227
  48.9 6.1 %collective-permute-start.6 = (f32[5,16,256]{2,1,0:T(8,128)S(1)}, f32[5,16,256]{2,1,0:T(8,128)S(1)}, u32[]{:S(2)}, u32[]{:S(2)}) collective-permute-start(f32[5,16,256]{2,1,0:T(8,128)S(1)} %get-tuple-element.26), channel_id=1, source_target_pairs={{1,2},{2,1},{3,4},{4,3},{5,6},{6,5},{9,10},{10,9},{11,12},{12,11},... | collective-permute-start | bytes 245768 | tf_op jit(solution)/shard_map/ppermute | solution.py:228
where the time goes:
time: 61.8 us; the launch traced here: 61.3 us
  Pallas kernels  27.1 us (44%)
  starting transfers between devices  19.6 us (32%)
  waiting for transfers between devices  7.82 us (13%)
  local copies, waits for them, and re-layouts  5.64 us (9%)
  between operations  0.95 us (2%)
    pallas_call x1, Pallas kernels, body(): pl.pallas_call(functools.partial(first_kernel, size=size, devices=devices...  14.1 us
    ppermute x4, starting transfers between devices, exchanged(): lax.ppermute(jnp.where(even, low_face, high_face), axis, swap_pairs(axis,...  11.2 us
    pallas_call x1, Pallas kernels, body(): pl.pallas_call(functools.partial(donor_kernel, size=size, devices=devices...  6.77 us
    ppermute x4, waiting for transfers between devices, exchanged(): lax.ppermute(jnp.where(even, low_face, high_face), axis, swap_pairs(axis,...  6.76 us
    all_to_all x1, starting transfers between devices, body(): got = lax.all_to_all(sent, AXES, split_axis=0, concat_axis=0, tiled=True)  6.32 us
    pallas_call x1, Pallas kernels, body(): pl.pallas_call(functools.partial(second_kernel, size=size), out_shape=jax...  6.28 us
    unnamed x21, local copies, waits for them, and re-layouts  5.43 us
    ppermute x4, starting transfers between devices, exchanged(): lax.ppermute(jnp.where(even, high_face, low_face), axis, swap_pairs(axis,...  2.13 us
  transfers between devices with their start and end apart: 9, of which 3 were waited for; matrix products, arithmetic and copies ran while one was open for 1% of the time, Pallas kernels for 0%

commit v1 on v0

--- a/solution.py
+++ b/solution.py
@@ -47,14 +47,16 @@
     return jnp.concatenate(pieces, axis=1)
 
 
-def donor_kernel(count, q_prev, q_now, base, frac, dest, cell, out, planes, lhs, spread, corner, place, values, sems, *, size, devices, capacity):
+def donor_kernel(count, q_prev, q_now, base_in, frac_in, dest_in, cell_in, out, planes, lhs, spread, corner, place, values, base, frac, dest, cell, sems, *, size, devices, capacity):
     nvars, size_x, size_y, size_z = size
     columns = size_x * size_y
     rows = base.shape[1]
-    copies = []
-    for k, ref in enumerate((q_prev, q_now)):
-        copies.append(pltpu.make_async_copy(ref, planes.at[k], sems.at[k]))
-        copies[-1].start()
+    small = [pltpu.make_async_copy(a, b, sems.at[2 + k]) for k, (a, b) in enumerate(((base_in, base), (frac_in, frac), (dest_in, dest), (cell_in, cell)))]
+    copies = [pltpu.make_async_copy(ref, planes.at[k], sems.at[k]) for k, ref in enumerate((q_prev, q_now))]
+    for copy in small + copies:
+        copy.start()
+    for copy in small:
+        copy.wait()
     start = base[...].astype(jnp.float32)
     in_y = jnp.floor((start + 0.5) * (1.0 / (size_z - 1)))
     base_z = start - in_y * (size_z - 1)
@@ -116,101 +118,141 @@
             out[to] = jnp.concatenate([piece[0:8], piece[8:16]], axis=1)
 
 
-def flux_of(coef, centre, neighbours):
-    nvars = len(centre)
-    total = [None] * nvars
-    for d, (behind, ahead) in enumerate(neighbours):
-        for side in range(2):
-            moved = [c - b for c, b in zip(centre, behind)] if side == 0 else [f - c for c, f in zip(centre, ahead)]
-            for a in range(nvars):
-                for b in range(nvars):
-                    term = coef[((d * 2 + side) * nvars + a) * nvars + b] * moved[b]
-                    total[a] = term if total[a] is None else total[a] + term
-    return total
-
-
-def neighbours_at(x, state, x_low, x_high, y_low, y_high, size):
-    nvars, size_x, size_y, size_z = size
-    rows_at = iota((size_y, size_z), 0)
-    z_at = iota((size_y, size_z), 1)
-    centre = [state[v, x] for v in range(nvars)]
-    back_x = [jnp.where(x == 0, x_low[v], state[v, jnp.maximum(x - 1, 0)]) for v in range(nvars)]
-    fore_x = [jnp.where(x == size_x - 1, x_high[v], state[v, jnp.minimum(x + 1, size_x - 1)]) for v in range(nvars)]
-    back_y = [jnp.where(rows_at == 0, y_low[v, pl.ds(x, 1), :], pltpu.roll(centre[v], 1, 0)) for v in range(nvars)]
-    fore_y = [jnp.where(rows_at == size_y - 1, y_high[v, pl.ds(x, 1), :], pltpu.roll(centre[v], size_y - 1, 0)) for v in range(nvars)]
-    back_z = [jnp.where(z_at == 0, 0.0, pltpu.roll(centre[v], 1, 1)) for v in range(nvars)]
-    fore_z = [jnp.where(z_at == size_z - 1, 0.0, pltpu.roll(centre[v], size_z - 1, 1)) for v in range(nvars)]
-    return centre, [(back_x, fore_x), (back_y, fore_y), (back_z, fore_z)]
-
-
-def first_kernel(coef, q_now, q_prev, jac, got, x_low, x_high, y_low, y_high, state, target, hits, face_xl, face_xh, face_yl, face_yh, rows, grid, *, size, devices, capacity):
+def mixing_weights(coef, high, low, size):
+    nvars, size_x, size_y, size_z = size
+    block = nvars * size_y
+    width = 3 * block + CHANNELS
+    row = iota((size_y, width), 0)
+    offset = iota((size_y, width), 1) - row
+    lane = iota((size_y, width), 1)
+
+    def at(d, side, a, b):
+        return coef[((d * 2 + side) * nvars + a) * nvars + b]
+
+    for a in range(nvars):
+        main = jnp.zeros((size_y, width), jnp.float32)
+        back = main
+        fore = main
+        for b in range(nvars):
+            first = b * size_y
+            same = at(0, 0, a, b) - at(0, 1, a, b) + at(1, 0, a, b) - at(1, 1, a, b) + at(2, 0, a, b) - at(2, 1, a, b)
+            main = jnp.where(offset == first, -at(0, 0, a, b), main)
+            main = jnp.where(offset == block + first, same, main)
+            main = jnp.where((offset == block + first - 1) & (row > 0), -at(1, 0, a, b), main)
+            main = jnp.where((offset == block + first + 1) & (row < size_y - 1), at(1, 1, a, b), main)
+            main = jnp.where(offset == 2 * block + first, at(0, 1, a, b), main)
+            main = jnp.where((lane == 3 * block + b) & (row == 0), -at(1, 0, a, b), main)
+            main = jnp.where((lane == 3 * block + nvars + b) & (row == size_y - 1), at(1, 1, a, b), main)
+            back = jnp.where(offset == block + first, -at(2, 0, a, b), back)
+            fore = jnp.where(offset == block + first, at(2, 1, a, b), fore)
+        for k, part in enumerate((main, back, fore)):
+            rows = slice(k * block + a * size_y, k * block + (a + 1) * size_y)
+            high[rows, :], low[rows, :] = halves(part)
+
+
+def fill_planes(state, x_low, x_high, y_low, y_high, planes, sides, size):
+    nvars, size_x, size_y, size_z = size
+    block = nvars * size_y
+    for x in range(size_x + 2):
+        for v in range(nvars):
+            value = x_low[v] if x == 0 else x_high[v] if x == size_x + 1 else state[v, x - 1]
+            rows = slice(x * block + v * size_y, x * block + (v + 1) * size_y)
+            planes[0, rows, :], planes[1, rows, :] = halves(value)
+    sides[...] = jnp.zeros(sides.shape, jnp.float32)
+    for v in range(nvars):
+        sides[:, v, :] = y_low[v]
+        sides[:, nvars + v, :] = y_high[v]
+
+
+def flux_at(x, weights, planes, sides, size):
+    nvars, size_x, size_y, size_z = size
+    block = nvars * size_y
+    high, low = halves(sides[x])
+    rows = slice(x * block, (x + 3) * block)
+    around_high = jnp.concatenate([planes[0, rows, :], high], axis=0)
+    around_low = jnp.concatenate([planes[1, rows, :], low], axis=0)
+    both = jnp.concatenate([weights[0], weights[1]], axis=0)
+    mixed = dot(both, around_high, ((1,), (0,)))
+    mixed = mixed[0 : 3 * block] + mixed[3 * block :] + dot(weights[0], around_low, ((1,), (0,)))
+    z_at = iota((block, size_z), 1)
+    back = jnp.where(z_at == 0, 0.0, pltpu.roll(mixed[block : 2 * block], 1, 1))
+    fore = jnp.where(z_at == size_z - 1, 0.0, pltpu.roll(mixed[2 * block :], size_z - 1, 1))
+    flux = mixed[0:block] + back + fore
+    return [flux[v * size_y : (v + 1) * size_y] for v in range(nvars)]
+
+
+def first_kernel(coef, q_now, q_prev, jac, got, x_low, x_high, y_low, y_high, state, target, hits, face_xl, face_xh, face_yl, face_yh, weights, rows, hot_xy, hot_z, grid, planes, sides, *, size, devices, capacity):
     nvars, size_x, size_y, size_z = size
     columns = size_x * size_y
+    slots = devices * capacity
+    mixing_weights(coef, weights.at[0], weights.at[1], size)
+    fill_planes(q_now, x_low, x_high, y_low, y_high, planes, sides, size)
     for d in range(devices):
         piece = got[d]
         lanes = slice(d * capacity, (d + 1) * capacity)
         rows[0:8, lanes] = piece[:, 0:capacity]
         rows[8:16, lanes] = piece[:, capacity : 2 * capacity]
-    grid[...] = jnp.zeros(grid.shape, jnp.float32)
-    place_xy = (iota((columns, LANES), 0) + 1).astype(jnp.float32)
-    place_z = iota((size_z, LANES), 0).astype(jnp.float32)
-
-    def chunk(n, carry):
-        block = rows[:, pl.ds(pl.multiple_of(n * LANES, LANES), LANES)]
-        hot_xy = (place_xy == block[2 * nvars : 2 * nvars + 1]).astype(jnp.float32).astype(jnp.bfloat16)
-        hot_z = (place_z == block[2 * nvars + 1 : 2 * nvars + 2]).astype(jnp.float32).astype(jnp.bfloat16)
-        high, low = halves(block[0 : 2 * nvars])
+    turned = jnp.transpose(rows[8:16, :])
+    land_z = turned[:, 2 * nvars + 1 - 8 : 2 * nvars + 2 - 8]
+    hot_z[...] = (iota((slots, size_z), 1).astype(jnp.float32) == land_z).astype(jnp.float32).astype(jnp.bfloat16)
+    land_xy = rows[2 * nvars : 2 * nvars + 1, :]
+    hot_xy[...] = ((iota((columns, slots), 0) + 1).astype(jnp.float32) == land_xy).astype(jnp.float32).astype(jnp.bfloat16)
+
+    def pair(g, carry):
         pieces = []
-        for c in range(2 * nvars):
-            pieces += [hot_xy * high[c : c + 1], hot_xy * low[c : c + 1]]
-        pieces.append(hot_xy)
-        landed = dot(jnp.concatenate(pieces, axis=0), hot_z, ((1,), (1,)))
-        for c in range(2 * nvars):
+        for c in range(2):
+            for half in halves(rows[pl.ds(2 * g + c, 1), :]):
+                pieces.append(hot_xy[...] * half)
+        landed = dot(jnp.concatenate(pieces, axis=0), hot_z[...], ((1,), (0,)))
+        for c in range(2):
             at = 2 * c * columns
-            grid[c] = grid[c] + (landed[at : at + columns] + landed[at + columns : at + 2 * columns])
-        grid[2 * nvars] = grid[2 * nvars] + landed[4 * nvars * columns :]
+            grid[2 * g + c] = landed[at : at + columns] + landed[at + columns : at + 2 * columns]
         return carry
 
-    lax.fori_loop(0, devices * capacity // LANES, chunk, 0)
+    lax.fori_loop(0, nvars, pair, 0)
+    hits[...] = dot(hot_xy[...], hot_z[...], ((1,), (0,)))
     target[...] = grid[nvars : 2 * nvars]
-    hits[...] = grid[2 * nvars]
-
-    def plane(x, carry):
-        at = pl.ds(pl.multiple_of(x * size_y, size_y), size_y)
-        centre, around = neighbours_at(x, q_now, x_low, x_high, y_low, y_high, size)
-        flux = flux_of(coef, centre, around)
-        landed = grid[2 * nvars, at, :]
-        scale = step_tau * jac[x]
-        for v in range(nvars):
-            physical = (3.0 * centre[v] - 4.0 * centre[v] + q_prev[v, x]) / (2.0 * step_phys)
-            coupling = penalty * (landed * centre[v] - grid[v, at, :])
-            new = centre[v] - scale * (flux[v] + physical + coupling)
-            state[v, x] = new
-            face_yl[v, pl.ds(x, 1), :] = new[0:1]
-            face_yh[v, pl.ds(x, 1), :] = new[size_y - 1 : size_y]
-        return carry
-
-    lax.fori_loop(0, size_x, plane, 0)
-    face_xl[...] = state[:, 0]
-    face_xh[...] = state[:, size_x - 1]
-
-
-def second_kernel(coef, state, q_now, q_prev, jac, target, hits, x_low, x_high, y_low, y_high, out, *, size):
-    nvars, size_x, size_y, size_z = size
-
-    def plane(x, carry):
-        at = pl.ds(pl.multiple_of(x * size_y, size_y), size_y)
-        centre, around = neighbours_at(x, state, x_low, x_high, y_low, y_high, size)
-        flux = flux_of(coef, centre, around)
+    for x in range(size_x):
+        at = slice(x * size_y, (x + 1) * size_y)
+        flux = flux_at(x, weights, planes, sides, size)
         landed = hits[at, :]
         scale = step_tau * jac[x]
         for v in range(nvars):
-            physical = (3.0 * centre[v] - 4.0 * q_now[v, x] + q_prev[v, x]) / (2.0 * step_phys)
-            coupling = penalty * (landed * centre[v] - target[v, at, :])
-            out[v, x] = centre[v] - scale * (flux[v] + physical + coupling)
-        return carry
-
-    lax.fori_loop(0, size_x, plane, 0)
+            centre = q_now[v, x]
+            physical = (q_prev[v, x] - centre) / (2.0 * step_phys)
+            coupling = penalty * (landed * centre - grid[v, at, :])
+            new = centre - scale * (flux[v] + physical + coupling)
+            state[v, x] = new
+            face_yl[v, x : x + 1, :] = new[0:1]
+            face_yh[v, x : x + 1, :] = new[size_y - 1 : size_y]
+            if x == 0:
+                face_xl[v] = new
+            if x == size_x - 1:
+                face_xh[v] = new
+
+
+def second_kernel(coef, state, q_now, q_prev, jac, target, hits, x_low, x_high, y_low, y_high, out, weights, planes, sides, buffer, sems, *, size):
+    nvars, size_x, size_y, size_z = size
+    mixing_weights(coef, weights.at[0], weights.at[1], size)
+    fill_planes(state, x_low, x_high, y_low, y_high, planes, sides, size)
+    part = size_x // 4
+    copies = []
+    for x in range(size_x):
+        at = slice(x * size_y, (x + 1) * size_y)
+        flux = flux_at(x, weights, planes, sides, size)
+        landed = hits[at, :]
+        scale = step_tau * jac[x]
+        for v in range(nvars):
+            centre = state[v, x]
+            physical = (3.0 * centre - 4.0 * q_now[v, x] + q_prev[v, x]) / (2.0 * step_phys)
+            coupling = penalty * (landed * centre - target[v, at, :])
+            buffer[v, x] = centre - scale * (flux[v] + physical + coupling)
+        if (x + 1) % part == 0:
+            some = pl.ds(x + 1 - part, part)
+            copies.append(pltpu.make_async_copy(buffer.at[:, some], out.at[:, some], sems.at[x // part]))
+            copies[-1].start()
+    for copy in copies:
+        copy.wait()
 
 
 def swap_pairs(axis, odd):
@@ -243,14 +285,18 @@
     slots = devices * capacity
     f32, bf16 = jnp.float32, jnp.bfloat16
     smem = pl.BlockSpec(memory_space=pltpu.SMEM)
-    hbm = pl.BlockSpec(memory_space=pl.ANY)
+    hbm = pl.BlockSpec(memory_space=pltpu.HBM)
     vmem = pl.BlockSpec(memory_space=pltpu.VMEM)
     coef = flux_split.reshape(-1)
+    block = nvars * size_y
+    weights = pltpu.VMEM((2, 3 * block, 3 * block + CHANNELS), bf16)
+    planes = pltpu.VMEM((2, (size_x + 2) * block, size_z), bf16)
+    sides = pltpu.VMEM((size_x, CHANNELS, size_z), f32)
     flat = (nvars, columns, size_z)
     sent = pl.pallas_call(
         functools.partial(donor_kernel, size=size, devices=devices, capacity=capacity),
         out_shape=jax.ShapeDtypeStruct((devices, 8, 2 * capacity), f32),
-        in_specs=[smem, hbm, hbm, vmem, vmem, vmem, vmem],
+        in_specs=[smem] + [hbm] * 6,
         out_specs=vmem,
         scratch_shapes=[
             pltpu.VMEM((2, nvars, columns, size_z), f32),
@@ -259,7 +305,11 @@
             pltpu.VMEM((columns, rows), f32),
             pltpu.VMEM((rows, 8), f32),
             pltpu.VMEM((CHANNELS, rows), f32),
-            pltpu.SemaphoreType.DMA((2,)),
+            pltpu.VMEM((1, rows), jnp.int32),
+            pltpu.VMEM((3, rows), f32),
+            pltpu.VMEM((1, rows), jnp.int32),
+            pltpu.VMEM((1, rows), jnp.int32),
+            pltpu.SemaphoreType.DMA((6,)),
         ],
         compiler_params=params(48),
         name="donor",
@@ -296,7 +346,15 @@
         ],
         in_specs=[smem] + [vmem] * 8,
         out_specs=[vmem] * 7,
-        scratch_shapes=[pltpu.VMEM((CHANNELS, slots), f32), pltpu.VMEM((2 * nvars + 1, columns, size_z), f32)],
+        scratch_shapes=[
+            weights,
+            pltpu.VMEM((CHANNELS, slots), f32),
+            pltpu.VMEM((columns, slots), bf16),
+            pltpu.VMEM((slots, size_z), bf16),
+            pltpu.VMEM((2 * nvars, columns, size_z), f32),
+            planes,
+            sides,
+        ],
         compiler_params=params(48),
         name="first",
     )(coef, q_now, q_prev, jacobian, got, *x_halo, *y_halo)
@@ -306,8 +364,9 @@
         functools.partial(second_kernel, size=size),
         out_shape=jax.ShapeDtypeStruct(size, f32),
         in_specs=[smem] + [vmem] * 10,
-        out_specs=vmem,
-        compiler_params=params(48),
+        out_specs=hbm,
+        scratch_shapes=[weights, planes, sides, pltpu.VMEM(size, f32), pltpu.SemaphoreType.DMA((4,))],
+        compiler_params=params(40),
         name="second",
     )(coef, state, q_now, q_prev, jacobian, target, hits, *x_halo, *y_halo)
 

time: 61.8 us -> 56.3 us (0.911)
  Pallas kernels: 27.1 us -> 21.6 us
    pallas_call x1, Pallas kernels: 14.1 us -> 11.2 us  [body(): pl.pallas_call(functools.partial(first_kernel, size=size, devices=devices...]
    pallas_call x1, Pallas kernels: 6.28 us -> 3.46 us  [body(): pl.pallas_call(functools.partial(second_kernel, size=size), out_shape=jax...]
where the time goes in v1:
time: 56.3 us; the launch traced here: 55.8 us
  Pallas kernels  21.6 us (38%)
  starting transfers between devices  19.6 us (35%)
  waiting for transfers between devices  7.82 us (14%)
  local copies, waits for them, and re-layouts  5.64 us (10%)
  between operations  0.95 us (2%)
    ppermute x4, starting transfers between devices, exchanged(): lax.ppermute(jnp.where(even, low_face, high_face), axis, swap_pairs(axis,...  11.2 us
    pallas_call x1, Pallas kernels, body(): pl.pallas_call(functools.partial(first_kernel, size=size, devices=devices...  11.2 us
    pallas_call x1, Pallas kernels, body(): pl.pallas_call(functools.partial(donor_kernel, size=size, devices=devices...  6.99 us
    ppermute x4, waiting for transfers between devices, exchanged(): lax.ppermute(jnp.where(even, low_face, high_face), axis, swap_pairs(axis,...  6.76 us
    all_to_all x1, starting transfers between devices, body(): got = lax.all_to_all(sent, AXES, split_axis=0, concat_axis=0, tiled=True)  6.33 us
    unnamed x21, local copies, waits for them, and re-layouts  5.43 us
    pallas_call x1, Pallas kernels, body(): pl.pallas_call(functools.partial(second_kernel, size=size), out_shape=jax...  3.46 us
    ppermute x4, starting transfers between devices, exchanged(): lax.ppermute(jnp.where(even, high_face, low_face), axis, swap_pairs(axis,...  2.12 us
  transfers between devices with their start and end apart: 9, of which 3 were waited for; matrix products, arithmetic and copies ran while one was open for 1% of the time, Pallas kernels for 0%

profile of v1, /device:TPU:9, one launch (start us, length us, event | category | flops | bytes accessed | tf_op | source)
XLA Modules:
  0.0 55.8 jit_solution(18357198842532078094)
XLA Ops:
  0.7 0.0 copy-start
  0.7 1.3 %copy-done = f32[5,16,16,256]{3,2,1,0:T(8,128)S(1)} copy-done((f32[5,16,16,256]{3,2,1,0:T(8,128)S(1)}, f32[5,16,16,256]{3,2,1,0:T(8,128)}, u32[]{:S(2)}) %copy-start) | copy-done | bytes 1310744
  2.0 0.0 copy-start.2
  2.0 1.3 %copy-done.2 = f32[5,16,16,256]{3,2,1,0:T(8,128)S(1)} copy-done((f32[5,16,16,256]{3,2,1,0:T(8,128)S(1)}, f32[5,16,16,256]{3,2,1,0:T(8,128)}, u32[]{:S(2)}) %copy-start.2) | copy-done | bytes 1310744
  3.3 0.0 copy-start.5
  3.3 0.7 %copy-done.5 = f32[3,1024]{1,0:T(4,128)S(1)} copy-done((f32[3,1024]{1,0:T(4,128)S(1)}, f32[3,1024]{1,0:T(4,128)}, u32[]{:S(2)}) %copy-start.5) | copy-done | bytes 12312
  4.0 0.0 copy-start.6
  4.0 0.7 %copy-done.6 = s32[1024]{0:T(1024)S(1)} copy-done((s32[1024]{0:T(1024)S(1)}, s32[1024]{0:T(1024)}, u32[]{:S(2)}) %copy-start.6) | copy-done | bytes 4120
  4.7 0.0 copy-start.7
  4.7 0.7 %copy-done.7 = s32[1024,1]{0,1:T(1,128)S(1)} copy-done((s32[1024,1]{0,1:T(1,128)S(1)}, s32[1024,1]{0,1:T(1,128)}, u32[]{:S(2)}) %copy-start.7) | copy-done | bytes 4120
  5.4 0.0 copy-start.8
  5.4 0.7 %copy-done.8 = s32[1024]{0:T(1024)S(1)} copy-done((s32[1024]{0:T(1024)S(1)}, s32[1024]{0:T(1024)}, u32[]{:S(2)}) %copy-start.8) | copy-done | bytes 4120
  6.1 0.0 copy-start.1
  6.1 7.0 %donor.1 = f32[32,8,128]{2,1,0:T(8,128)} custom-call(s32[1]{0:T(128)S(6)} %copy.27.count, f32[5,256,256]{2,1,0:T(8,128)S(1)} %bitcast.24, f32[5,256,256]{2,1,0:T(8,128)S(1)} %bitcast.23, s32[1,1024]{1,0:T(1,128)S(1)} %bitcast.25, f32[3,1024]{1,0:T(4,128)S(1)} %copy-done.5, s32[1,1024]{1,0:T(1,128)S(1)} %bitcast.26, s32[1,1024]{1,0:T(1,128)S(1)} %bitcast.27), custom_call_target="tpu_custom_call" | custom-call | tf_op jit(solution)/shard_map/donor/pallas_call | solution.py:296
  13.1 0.0 copy-start.9
  13.1 0.0 copy-start.4
  13.1 6.3 %all-to-all-start = ((f32[32,8,128]{2,1,0:T(8,128)}), f32[32,8,128]{2,1,0:T(8,128)S(1)}, u32[]{:S(2)}, u32[]{:S(2)}) async-start(f32[32,8,128]{2,1,0:T(8,128)} %donor.1), calls=%async_computation | async-start | bytes 262144 | tf_op jit(solution)/shard_map/all_to_all | solution.py:325
  19.4 0.0 copy-done.1
  19.5 0.5 collective-permute-start.1
  19.9 3.1 %collective-permute-start = (f32[5,16,256]{2,1,0:T(8,128)S(1)}, f32[5,16,256]{2,1,0:T(8,128)S(1)}, u32[]{:S(2)}, u32[]{:S(2)}) collective-permute-start(f32[5,16,256]{2,1,0:T(8,128)S(1)} %get-tuple-element.22), channel_id=1, source_target_pairs={{8,16},{16,8},{9,17},{17,9},{10,18},{18,10},{11,19},{19,11},{12,20... | collective-permute-start | bytes 245768 | tf_op jit(solution)/shard_map/ppermute | solution.py:270
  23.0 0.1 fusion.2
  23.2 1.2 %collective-permute-start.3 = (f32[5,16,256]{2,1,0:T(8,128)S(1)}, f32[5,16,256]{2,1,0:T(8,128)S(1)}, u32[]{:S(2)}, u32[]{:S(2)}) collective-permute-start(f32[5,16,256]{2,1,0:T(8,128)S(1)} %get-tuple-element.33), channel_id=1, source_target_pairs={{0,1},{1,0},{2,3},{3,2},{4,5},{5,4},{6,7},{7,6},{8,9},{9,8},{10,11... | collective-permute-start | bytes 245768 | tf_op jit(solution)/shard_map/ppermute | solution.py:269
  24.4 2.2 %collective-permute-start.2 = (f32[5,16,256]{2,1,0:T(8,128)S(1)}, f32[5,16,256]{2,1,0:T(8,128)S(1)}, u32[]{:S(2)}, u32[]{:S(2)}) collective-permute-start(f32[5,16,256]{2,1,0:T(8,128)S(1)} %get-tuple-element.34), channel_id=1, source_target_pairs={{1,2},{2,1},{3,4},{4,3},{5,6},{6,5},{9,10},{10,9},{11,12},{12,11},... | collective-permute-start | bytes 245768 | tf_op jit(solution)/shard_map/ppermute | solution.py:270
  26.6 0.0 copy-done.9
  26.7 0.1 reshape.26.coef
  26.8 0.0 collective-permute-done.1
  26.8 0.0 collective-permute-done
  26.8 0.0 collective-permute-done.3
  26.8 3.7 %collective-permute-done.2 = f32[5,16,256]{2,1,0:T(8,128)S(1)} collective-permute-done((f32[5,16,256]{2,1,0:T(8,128)S(1)}, f32[5,16,256]{2,1,0:T(8,128)S(1)}, u32[]{:S(2)}, u32[]{:S(2)}) %collective-permute-start.2) | collective-permute-done | bytes 81952 | tf_op jit(solution)/shard_map/ppermute | solution.py:270
  30.5 0.0 all-to-all-done.got
  30.5 0.0 copy-done.4
  30.5 11.2 %first.1 = (f32[5,16,16,256]{3,2,1,0:T(8,128)S(1)}, f32[5,256,256]{2,1,0:T(8,128)S(1)}, f32[256,256]{1,0:T(8,128)S(1)}, f32[5,16,256]{2,1,0:T(8,128)S(1)}, f32[5...) custom-call(f32[150]{0:T(256)S(1)} %reshape.26.coef, f32[5,16,16,256]{3,2,1,0:T(8,128)S(1)} %copy-done.1, ...), custom_call_target="tpu_custom_call" | custom-call | tf_op jit(solution)/shard_map/first/pallas_call | solution.py:336
  41.7 0.0 copy-start.3
  41.7 0.1 collective-permute-start.5
  41.8 4.0 %collective-permute-start.4 = (f32[5,16,256]{2,1,0:T(8,128)S(1)}, f32[5,16,256]{2,1,0:T(8,128)S(1)}, u32[]{:S(2)}, u32[]{:S(2)}) collective-permute-start(f32[5,16,256]{2,1,0:T(8,128)S(1)} %get-tuple-element.30), channel_id=1, source_target_pairs={{8,16},{16,8},{9,17},{17,9},{10,18},{18,10},{11,19},{19,11},{12,20... | collective-permute-start | bytes 245768 | tf_op jit(solution)/shard_map/ppermute | solution.py:270
  45.9 0.3 collective-permute-start.7
  46.2 1.9 %collective-permute-start.6 = (f32[5,16,256]{2,1,0:T(8,128)S(1)}, f32[5,16,256]{2,1,0:T(8,128)S(1)}, u32[]{:S(2)}, u32[]{:S(2)}) collective-permute-start(f32[5,16,256]{2,1,0:T(8,128)S(1)} %get-tuple-element.26), channel_id=1, source_target_pairs={{1,2},{2,1},{3,4},{4,3},{5,6},{6,5},{9,10},{10,9},{11,12},{12,11},... | collective-permute-start | bytes 245768 | tf_op jit(solution)/shard_map/ppermute | solution.py:270
  48.1 0.0 collective-permute-done.5
  48.2 0.0 collective-permute-done.4
  48.2 1.1 %collective-permute-done.7 = f32[5,16,256]{2,1,0:T(8,128)S(1)} collective-permute-done((f32[5,16,256]{2,1,0:T(8,128)S(1)}, f32[5,16,256]{2,1,0:T(8,128)S(1)}, u32[]{:S(2)}, u32[]{:S(2)}) %collective-permute-start.7) | collective-permute-done | bytes 81952 | tf_op jit(solution)/shard_map/ppermute | solution.py:269
  49.2 3.1 %collective-permute-done.6 = f32[5,16,256]{2,1,0:T(8,128)S(1)} collective-permute-done((f32[5,16,256]{2,1,0:T(8,128)S(1)}, f32[5,16,256]{2,1,0:T(8,128)S(1)}, u32[]{:S(2)}, u32[]{:S(2)}) %collective-permute-start.6) | collective-permute-done | bytes 81952 | tf_op jit(solution)/shard_map/ppermute | solution.py:270
  52.3 0.0 copy-done.3
  52.3 3.5 %second.1 = f32[5,16,16,256]{3,2,1,0:T(8,128)} custom-call(f32[150]{0:T(256)S(1)} %reshape.26.coef, f32[5,16,16,256]{3,2,1,0:T(8,128)S(1)} %get-tuple-element.12.state, f32[5,16,16,256]{3,2,1,0:T(8,128)S(1)} %copy-done.1, f32[5,16,16,256]{3,2,1,0:T(8,128)S(1)} %copy-done.3, f32[16,16,256]{2,1,0:T(8,128)S(1)} %copy-done.4, ...), custom_call_target="tpu_custom_call" | custom-call | tf_op jit(solution)/shard_map/second/pallas_call | solution.py:363
  (9 shorter events, 0.1 us)
Async XLA Ops:
  0.7 1.3 %copy-start = (f32[5,16,16,256]{3,2,1,0:T(8,128)S(1)}, f32[5,16,16,256]{3,2,1,0:T(8,128)}, u32[]{:S(2)}) copy-start(f32[5,16,16,256]{3,2,1,0:T(8,128)} %q_now.3) | copy-start | bytes 3932164
  2.0 1.3 %copy-start.2 = (f32[5,16,16,256]{3,2,1,0:T(8,128)S(1)}, f32[5,16,16,256]{3,2,1,0:T(8,128)}, u32[]{:S(2)}) copy-start(f32[5,16,16,256]{3,2,1,0:T(8,128)} %q_prev.3) | copy-start | bytes 3932164
  3.3 0.7 %copy-start.5 = (f32[3,1024]{1,0:T(4,128)S(1)}, f32[3,1024]{1,0:T(4,128)}, u32[]{:S(2)}) copy-start(f32[3,1024]{1,0:T(4,128)} %frac_in.1) | copy-start | bytes 36868
  4.0 0.7 %copy-start.6 = (s32[1024]{0:T(1024)S(1)}, s32[1024]{0:T(1024)}, u32[]{:S(2)}) copy-start(s32[1024]{0:T(1024)} %param.13) | copy-start | bytes 12292
  4.7 0.7 %copy-start.7 = (s32[1024,1]{0,1:T(1,128)S(1)}, s32[1024,1]{0,1:T(1,128)}, u32[]{:S(2)}) copy-start(s32[1024,1]{0,1:T(1,128)} %param.15) | copy-start | bytes 12292
  5.4 0.7 %copy-start.8 = (s32[1024]{0:T(1024)S(1)}, s32[1024]{0:T(1024)}, u32[]{:S(2)}) copy-start(s32[1024]{0:T(1024)} %param.16) | copy-start | bytes 12292
  6.1 13.4 %copy-start.1 = (f32[5,16,16,256]{3,2,1,0:T(8,128)S(1)}, f32[5,16,16,256]{3,2,1,0:T(8,128)}, u32[]{:S(2)}) copy-start(f32[5,16,16,256]{3,2,1,0:T(8,128)} %q_now.3) | copy-start | bytes 3932164
  13.1 13.6 %copy-start.9 = (f32[3,2,5,5]{3,1,2,0:T(2,128)S(1)}, f32[3,2,5,5]{3,1,2,0:T(2,128)}, u32[]{:S(2)}) copy-start(f32[3,2,5,5]{3,1,2,0:T(2,128)} %param.12) | copy-start | bytes 1804
  13.1 17.5 %copy-start.4 = (f32[16,16,256]{2,1,0:T(8,128)S(1)}, f32[16,16,256]{2,1,0:T(8,128)}, u32[]{:S(2)}) copy-start(f32[16,16,256]{2,1,0:T(8,128)} %jac.3) | copy-start | bytes 786436
  13.1 17.4 %all-to-all-start = ((f32[32,8,128]{2,1,0:T(8,128)}), f32[32,8,128]{2,1,0:T(8,128)S(1)}, u32[]{:S(2)}, u32[]{:S(2)}) async-start(f32[32,8,128]{2,1,0:T(8,128)} %donor.1), calls=%async_computation | async-start | bytes 262144 | tf_op jit(solution)/shard_map/all_to_all | solution.py:325
  19.5 7.3 %collective-permute-start.1 = (f32[5,16,256]{2,1,0:T(8,128)S(1)}, f32[5,16,256]{2,1,0:T(8,128)S(1)}, u32[]{:S(2)}, u32[]{:S(2)}) collective-permute-start(f32[5,16,256]{2,1,0:T(8,128)S(1)} %get-tuple-element.21), channel_id=1, source_target_pairs={{0,8},{8,0},{16,24},{24,16},{1,9},{9,1},{17,25},{25,17},{2,10},{10... | collective-permute-start | bytes 245768 | tf_op jit(solution)/shard_map/ppermute | solution.py:269
  19.9 6.8 %collective-permute-start = (f32[5,16,256]{2,1,0:T(8,128)S(1)}, f32[5,16,256]{2,1,0:T(8,128)S(1)}, u32[]{:S(2)}, u32[]{:S(2)}) collective-permute-start(f32[5,16,256]{2,1,0:T(8,128)S(1)} %get-tuple-element.22), channel_id=1, source_target_pairs={{8,16},{16,8},{9,17},{17,9},{10,18},{18,10},{11,19},{19,11},{12,20... | collective-permute-start | bytes 245768 | tf_op jit(solution)/shard_map/ppermute | solution.py:270
  23.2 3.6 %collective-permute-start.3 = (f32[5,16,256]{2,1,0:T(8,128)S(1)}, f32[5,16,256]{2,1,0:T(8,128)S(1)}, u32[]{:S(2)}, u32[]{:S(2)}) collective-permute-start(f32[5,16,256]{2,1,0:T(8,128)S(1)} %get-tuple-element.33), channel_id=1, source_target_pairs={{0,1},{1,0},{2,3},{3,2},{4,5},{5,4},{6,7},{7,6},{8,9},{9,8},{10,11... | collective-permute-start | bytes 245768 | tf_op jit(solution)/shard_map/ppermute | solution.py:269
  24.4 6.1 %collective-permute-start.2 = (f32[5,16,256]{2,1,0:T(8,128)S(1)}, f32[5,16,256]{2,1,0:T(8,128)S(1)}, u32[]{:S(2)}, u32[]{:S(2)}) collective-permute-start(f32[5,16,256]{2,1,0:T(8,128)S(1)} %get-tuple-element.34), channel_id=1, source_target_pairs={{1,2},{2,1},{3,4},{4,3},{5,6},{6,5},{9,10},{10,9},{11,12},{12,11},... | collective-permute-start | bytes 245768 | tf_op jit(solution)/shard_map/ppermute | solution.py:270
  41.7 10.6 %copy-start.3 = (f32[5,16,16,256]{3,2,1,0:T(8,128)S(1)}, f32[5,16,16,256]{3,2,1,0:T(8,128)}, u32[]{:S(2)}) copy-start(f32[5,16,16,256]{3,2,1,0:T(8,128)} %q_prev.3) | copy-start | bytes 3932164
  41.7 6.4 %collective-permute-start.5 = (f32[5,16,256]{2,1,0:T(8,128)S(1)}, f32[5,16,256]{2,1,0:T(8,128)S(1)}, u32[]{:S(2)}, u32[]{:S(2)}) collective-permute-start(f32[5,16,256]{2,1,0:T(8,128)S(1)} %get-tuple-element.29), channel_id=1, source_target_pairs={{0,8},{8,0},{16,24},{24,16},{1,9},{9,1},{17,25},{25,17},{2,10},{10... | collective-permute-start | bytes 245768 | tf_op jit(solution)/shard_map/ppermute | solution.py:269
  41.8 6.3 %collective-permute-start.4 = (f32[5,16,256]{2,1,0:T(8,128)S(1)}, f32[5,16,256]{2,1,0:T(8,128)S(1)}, u32[]{:S(2)}, u32[]{:S(2)}) collective-permute-start(f32[5,16,256]{2,1,0:T(8,128)S(1)} %get-tuple-element.30), channel_id=1, source_target_pairs={{8,16},{16,8},{9,17},{17,9},{10,18},{18,10},{11,19},{19,11},{12,20... | collective-permute-start | bytes 245768 | tf_op jit(solution)/shard_map/ppermute | solution.py:270
  45.9 3.4 %collective-permute-start.7 = (f32[5,16,256]{2,1,0:T(8,128)S(1)}, f32[5,16,256]{2,1,0:T(8,128)S(1)}, u32[]{:S(2)}, u32[]{:S(2)}) collective-permute-start(f32[5,16,256]{2,1,0:T(8,128)S(1)} %get-tuple-element.25), channel_id=1, source_target_pairs={{0,1},{1,0},{2,3},{3,2},{4,5},{5,4},{6,7},{7,6},{8,9},{9,8},{10,11... | collective-permute-start | bytes 245768 | tf_op jit(solution)/shard_map/ppermute | solution.py:269
  46.2 6.1 %collective-permute-start.6 = (f32[5,16,256]{2,1,0:T(8,128)S(1)}, f32[5,16,256]{2,1,0:T(8,128)S(1)}, u32[]{:S(2)}, u32[]{:S(2)}) collective-permute-start(f32[5,16,256]{2,1,0:T(8,128)S(1)} %get-tuple-element.26), channel_id=1, source_target_pairs={{1,2},{2,1},{3,4},{4,3},{5,6},{6,5},{9,10},{10,9},{11,12},{12,11},... | collective-permute-start | bytes 245768 | tf_op jit(solution)/shard_map/ppermute | solution.py:270

commit v2 on v1

--- a/solution.py
+++ b/solution.py
@@ -6,6 +6,7 @@
 from jax.experimental import pallas as pl
 from jax.experimental.pallas import tpu as pltpu
 from jax.sharding import PartitionSpec as P
+
 
 step_tau = 0.2
 step_phys = 0.5
@@ -119,7 +120,7 @@
 
 
 def mixing_weights(coef, high, low, size):
-    nvars, size_x, size_y, size_z = size
+    nvars, _, size_y, _ = size
     block = nvars * size_y
     width = 3 * block + CHANNELS
     row = iota((size_y, width), 0)
@@ -151,7 +152,7 @@
 
 
 def fill_planes(state, x_low, x_high, y_low, y_high, planes, sides, size):
-    nvars, size_x, size_y, size_z = size
+    nvars, size_x, size_y, _ = size
     block = nvars * size_y
     for x in range(size_x + 2):
         for v in range(nvars):
@@ -165,7 +166,7 @@
 
 
 def flux_at(x, weights, planes, sides, size):
-    nvars, size_x, size_y, size_z = size
+    nvars, _, size_y, size_z = size
     block = nvars * size_y
     high, low = halves(sides[x])
     rows = slice(x * block, (x + 3) * block)
@@ -181,12 +182,37 @@
     return [flux[v * size_y : (v + 1) * size_y] for v in range(nvars)]
 
 
-def first_kernel(coef, q_now, q_prev, jac, got, x_low, x_high, y_low, y_high, state, target, hits, face_xl, face_xh, face_yl, face_yh, weights, rows, hot_xy, hot_z, grid, planes, sides, *, size, devices, capacity):
+def early_kernel(coef, q_now, q_prev, jac, x_low, x_high, y_low, y_high, base, weights, planes, sides, *, size):
+    nvars, size_x, _, _ = size
+    mixing_weights(coef, weights.at[0], weights.at[1], size)
+    fill_planes(q_now, x_low, x_high, y_low, y_high, planes, sides, size)
+    for x in range(size_x):
+        flux = flux_at(x, weights, planes, sides, size)
+        scale = step_tau * jac[x]
+        for v in range(nvars):
+            centre = q_now[v, x]
+            physical = (q_prev[v, x] - centre) / (2.0 * step_phys)
+            base[v, x] = centre - scale * (flux[v] + physical)
+
+
+def land(rows, hot_xy, hot_z, store, nvars):
+    columns = hot_xy.shape[0]
+    for first in range(0, nvars, 2):
+        some = range(first, min(first + 2, nvars))
+        pieces = []
+        for c in some:
+            for half in halves(rows[c : c + 1, :]):
+                pieces.append(hot_xy[...] * half)
+        landed = dot(jnp.concatenate(pieces, axis=0), hot_z[...], ((1,), (0,)))
+        for c in some:
+            at = 2 * (c - first) * columns
+            store(c, landed[at : at + columns] + landed[at + columns : at + 2 * columns])
+
+
+def first_kernel(got, base, q_now, jac, state, hits, face_xl, face_xh, face_yl, face_yh, later, hot_xy, hot_z, rows, grid, *, size, devices, capacity):
     nvars, size_x, size_y, size_z = size
     columns = size_x * size_y
     slots = devices * capacity
-    mixing_weights(coef, weights.at[0], weights.at[1], size)
-    fill_planes(q_now, x_low, x_high, y_low, y_high, planes, sides, size)
     for d in range(devices):
         piece = got[d]
         lanes = slice(d * capacity, (d + 1) * capacity)
@@ -197,31 +223,19 @@
     hot_z[...] = (iota((slots, size_z), 1).astype(jnp.float32) == land_z).astype(jnp.float32).astype(jnp.bfloat16)
     land_xy = rows[2 * nvars : 2 * nvars + 1, :]
     hot_xy[...] = ((iota((columns, slots), 0) + 1).astype(jnp.float32) == land_xy).astype(jnp.float32).astype(jnp.bfloat16)
-
-    def pair(g, carry):
-        pieces = []
-        for c in range(2):
-            for half in halves(rows[pl.ds(2 * g + c, 1), :]):
-                pieces.append(hot_xy[...] * half)
-        landed = dot(jnp.concatenate(pieces, axis=0), hot_z[...], ((1,), (0,)))
-        for c in range(2):
-            at = 2 * c * columns
-            grid[2 * g + c] = landed[at : at + columns] + landed[at + columns : at + 2 * columns]
-        return carry
-
-    lax.fori_loop(0, nvars, pair, 0)
+    later[...] = rows[nvars : 2 * nvars, :]
+
+    def keep(c, value):
+        grid[c] = value
+
     hits[...] = dot(hot_xy[...], hot_z[...], ((1,), (0,)))
-    target[...] = grid[nvars : 2 * nvars]
+    land(rows, hot_xy, hot_z, keep, nvars)
     for x in range(size_x):
         at = slice(x * size_y, (x + 1) * size_y)
-        flux = flux_at(x, weights, planes, sides, size)
         landed = hits[at, :]
-        scale = step_tau * jac[x]
+        scale = (step_tau * penalty) * jac[x]
         for v in range(nvars):
-            centre = q_now[v, x]
-            physical = (q_prev[v, x] - centre) / (2.0 * step_phys)
-            coupling = penalty * (landed * centre - grid[v, at, :])
-            new = centre - scale * (flux[v] + physical + coupling)
+            new = base[v, x] - scale * (landed * q_now[v, x] - grid[v, at, :])
             state[v, x] = new
             face_yl[v, x : x + 1, :] = new[0:1]
             face_yh[v, x : x + 1, :] = new[size_y - 1 : size_y]
@@ -231,9 +245,15 @@
                 face_xh[v] = new
 
 
-def second_kernel(coef, state, q_now, q_prev, jac, target, hits, x_low, x_high, y_low, y_high, out, weights, planes, sides, buffer, sems, *, size):
-    nvars, size_x, size_y, size_z = size
-    mixing_weights(coef, weights.at[0], weights.at[1], size)
+def late_kernel(rows, hot_xy, hot_z, target):
+    def keep(c, value):
+        target[c] = value
+
+    land(rows, hot_xy, hot_z, keep, rows.shape[0])
+
+
+def second_kernel(state, weights, q_now, q_prev, jac, target, hits, x_low, x_high, y_low, y_high, out, planes, sides, buffer, sems, *, size):
+    nvars, size_x, size_y, _ = size
     fill_planes(state, x_low, x_high, y_low, y_high, planes, sides, size)
     part = size_x // 4
     copies = []
@@ -272,13 +292,19 @@
 
 
 def params(limit):
-    return pltpu.CompilerParams(vmem_limit_bytes=limit * MIB)
+    return pltpu.CompilerParams(vmem_limit_bytes=limit)
+
+
+def edges(halo, axis):
+    here, last = lax.axis_index(axis), lax.axis_size(axis) - 1
+    return jnp.where(here == 0, 0.0, halo[0]), jnp.where(here == last, 0.0, halo[1])
 
 
 def body(q_now, q_prev, jacobian, flux_split, donor_base, donor_frac, fringe_dest, receptor_cell, fringe_count):
     size = q_now.shape
     nvars, size_x, size_y, size_z = size
     columns = size_x * size_y
+    block = nvars * size_y
     devices = lax.axis_size("gx") * lax.axis_size("gy")
     rows = donor_base.shape[0]
     capacity = 2 * rows // devices
@@ -287,15 +313,22 @@
     smem = pl.BlockSpec(memory_space=pltpu.SMEM)
     hbm = pl.BlockSpec(memory_space=pltpu.HBM)
     vmem = pl.BlockSpec(memory_space=pltpu.VMEM)
-    coef = flux_split.reshape(-1)
-    block = nvars * size_y
-    weights = pltpu.VMEM((2, 3 * block, 3 * block + CHANNELS), bf16)
+    flat = (nvars, columns, size_z)
+    shape = jax.ShapeDtypeStruct
+    weights_shape = (2, 3 * block, 3 * block + CHANNELS)
     planes = pltpu.VMEM((2, (size_x + 2) * block, size_z), bf16)
     sides = pltpu.VMEM((size_x, CHANNELS, size_z), f32)
-    flat = (nvars, columns, size_z)
+    face_x, face_y = shape((nvars, size_y, size_z), f32), shape((nvars, size_x, size_z), f32)
+
+    def halos(low_x, high_x, low_y, high_y):
+        x_halo = exchanged(low_x, high_x, "gx")
+        y_halo = exchanged(low_y, high_y, "gy")
+        return *edges(x_halo, "gx"), *edges(y_halo, "gy")
+
+    around = halos(q_now[:, 0], q_now[:, size_x - 1], q_now[:, :, 0], q_now[:, :, size_y - 1])
     sent = pl.pallas_call(
         functools.partial(donor_kernel, size=size, devices=devices, capacity=capacity),
-        out_shape=jax.ShapeDtypeStruct((devices, 8, 2 * capacity), f32),
+        out_shape=shape((devices, 8, 2 * capacity), f32),
         in_specs=[smem] + [hbm] * 6,
         out_specs=vmem,
         scratch_shapes=[
@@ -311,7 +344,7 @@
             pltpu.VMEM((1, rows), jnp.int32),
             pltpu.SemaphoreType.DMA((6,)),
         ],
-        compiler_params=params(48),
+        compiler_params=params(60 * 1024 * 1024),
         name="donor",
     )(
         fringe_count,
@@ -323,52 +356,52 @@
         receptor_cell.reshape(1, rows),
     )
     got = lax.all_to_all(sent, AXES, split_axis=0, concat_axis=0, tiled=True)
-    x_halo = exchanged(q_now[:, 0], q_now[:, size_x - 1], "gx")
-    y_halo = exchanged(q_now[:, :, 0], q_now[:, :, size_y - 1], "gy")
-    face_x = jax.ShapeDtypeStruct((nvars, size_y, size_z), f32)
-    face_y = jax.ShapeDtypeStruct((nvars, size_x, size_z), f32)
-
-    def edges(halo, axis):
-        here, last = lax.axis_index(axis), lax.axis_size(axis) - 1
-        return jnp.where(here == 0, 0.0, halo[0]), jnp.where(here == last, 0.0, halo[1])
-
-    x_halo, y_halo = edges(x_halo, "gx"), edges(y_halo, "gy")
-    state, target, hits, *faces = pl.pallas_call(
+    base, weights = pl.pallas_call(
+        functools.partial(early_kernel, size=size),
+        out_shape=[shape(size, f32), shape(weights_shape, bf16)],
+        in_specs=[smem] + [vmem] * 7,
+        out_specs=[vmem] * 2,
+        scratch_shapes=[planes, sides],
+        compiler_params=params(20 * MIB),
+        name="early",
+    )(flux_split.reshape(-1), q_now, q_prev, jacobian, *around)
+    state, hits, *faces, later, hot_xy, hot_z = pl.pallas_call(
         functools.partial(first_kernel, size=size, devices=devices, capacity=capacity),
         out_shape=[
-            jax.ShapeDtypeStruct(size, f32),
-            jax.ShapeDtypeStruct(flat, f32),
-            jax.ShapeDtypeStruct((columns, size_z), f32),
+            shape(size, f32),
+            shape((columns, size_z), f32),
             face_x,
             face_x,
             face_y,
             face_y,
+            shape((nvars, slots), f32),
+            shape((columns, slots), bf16),
+            shape((slots, size_z), bf16),
         ],
-        in_specs=[smem] + [vmem] * 8,
-        out_specs=[vmem] * 7,
-        scratch_shapes=[
-            weights,
-            pltpu.VMEM((CHANNELS, slots), f32),
-            pltpu.VMEM((columns, slots), bf16),
-            pltpu.VMEM((slots, size_z), bf16),
-            pltpu.VMEM((2 * nvars, columns, size_z), f32),
-            planes,
-            sides,
-        ],
-        compiler_params=params(48),
+        in_specs=[vmem] * 4,
+        out_specs=[vmem] * 9,
+        scratch_shapes=[pltpu.VMEM((CHANNELS, slots), f32), pltpu.VMEM((nvars, columns, size_z), f32)],
+        compiler_params=params(20 * MIB),
         name="first",
-    )(coef, q_now, q_prev, jacobian, got, *x_halo, *y_halo)
-    x_halo = edges(exchanged(faces[0], faces[1], "gx"), "gx")
-    y_halo = edges(exchanged(faces[2], faces[3], "gy"), "gy")
+    )(got, base, q_now, jacobian)
+    around = halos(*faces)
+    target = pl.pallas_call(
+        late_kernel,
+        out_shape=shape(flat, f32),
+        in_specs=[vmem] * 3,
+        out_specs=vmem,
+        compiler_params=params(20 * MIB),
+        name="late",
+    )(later, hot_xy, hot_z)
     return pl.pallas_call(
         functools.partial(second_kernel, size=size),
-        out_shape=jax.ShapeDtypeStruct(size, f32),
-        in_specs=[smem] + [vmem] * 10,
+        out_shape=shape(size, f32),
+        in_specs=[vmem] * 11,
         out_specs=hbm,
-        scratch_shapes=[weights, planes, sides, pltpu.VMEM(size, f32), pltpu.SemaphoreType.DMA((4,))],
-        compiler_params=params(40),
+        scratch_shapes=[planes, sides, pltpu.VMEM(size, f32), pltpu.SemaphoreType.DMA((4,))],
+        compiler_params=params(20 * MIB),
         name="second",
-    )(coef, state, q_now, q_prev, jacobian, target, hits, *x_halo, *y_halo)
+    )(state, weights, q_now, q_prev, jacobian, target, hits, *around)
 
 
 def solution(mesh):

time: 56.3 us -> 50.1 us (0.89)
  local copies, waits for them, and re-layouts: 5.64 us -> 2.61 us
  waiting for transfers between devices: 7.82 us -> 5.08 us
  Pallas kernels: 21.6 us -> 19.5 us
  other arithmetic: 0.13 us -> 1.67 us
    pallas_call x1, Pallas kernels: 11.2 us -> 3.7 us  [body(): pl.pallas_call(functools.partial(first_kernel, size=size, devices=devices...]
    pallas_call x1 -> x3, Pallas kernels: 3.46 us -> 8.13 us  [the longest x1 2.86 us: body(): pl.pallas_call(late_kernel, out_shape=shape(flat, f32), in_specs=[vmem] *...]
    unnamed x21 -> x13, local copies, waits for them, and re-layouts: 5.43 us -> 2.39 us
    ppermute x4, waiting for transfers between devices: 6.76 us -> 5.06 us  [exchanged(): lax.ppermute(jnp.where(even, low_face, high_face), axis, swap_pairs(axis,...]
    ppermute x4, waiting for transfers between devices: 1.06 us -> 0.01 us  [exchanged(): lax.ppermute(jnp.where(even, high_face, low_face), axis, swap_pairs(axis,...]
    select_n x4, other arithmetic: 0.07 us -> 0.96 us  [edges(): jnp.where(here == last, 0.0, halo[1])]
    select_n x4, other arithmetic: 0.06 us -> 0.71 us  [exchanged(): jnp.where(even, high_face, low_face)]
    pallas_call x1, Pallas kernels: 6.99 us -> 7.63 us  [body(): pl.pallas_call(functools.partial(donor_kernel, size=size, devices=devices...]
  transfers between devices with their start and end apart: 9 -> 9, of which waited for: 3 -> 2; matrix products, arithmetic and copies ran while one was open for 1% -> 4% of each run, Pallas kernels for 0% -> 11%
where the time goes in v2:
time: 50.1 us; the launch traced here: 49.6 us
  starting transfers between devices  19.6 us (39%)
  Pallas kernels  19.5 us (39%)
  waiting for transfers between devices  5.08 us (10%)
  local copies, waits for them, and re-layouts  2.61 us (5%)
  other arithmetic  1.67 us (3%)
  between operations  1.12 us (2%)
    ppermute x4, starting transfers between devices, exchanged(): lax.ppermute(jnp.where(even, low_face, high_face), axis, swap_pairs(axis,...  11.2 us
    pallas_call x1, Pallas kernels, body(): pl.pallas_call(functools.partial(donor_kernel, size=size, devices=devices...  7.63 us
    all_to_all x1, starting transfers between devices, body(): got = lax.all_to_all(sent, AXES, split_axis=0, concat_axis=0, tiled=True)  6.32 us
    ppermute x4, waiting for transfers between devices, exchanged(): lax.ppermute(jnp.where(even, low_face, high_face), axis, swap_pairs(axis,...  5.06 us
    pallas_call x1, Pallas kernels, body(): pl.pallas_call(functools.partial(first_kernel, size=size, devices=devices...  3.7 us
    pallas_call x1, Pallas kernels, body(): pl.pallas_call(late_kernel, out_shape=shape(flat, f32), in_specs=[vmem] *...  2.86 us
    pallas_call x1, Pallas kernels, body(): pl.pallas_call(functools.partial(second_kernel, size=size), out_shape=sha...  2.69 us
    pallas_call x1, Pallas kernels, body(): pl.pallas_call(functools.partial(early_kernel, size=size), out_shape=[sha...  2.57 us
  transfers between devices with their start and end apart: 9, of which 2 were waited for; matrix products, arithmetic and copies ran while one was open for 4% of the time, Pallas kernels for 11%

profile of v2, /device:TPU:9, one launch (start us, length us, event | category | flops | bytes accessed | tf_op | source)
XLA Modules:
  0.0 49.6 jit_solution(1821869397130075063)
XLA Ops:
  0.7 0.0 copy-start
  0.7 0.0 copy-start.5
  0.7 7.6 %donor.1 = f32[32,8,128]{2,1,0:T(8,128)} custom-call(s32[1]{0:T(128)S(6)} %copy.27.count, f32[5,256,256]{2,1,0:T(8,128)} %bitcast.24, f32[5,256,256]{2,1,0:T(8,128)} %bitcast.23, s32[1,1024]{1,0:T(1,128)} %bitcast.25, f32[3,1024]{1,0:T(4,128)} %frac_in.1, s32[1,1024]{1,0:T(1,128)} %bitcast.26, s32[1,1024]{1,0:T(1,128)} %bitcast.27), custom_call_target="tpu_custom_call" | custom-call | tf_op jit(solution)/shard_map/donor/pallas_call | solution.py:329
  8.3 0.0 copy-start.1
  8.3 0.0 copy-start.2
  8.3 6.3 %all-to-all-start = ((f32[32,8,128]{2,1,0:T(8,128)}), f32[32,8,128]{2,1,0:T(8,128)S(1)}, u32[]{:S(2)}, u32[]{:S(2)}) async-start(f32[32,8,128]{2,1,0:T(8,128)} %donor.1), calls=%async_computation | async-start | bytes 262144 | tf_op jit(solution)/shard_map/all_to_all | solution.py:358
  14.7 0.0 copy-done
  14.7 0.5 collective-permute-start.1
  15.2 3.1 %collective-permute-start = (f32[5,16,256]{2,1,0:T(8,128)S(1)}, f32[5,16,256]{2,1,0:T(8,128)S(1)}, u32[]{:S(2)}, u32[]{:S(2)}) collective-permute-start(f32[5,16,256]{2,1,0:T(8,128)S(1)} %get-tuple-element.30), channel_id=1, source_target_pairs={{8,16},{16,8},{9,17},{17,9},{10,18},{18,10},{11,19},{19,11},{12,20... | collective-permute-start | bytes 245768 | tf_op jit(solution)/shard_map/ppermute | solution.py:290
  18.3 0.1 fusion.2
  18.4 0.7 %select_bitcast_fusion = (f32[5,16,256]{2,1,0:T(8,128)}, f32[5,16,256]{2,1,0:T(8,128)}) fusion(f32[5,16,1,256]{3,2,1,0:T(1,128)S(1)} %get-tuple-element.28, f32[5,16,1,256]{3,2,1,0:T(1,128)S(1)} %get-tuple-element.27, pred[]{:T(512)S(6)} %eq.33), kind=kLoop, calls=%fused_computation.10 | loop fusion | flops 40960 | bytes 327681 | tf_op jit(solution)/shard_map/jit(_where)/select_n | solution.py:289
  19.1 1.2 %collective-permute-start.3 = (f32[5,16,256]{2,1,0:T(8,128)}, f32[5,16,256]{2,1,0:T(8,128)S(1)}, u32[]{:S(2)}, u32[]{:S(2)}) collective-permute-start(f32[5,16,256]{2,1,0:T(8,128)} %get-tuple-element.41), channel_id=1, source_target_pairs={{0,1},{1,0},{2,3},{3,2},{4,5},{5,4},{6,7},{7,6},{8,9},{9,8},{10,11... | collective-permute-start | bytes 245768 | tf_op jit(solution)/shard_map/ppermute | solution.py:289
  20.2 2.2 %collective-permute-start.2 = (f32[5,16,256]{2,1,0:T(8,128)}, f32[5,16,256]{2,1,0:T(8,128)}, u32[]{:S(2)}, u32[]{:S(2)}) collective-permute-start(f32[5,16,256]{2,1,0:T(8,128)} %get-tuple-element.42), channel_id=1, source_target_pairs={{1,2},{2,1},{3,4},{4,3},{5,6},{6,5},{9,10},{10,9},{11,12},{12,11},... | collective-permute-start | bytes 245768 | tf_op jit(solution)/shard_map/ppermute | solution.py:290
  22.4 0.0 copy-done.5
  22.5 0.1 reshape.31.coef
  22.6 0.0 collective-permute-done.1
  22.6 0.0 collective-permute-done
  22.6 0.0 collective-permute-done.3
  22.6 4.0 %collective-permute-done.2 = f32[5,16,256]{2,1,0:T(8,128)} collective-permute-done((f32[5,16,256]{2,1,0:T(8,128)}, f32[5,16,256]{2,1,0:T(8,128)}, u32[]{:S(2)}, u32[]{:S(2)}) %collective-permute-start.2) | collective-permute-done | bytes 81952 | tf_op jit(solution)/shard_map/ppermute | solution.py:290
  26.6 0.9 %select_select_fusion.4 = (f32[5,16,256]{2,1,0:T(8,128)S(1)}, f32[5,16,256]{2,1,0:T(8,128)S(1)}) fusion(f32[5,16,256]{2,1,0:T(8,128)S(1)} %collective-permute-done.3, f32[5,16,256]{2,1,0:T(8,128)} %collective-permute-done.2, pred[]{:T(512)S(6)} %eq.34, pred[]{:T(512)S(6)} %eq.33, pred[]{:T(512)S(6)} %eq.32), kind=kLoop, calls=%fused_computation.8 | loop fusion | flops 81920 | bytes 327683 | tf_op jit(solution)/shard_map/jit(_where)/select_n | solution.py:300
  27.5 0.0 copy-done.1
  27.6 0.0 copy-done.2
  27.6 2.6 %early.1 = (f32[5,16,16,256]{3,2,1,0:T(8,128)S(1)}, bf16[2,240,256]{2,1,0:T(8,128)(2,1)S(1)}) custom-call(f32[150]{0:T(256)S(1)} %reshape.31.coef, f32[5,16,16,256]{3,2,1,0:T(8,128)S(1)} %copy-done, f32[5,16,16,256]{3,2,1,0:T(8,128)S(1)} %copy-done.1, f32[16,16,256]{2,1,0:T(8,128)S(1)} %copy-done.2, f32[5,16,256]{2,1,0:T(8,128)S(1)} %get-tuple-element.44.x_low, ...), custom_call_target="tpu_custom_call" | custom-call | tf_op jit(solution)/shard_map/early/pallas_call | solution.py:359
  30.1 0.0 copy-start.3
  30.2 1.0 %copy-done.3 = f32[5,16,16,256]{3,2,1,0:T(8,128)} copy-done((f32[5,16,16,256]{3,2,1,0:T(8,128)}, f32[5,16,16,256]{3,2,1,0:T(8,128)S(1)}, u32[]{:S(2)}) %copy-start.3) | copy-done | bytes 1310744
  31.2 0.0 all-to-all-done.got
  31.2 0.0 copy-start.4
  31.2 1.3 %copy-done.4 = f32[5,16,16,256]{3,2,1,0:T(8,128)S(1)} copy-done((f32[5,16,16,256]{3,2,1,0:T(8,128)S(1)}, f32[5,16,16,256]{3,2,1,0:T(8,128)}, u32[]{:S(2)}) %copy-start.4) | copy-done | bytes 1310744
  32.5 3.7 %first.1 = (f32[5,16,16,256]{3,2,1,0:T(8,128)S(1)}, f32[256,256]{1,0:T(8,128)S(1)}, f32[5,16,256]{2,1,0:T(8,128)S(1)}, f32[5,16,256]{2,1,0:T(8,128)S(1)}, f32[5,...) custom-call(f32[32,8,128]{2,1,0:T(8,128)S(1)} %all-to-all-done.got, ...), custom_call_target="tpu_custom_call" | custom-call | tf_op jit(solution)/shard_map/first/pallas_call | solution.py:368
  36.3 0.1 collective-permute-start.5
  36.3 3.9 %collective-permute-start.4 = (f32[5,16,256]{2,1,0:T(8,128)S(1)}, f32[5,16,256]{2,1,0:T(8,128)S(1)}, u32[]{:S(2)}, u32[]{:S(2)}) collective-permute-start(f32[5,16,256]{2,1,0:T(8,128)S(1)} %get-tuple-element.38), channel_id=1, source_target_pairs={{8,16},{16,8},{9,17},{17,9},{10,18},{18,10},{11,19},{19,11},{12,20... | collective-permute-start | bytes 245768 | tf_op jit(solution)/shard_map/ppermute | solution.py:290
  40.3 0.4 collective-permute-start.7
  40.6 2.1 %collective-permute-start.6 = (f32[5,16,256]{2,1,0:T(8,128)S(1)}, f32[5,16,256]{2,1,0:T(8,128)S(1)}, u32[]{:S(2)}, u32[]{:S(2)}) collective-permute-start(f32[5,16,256]{2,1,0:T(8,128)S(1)} %get-tuple-element.34), channel_id=1, source_target_pairs={{1,2},{2,1},{3,4},{4,3},{5,6},{6,5},{9,10},{10,9},{11,12},{12,11},... | collective-permute-start | bytes 245768 | tf_op jit(solution)/shard_map/ppermute | solution.py:290
  42.7 2.9 %late.1.target = f32[5,256,256]{2,1,0:T(8,128)S(1)} custom-call(f32[5,2048]{1,0:T(8,128)S(1)} %get-tuple-element.19.rows, bf16[256,2048]{1,0:T(8,128)(2,1)S(1)} %get-tuple-element.20.hot_xy, bf16[2048,256]{1,0:T(8,128)(2,1)S(1)} %get-tuple-element.21.hot_z), custom_call_target="tpu_custom_call" | custom-call | tf_op jit(solution)/shard_map/late/pallas_call | solution.py:388
  45.6 0.0 collective-permute-done.5
  45.6 0.0 collective-permute-done.4
  45.6 0.0 collective-permute-done.7
  45.6 1.0 %collective-permute-done.6 = f32[5,16,256]{2,1,0:T(8,128)S(1)} collective-permute-done((f32[5,16,256]{2,1,0:T(8,128)S(1)}, f32[5,16,256]{2,1,0:T(8,128)S(1)}, u32[]{:S(2)}, u32[]{:S(2)}) %collective-permute-start.6) | collective-permute-done | bytes 81952 | tf_op jit(solution)/shard_map/ppermute | solution.py:290
  46.7 2.7 %second.1 = f32[5,16,16,256]{3,2,1,0:T(8,128)} custom-call(f32[5,16,16,256]{3,2,1,0:T(8,128)S(1)} %get-tuple-element.17.state, bf16[2,240,256]{2,1,0:T(8,128)(2,1)S(1)} %get-tuple-element.18.weights, f32[5,16,16,256]{3,2,1,0:T(8,128)S(1)} %copy-done, f32[5,16,16,256]{3,2,1,0:T(8,128)S(1)} %copy-done.1, f32[16,16,256]{2,1,0:T(8,128)S(1)} %copy-done.2, ...), custom_call_target="tpu_custom_call" | custom-call | tf_op jit(solution)/shard_map/second/pallas_call | solution.py:396
  (7 shorter events, 0.1 us)
Async XLA Ops:
  0.7 14.0 %copy-start = (f32[5,16,16,256]{3,2,1,0:T(8,128)S(1)}, f32[5,16,16,256]{3,2,1,0:T(8,128)}, u32[]{:S(2)}) copy-start(f32[5,16,16,256]{3,2,1,0:T(8,128)} %q_now.5) | copy-start | bytes 3932164
  0.7 21.8 %copy-start.5 = (f32[3,2,5,5]{3,1,2,0:T(2,128)S(1)}, f32[3,2,5,5]{3,1,2,0:T(2,128)}, u32[]{:S(2)}) copy-start(f32[3,2,5,5]{3,1,2,0:T(2,128)} %param.12) | copy-start | bytes 1804
  8.3 19.2 %copy-start.1 = (f32[5,16,16,256]{3,2,1,0:T(8,128)S(1)}, f32[5,16,16,256]{3,2,1,0:T(8,128)}, u32[]{:S(2)}) copy-start(f32[5,16,16,256]{3,2,1,0:T(8,128)} %q_prev.3) | copy-start | bytes 3932164
  8.3 19.2 %copy-start.2 = (f32[16,16,256]{2,1,0:T(8,128)S(1)}, f32[16,16,256]{2,1,0:T(8,128)}, u32[]{:S(2)}) copy-start(f32[16,16,256]{2,1,0:T(8,128)} %jac.5) | copy-start | bytes 786436
  8.3 22.9 %all-to-all-start = ((f32[32,8,128]{2,1,0:T(8,128)}), f32[32,8,128]{2,1,0:T(8,128)S(1)}, u32[]{:S(2)}, u32[]{:S(2)}) async-start(f32[32,8,128]{2,1,0:T(8,128)} %donor.1), calls=%async_computation | async-start | bytes 262144 | tf_op jit(solution)/shard_map/all_to_all | solution.py:358
  14.7 7.9 %collective-permute-start.1 = (f32[5,16,256]{2,1,0:T(8,128)S(1)}, f32[5,16,256]{2,1,0:T(8,128)S(1)}, u32[]{:S(2)}, u32[]{:S(2)}) collective-permute-start(f32[5,16,256]{2,1,0:T(8,128)S(1)} %get-tuple-element.29), channel_id=1, source_target_pairs={{0,8},{8,0},{16,24},{24,16},{1,9},{9,1},{17,25},{25,17},{2,10},{10... | collective-permute-start | bytes 245768 | tf_op jit(solution)/shard_map/ppermute | solution.py:289
  15.2 7.4 %collective-permute-start = (f32[5,16,256]{2,1,0:T(8,128)S(1)}, f32[5,16,256]{2,1,0:T(8,128)S(1)}, u32[]{:S(2)}, u32[]{:S(2)}) collective-permute-start(f32[5,16,256]{2,1,0:T(8,128)S(1)} %get-tuple-element.30), channel_id=1, source_target_pairs={{8,16},{16,8},{9,17},{17,9},{10,18},{18,10},{11,19},{19,11},{12,20... | collective-permute-start | bytes 245768 | tf_op jit(solution)/shard_map/ppermute | solution.py:290
  19.1 3.6 %collective-permute-start.3 = (f32[5,16,256]{2,1,0:T(8,128)}, f32[5,16,256]{2,1,0:T(8,128)S(1)}, u32[]{:S(2)}, u32[]{:S(2)}) collective-permute-start(f32[5,16,256]{2,1,0:T(8,128)} %get-tuple-element.41), channel_id=1, source_target_pairs={{0,1},{1,0},{2,3},{3,2},{4,5},{5,4},{6,7},{7,6},{8,9},{9,8},{10,11... | collective-permute-start | bytes 245768 | tf_op jit(solution)/shard_map/ppermute | solution.py:289
  20.2 6.4 %collective-permute-start.2 = (f32[5,16,256]{2,1,0:T(8,128)}, f32[5,16,256]{2,1,0:T(8,128)}, u32[]{:S(2)}, u32[]{:S(2)}) collective-permute-start(f32[5,16,256]{2,1,0:T(8,128)} %get-tuple-element.42), channel_id=1, source_target_pairs={{1,2},{2,1},{3,4},{4,3},{5,6},{6,5},{9,10},{10,9},{11,12},{12,11},... | collective-permute-start | bytes 245768 | tf_op jit(solution)/shard_map/ppermute | solution.py:290
  30.1 1.1 %copy-start.3 = (f32[5,16,16,256]{3,2,1,0:T(8,128)}, f32[5,16,16,256]{3,2,1,0:T(8,128)S(1)}, u32[]{:S(2)}) copy-start(f32[5,16,16,256]{3,2,1,0:T(8,128)S(1)} %get-tuple-element.16.base) | copy-start | bytes 3932164
  31.2 1.3 %copy-start.4 = (f32[5,16,16,256]{3,2,1,0:T(8,128)S(1)}, f32[5,16,16,256]{3,2,1,0:T(8,128)}, u32[]{:S(2)}) copy-start(f32[5,16,16,256]{3,2,1,0:T(8,128)} %copy-done.3) | copy-start | bytes 3932164
  36.3 9.3 %collective-permute-start.5 = (f32[5,16,256]{2,1,0:T(8,128)S(1)}, f32[5,16,256]{2,1,0:T(8,128)S(1)}, u32[]{:S(2)}, u32[]{:S(2)}) collective-permute-start(f32[5,16,256]{2,1,0:T(8,128)S(1)} %get-tuple-element.37), channel_id=1, source_target_pairs={{0,8},{8,0},{16,24},{24,16},{1,9},{9,1},{17,25},{25,17},{2,10},{10... | collective-permute-start | bytes 245768 | tf_op jit(solution)/shard_map/ppermute | solution.py:289
  36.3 9.3 %collective-permute-start.4 = (f32[5,16,256]{2,1,0:T(8,128)S(1)}, f32[5,16,256]{2,1,0:T(8,128)S(1)}, u32[]{:S(2)}, u32[]{:S(2)}) collective-permute-start(f32[5,16,256]{2,1,0:T(8,128)S(1)} %get-tuple-element.38), channel_id=1, source_target_pairs={{8,16},{16,8},{9,17},{17,9},{10,18},{18,10},{11,19},{19,11},{12,20... | collective-permute-start | bytes 245768 | tf_op jit(solution)/shard_map/ppermute | solution.py:290
  40.3 5.4 %collective-permute-start.7 = (f32[5,16,256]{2,1,0:T(8,128)S(1)}, f32[5,16,256]{2,1,0:T(8,128)S(1)}, u32[]{:S(2)}, u32[]{:S(2)}) collective-permute-start(f32[5,16,256]{2,1,0:T(8,128)S(1)} %get-tuple-element.33), channel_id=1, source_target_pairs={{0,1},{1,0},{2,3},{3,2},{4,5},{5,4},{6,7},{7,6},{8,9},{9,8},{10,11... | collective-permute-start | bytes 245768 | tf_op jit(solution)/shard_map/ppermute | solution.py:289
  40.6 6.1 %collective-permute-start.6 = (f32[5,16,256]{2,1,0:T(8,128)S(1)}, f32[5,16,256]{2,1,0:T(8,128)S(1)}, u32[]{:S(2)}, u32[]{:S(2)}) collective-permute-start(f32[5,16,256]{2,1,0:T(8,128)S(1)} %get-tuple-element.34), channel_id=1, source_target_pairs={{1,2},{2,1},{3,4},{4,3},{5,6},{6,5},{9,10},{10,9},{11,12},{12,11},... | collective-permute-start | bytes 245768 | tf_op jit(solution)/shard_map/ppermute | solution.py:290

commit v3 on v2

--- a/solution.py
+++ b/solution.py
@@ -71,9 +71,8 @@
 
     along_z = weights(base_z, frac_z, (size_z, rows))
     high, low = halves(along_z)
-    spread[0:size_z, :] = high
-    spread[size_z : 2 * size_z, :] = low
-    spread[2 * size_z : 3 * size_z, :] = high
+    spread[0] = high
+    spread[1] = low
     along_x = weights(base_x, frac_x, (size_x, rows))
     along_y = weights(base_y, frac_y, (size_y, rows))
     for x in range(size_x):
@@ -92,13 +91,15 @@
         for v in range(nvars):
             at = pl.ds((k * nvars + v) * columns, columns)
             high, low = halves(planes[k, v])
-            lhs[at, 0:size_z] = high
-            lhs[at, size_z : 2 * size_z] = high
-            lhs[at, 2 * size_z : 3 * size_z] = low
+            lhs[0, at, :] = high
+            lhs[1, at, :] = low
     for n in range(rows // LANES):
         lanes = slice(n * LANES, (n + 1) * LANES)
         for k in range(2):
-            part = dot(lhs[k * nvars * columns : (k + 1) * nvars * columns, :], spread[:, lanes], ((1,), (0,)))
+            at = slice(k * nvars * columns, (k + 1) * nvars * columns)
+            part = dot(lhs[0, at, :], spread[0, :, lanes], ((1,), (0,)))
+            part = part + dot(lhs[0, at, :], spread[1, :, lanes], ((1,), (0,)))
+            part = part + dot(lhs[1, at, :], spread[0, :, lanes], ((1,), (0,)))
             for v in range(nvars):
                 picked = part[v * columns : (v + 1) * columns] * corner[:, lanes]
                 values[k * nvars + v : k * nvars + v + 1, lanes] = jnp.sum(picked, axis=0, keepdims=True)
@@ -151,24 +152,32 @@
             high[rows, :], low[rows, :] = halves(part)
 
 
-def fill_planes(state, x_low, x_high, y_low, y_high, planes, sides, size):
-    nvars, size_x, size_y, _ = size
+def fill_planes(state, around, planes, sides, size):
+    nvars, size_x, size_y, size_z = size
     block = nvars * size_y
     for x in range(size_x + 2):
         for v in range(nvars):
-            value = x_low[v] if x == 0 else x_high[v] if x == size_x + 1 else state[v, x - 1]
             rows = slice(x * block + v * size_y, x * block + (v + 1) * size_y)
-            planes[0, rows, :], planes[1, rows, :] = halves(value)
-    sides[...] = jnp.zeros(sides.shape, jnp.float32)
-    for v in range(nvars):
-        sides[:, v, :] = y_low[v]
-        sides[:, nvars + v, :] = y_high[v]
+            if 0 < x <= size_x:
+                planes[0, rows, :], planes[1, rows, :] = halves(state[v, x - 1])
+            elif around is None:
+                planes[0, rows, :] = planes[1, rows, :] = jnp.zeros((size_y, size_z), jnp.bfloat16)
+            else:
+                planes[0, rows, :], planes[1, rows, :] = halves(around[0 if x == 0 else 1][v])
+    if around is not None:
+        sides[...] = jnp.zeros(sides.shape, jnp.float32)
+        for v in range(nvars):
+            sides[:, v, :] = around[2][v]
+            sides[:, nvars + v, :] = around[3][v]
 
 
 def flux_at(x, weights, planes, sides, size):
     nvars, _, size_y, size_z = size
     block = nvars * size_y
-    high, low = halves(sides[x])
+    if sides is None:
+        high = low = jnp.zeros((CHANNELS, size_z), jnp.bfloat16)
+    else:
+        high, low = halves(sides[x])
     rows = slice(x * block, (x + 3) * block)
     around_high = jnp.concatenate([planes[0, rows, :], high], axis=0)
     around_low = jnp.concatenate([planes[1, rows, :], low], axis=0)
@@ -182,17 +191,43 @@
     return [flux[v * size_y : (v + 1) * size_y] for v in range(nvars)]
 
 
-def early_kernel(coef, q_now, q_prev, jac, x_low, x_high, y_low, y_high, base, weights, planes, sides, *, size):
+def sent_out(x, size_x, buffer, out, sems, copies):
+    part = size_x // 4
+    if (x + 1) % part == 0:
+        some = pl.ds(x + 1 - part, part)
+        copies.append(pltpu.make_async_copy(buffer.at[:, some], out.at[:, some], sems.at[x // part]))
+        copies[-1].start()
+
+
+def early_kernel(coef, q_now, q_prev, jac, base, weights, planes, buffer, sems, *, size):
     nvars, size_x, _, _ = size
     mixing_weights(coef, weights.at[0], weights.at[1], size)
-    fill_planes(q_now, x_low, x_high, y_low, y_high, planes, sides, size)
+    fill_planes(q_now, None, planes, None, size)
+    copies = []
     for x in range(size_x):
-        flux = flux_at(x, weights, planes, sides, size)
+        flux = flux_at(x, weights, planes, None, size)
         scale = step_tau * jac[x]
         for v in range(nvars):
             centre = q_now[v, x]
             physical = (q_prev[v, x] - centre) / (2.0 * step_phys)
-            base[v, x] = centre - scale * (flux[v] + physical)
+            buffer[v, x] = centre - scale * (flux[v] + physical)
+        sent_out(x, size_x, buffer, base, sems, copies)
+    for copy in copies:
+        copy.wait()
+
+
+def crossing(coef, direction, low, high, nvars):
+    parts = []
+    for side, face in enumerate((low, high)):
+        mixed = []
+        for a in range(nvars):
+            total = None
+            for b in range(nvars):
+                term = coef[((direction * 2 + side) * nvars + a) * nvars + b] * face[b]
+                total = term if total is None else total + term
+            mixed.append(total if side else -total)
+        parts.append(mixed)
+    return parts
 
 
 def land(rows, hot_xy, hot_z, store, nvars):
@@ -209,10 +244,12 @@
             store(c, landed[at : at + columns] + landed[at + columns : at + 2 * columns])
 
 
-def first_kernel(got, base, q_now, jac, state, hits, face_xl, face_xh, face_yl, face_yh, later, hot_xy, hot_z, rows, grid, *, size, devices, capacity):
+def first_kernel(coef, got, base_in, q_now, jac, x_low, x_high, y_low, y_high, state, hits, face_xl, face_xh, face_yl, face_yh, later, hot_xy, hot_z, rows, grid, base, sem, *, size, devices, capacity):
     nvars, size_x, size_y, size_z = size
     columns = size_x * size_y
     slots = devices * capacity
+    fetch = pltpu.make_async_copy(base_in, base, sem)
+    fetch.start()
     for d in range(devices):
         piece = got[d]
         lanes = slice(d * capacity, (d + 1) * capacity)
@@ -230,12 +267,23 @@
 
     hits[...] = dot(hot_xy[...], hot_z[...], ((1,), (0,)))
     land(rows, hot_xy, hot_z, keep, nvars)
+    from_x = crossing(coef, 0, x_low, x_high, nvars)
+    from_y = crossing(coef, 1, y_low, y_high, nvars)
+    row_at = iota((size_y, size_z), 0)
+    fetch.wait()
     for x in range(size_x):
         at = slice(x * size_y, (x + 1) * size_y)
         landed = hits[at, :]
-        scale = (step_tau * penalty) * jac[x]
-        for v in range(nvars):
-            new = base[v, x] - scale * (landed * q_now[v, x] - grid[v, at, :])
+        scale = step_tau * jac[x]
+        for v in range(nvars):
+            change = penalty * (landed * q_now[v, x] - grid[v, at, :])
+            change = change + jnp.where(row_at == 0, from_y[0][v][x : x + 1], 0.0)
+            change = change + jnp.where(row_at == size_y - 1, from_y[1][v][x : x + 1], 0.0)
+            if x == 0:
+                change = change + from_x[0][v]
+            if x == size_x - 1:
+                change = change + from_x[1][v]
+            new = base[v, x] - scale * change
             state[v, x] = new
             face_yl[v, x : x + 1, :] = new[0:1]
             face_yh[v, x : x + 1, :] = new[size_y - 1 : size_y]
@@ -254,8 +302,7 @@
 
 def second_kernel(state, weights, q_now, q_prev, jac, target, hits, x_low, x_high, y_low, y_high, out, planes, sides, buffer, sems, *, size):
     nvars, size_x, size_y, _ = size
-    fill_planes(state, x_low, x_high, y_low, y_high, planes, sides, size)
-    part = size_x // 4
+    fill_planes(state, (x_low, x_high, y_low, y_high), planes, sides, size)
     copies = []
     for x in range(size_x):
         at = slice(x * size_y, (x + 1) * size_y)
@@ -267,10 +314,7 @@
             physical = (3.0 * centre - 4.0 * q_now[v, x] + q_prev[v, x]) / (2.0 * step_phys)
             coupling = penalty * (landed * centre - target[v, at, :])
             buffer[v, x] = centre - scale * (flux[v] + physical + coupling)
-        if (x + 1) % part == 0:
-            some = pl.ds(x + 1 - part, part)
-            copies.append(pltpu.make_async_copy(buffer.at[:, some], out.at[:, some], sems.at[x // part]))
-            copies[-1].start()
+        sent_out(x, size_x, buffer, out, sems, copies)
     for copy in copies:
         copy.wait()
 
@@ -325,6 +369,7 @@
         y_halo = exchanged(low_y, high_y, "gy")
         return *edges(x_halo, "gx"), *edges(y_halo, "gy")
 
+    coef = flux_split.reshape(-1)
     around = halos(q_now[:, 0], q_now[:, size_x - 1], q_now[:, :, 0], q_now[:, :, size_y - 1])
     sent = pl.pallas_call(
         functools.partial(donor_kernel, size=size, devices=devices, capacity=capacity),
@@ -333,8 +378,8 @@
         out_specs=vmem,
         scratch_shapes=[
             pltpu.VMEM((2, nvars, columns, size_z), f32),
-            pltpu.VMEM((2 * nvars * columns, 3 * size_z), bf16),
-            pltpu.VMEM((3 * size_z, rows), bf16),
+            pltpu.VMEM((2, 2 * nvars * columns, size_z), bf16),
+            pltpu.VMEM((2, size_z, rows), bf16),
             pltpu.VMEM((columns, rows), f32),
             pltpu.VMEM((rows, 8), f32),
             pltpu.VMEM((CHANNELS, rows), f32),
@@ -358,13 +403,13 @@
     got = lax.all_to_all(sent, AXES, split_axis=0, concat_axis=0, tiled=True)
     base, weights = pl.pallas_call(
         functools.partial(early_kernel, size=size),
-        out_shape=[shape(size, f32), shape(weights_shape, bf16)],
-        in_specs=[smem] + [vmem] * 7,
-        out_specs=[vmem] * 2,
-        scratch_shapes=[planes, sides],
+        out_shape=[pltpu.HBM(size, f32), shape(weights_shape, bf16)],
+        in_specs=[smem] + [vmem] * 3,
+        out_specs=[hbm, vmem],
+        scratch_shapes=[planes, pltpu.VMEM(size, f32), pltpu.SemaphoreType.DMA((4,))],
         compiler_params=params(20 * MIB),
         name="early",
-    )(flux_split.reshape(-1), q_now, q_prev, jacobian, *around)
+    )(coef, q_now, q_prev, jacobian)
     state, hits, *faces, later, hot_xy, hot_z = pl.pallas_call(
         functools.partial(first_kernel, size=size, devices=devices, capacity=capacity),
         out_shape=[
@@ -378,12 +423,17 @@
             shape((columns, slots), bf16),
             shape((slots, size_z), bf16),
         ],
-        in_specs=[vmem] * 4,
+        in_specs=[smem, vmem, hbm] + [vmem] * 6,
         out_specs=[vmem] * 9,
-        scratch_shapes=[pltpu.VMEM((CHANNELS, slots), f32), pltpu.VMEM((nvars, columns, size_z), f32)],
+        scratch_shapes=[
+            pltpu.VMEM((CHANNELS, slots), f32),
+            pltpu.VMEM((nvars, columns, size_z), f32),
+            pltpu.VMEM(size, f32),
+            pltpu.SemaphoreType.DMA,
+        ],
         compiler_params=params(20 * MIB),
         name="first",
-    )(got, base, q_now, jacobian)
+    )(coef, got, pltpu.with_memory_space_constraint(base, pltpu.HBM), q_now, jacobian, *around)
     around = halos(*faces)
     target = pl.pallas_call(
         late_kernel,

time: 50.1 us -> 48 us (0.958)
  waiting for transfers between devices: 5.08 us -> 1.74 us
  Pallas kernels: 19.5 us -> 22 us
  local copies, waits for them, and re-layouts: 2.61 us -> 0.25 us
  starting transfers between devices: 19.6 us -> 20.5 us
    ppermute x4, waiting for transfers between devices: 5.06 us -> 1.73 us  [exchanged(): lax.ppermute(jnp.where(even, low_face, high_face), axis, swap_pairs(axis,...]
    unnamed x13, local copies, waits for them, and re-layouts: 2.39 us -> 0.03 us
    pallas_call x1, Pallas kernels: 3.7 us -> 5.55 us  [body(): pl.pallas_call(functools.partial(first_kernel, size=size, devices=devices...]
    ppermute x4, starting transfers between devices: 2.07 us -> 2.94 us  [exchanged(): lax.ppermute(jnp.where(even, high_face, low_face), axis, swap_pairs(axis,...]
    pallas_call x1, Pallas kernels: 2.57 us -> 3.28 us  [body(): pl.pallas_call(functools.partial(early_kernel, size=size), out_shape=[plt...]
  transfers between devices with their start and end apart: 9 -> 9, of which waited for: 2 -> 2; matrix products, arithmetic and copies ran while one was open for 4% -> 4% of each run, Pallas kernels for 11% -> 13%
where the time goes in v3:
time: 48 us; the launch traced here: 47.4 us
  Pallas kernels  22 us (46%)
  starting transfers between devices  20.5 us (43%)
  waiting for transfers between devices  1.74 us (4%)
  other arithmetic  1.72 us (4%)
  between operations  1.15 us (2%)
    ppermute x4, starting transfers between devices, exchanged(): lax.ppermute(jnp.where(even, low_face, high_face), axis, swap_pairs(axis,...  11.3 us
    pallas_call x1, Pallas kernels, body(): pl.pallas_call(functools.partial(donor_kernel, size=size, devices=devices...  7.63 us
    all_to_all x1, starting transfers between devices, body(): got = lax.all_to_all(sent, AXES, split_axis=0, concat_axis=0, tiled=True)  6.33 us
    pallas_call x1, Pallas kernels, body(): pl.pallas_call(functools.partial(first_kernel, size=size, devices=devices...  5.55 us
    pallas_call x1, Pallas kernels, body(): pl.pallas_call(functools.partial(early_kernel, size=size), out_shape=[plt...  3.28 us
    ppermute x4, starting transfers between devices, exchanged(): lax.ppermute(jnp.where(even, high_face, low_face), axis, swap_pairs(axis,...  2.94 us
    pallas_call x1, Pallas kernels, body(): pl.pallas_call(late_kernel, out_shape=shape(flat, f32), in_specs=[vmem] *...  2.86 us
    pallas_call x1, Pallas kernels, body(): pl.pallas_call(functools.partial(second_kernel, size=size), out_shape=sha...  2.69 us
  transfers between devices with their start and end apart: 9, of which 2 were waited for; matrix products, arithmetic and copies ran while one was open for 4% of the time, Pallas kernels for 13%

profile of v3, /device:TPU:9, one launch (start us, length us, event | category | flops | bytes accessed | tf_op | source)
XLA Modules:
  0.0 47.4 jit_solution(6721620610994169258)
XLA Ops:
  0.7 0.0 copy-start
  0.7 0.0 copy-start.5
  0.7 0.0 copy-start.2
  0.7 7.6 %donor.1 = f32[32,8,128]{2,1,0:T(8,128)} custom-call(s32[1]{0:T(128)S(6)} %copy.27.count, f32[5,256,256]{2,1,0:T(8,128)} %bitcast.24, f32[5,256,256]{2,1,0:T(8,128)} %bitcast.23, s32[1,1024]{1,0:T(1,128)} %bitcast.25, f32[3,1024]{1,0:T(4,128)} %frac_in.1, s32[1,1024]{1,0:T(1,128)} %bitcast.26, s32[1,1024]{1,0:T(1,128)} %bitcast.27), custom_call_target="tpu_custom_call" | custom-call | tf_op jit(solution)/shard_map/donor/pallas_call | solution.py:374
  8.3 0.0 copy-start.1
  8.3 6.3 %all-to-all-start = ((f32[32,8,128]{2,1,0:T(8,128)}), f32[32,8,128]{2,1,0:T(8,128)S(1)}, u32[]{:S(2)}, u32[]{:S(2)}) async-start(f32[32,8,128]{2,1,0:T(8,128)} %donor.1), calls=%async_computation | async-start | bytes 262144 | tf_op jit(solution)/shard_map/all_to_all | solution.py:403
  14.7 0.0 copy-done
  14.7 0.5 collective-permute-start.1
  15.2 3.1 %collective-permute-start = (f32[5,16,256]{2,1,0:T(8,128)S(1)}, f32[5,16,256]{2,1,0:T(8,128)S(1)}, u32[]{:S(2)}, u32[]{:S(2)}) collective-permute-start(f32[5,16,256]{2,1,0:T(8,128)S(1)} %get-tuple-element.30), channel_id=1, source_target_pairs={{8,16},{16,8},{9,17},{17,9},{10,18},{18,10},{11,19},{19,11},{12,20... | collective-permute-start | bytes 245768 | tf_op jit(solution)/shard_map/ppermute | solution.py:334
  18.3 0.1 fusion.2
  18.4 0.7 %select_bitcast_fusion = (f32[5,16,256]{2,1,0:T(8,128)}, f32[5,16,256]{2,1,0:T(8,128)}) fusion(f32[5,16,1,256]{3,2,1,0:T(1,128)S(1)} %get-tuple-element.28, f32[5,16,1,256]{3,2,1,0:T(1,128)S(1)} %get-tuple-element.27, pred[]{:T(512)S(6)} %eq.33), kind=kLoop, calls=%fused_computation.10 | loop fusion | flops 40960 | bytes 327681 | tf_op jit(solution)/shard_map/jit(_where)/select_n | solution.py:333
  19.1 1.2 %collective-permute-start.3 = (f32[5,16,256]{2,1,0:T(8,128)}, f32[5,16,256]{2,1,0:T(8,128)}, u32[]{:S(2)}, u32[]{:S(2)}) collective-permute-start(f32[5,16,256]{2,1,0:T(8,128)} %get-tuple-element.41), channel_id=1, source_target_pairs={{0,1},{1,0},{2,3},{3,2},{4,5},{5,4},{6,7},{7,6},{8,9},{9,8},{10,11... | collective-permute-start | bytes 245768 | tf_op jit(solution)/shard_map/ppermute | solution.py:333
  20.3 2.2 %collective-permute-start.2 = (f32[5,16,256]{2,1,0:T(8,128)}, f32[5,16,256]{2,1,0:T(8,128)}, u32[]{:S(2)}, u32[]{:S(2)}) collective-permute-start(f32[5,16,256]{2,1,0:T(8,128)} %get-tuple-element.42), channel_id=1, source_target_pairs={{1,2},{2,1},{3,4},{4,3},{5,6},{6,5},{9,10},{10,9},{11,12},{12,11},... | collective-permute-start | bytes 245768 | tf_op jit(solution)/shard_map/ppermute | solution.py:334
  22.5 0.0 copy-done.5
  22.5 0.1 reshape.26.coef
  22.6 0.0 copy-done.2
  22.6 0.0 copy-done.1
  22.6 3.3 %early.1 = (f32[5,16,16,256]{3,2,1,0:T(8,128)}, bf16[2,240,256]{2,1,0:T(8,128)(2,1)S(1)}) custom-call(f32[150]{0:T(256)S(1)} %reshape.26.coef, f32[5,16,16,256]{3,2,1,0:T(8,128)S(1)} %copy-done, f32[5,16,16,256]{3,2,1,0:T(8,128)S(1)} %copy-done.1, f32[16,16,256]{2,1,0:T(8,128)S(1)} %copy-done.2), custom_call_target="tpu_custom_call" | custom-call | tf_op jit(solution)/shard_map/early/pallas_call | solution.py:404
  25.9 0.0 copy-start.3
  25.9 0.0 collective-permute-done.1
  25.9 0.0 collective-permute-done
  26.0 0.0 collective-permute-done.3
  26.0 0.7 %collective-permute-done.2 = f32[5,16,256]{2,1,0:T(8,128)} collective-permute-done((f32[5,16,256]{2,1,0:T(8,128)}, f32[5,16,256]{2,1,0:T(8,128)}, u32[]{:S(2)}, u32[]{:S(2)}) %collective-permute-start.2) | collective-permute-done | bytes 81952 | tf_op jit(solution)/shard_map/ppermute | solution.py:334
  26.7 0.0 copy-done.3
  26.7 0.9 %select_select_fusion.4 = (f32[5,16,256]{2,1,0:T(8,128)S(1)}, f32[5,16,256]{2,1,0:T(8,128)S(1)}) fusion(f32[5,16,256]{2,1,0:T(8,128)} %collective-permute-done.3, f32[5,16,256]{2,1,0:T(8,128)} %collective-permute-done.2, pred[]{:T(512)S(6)} %eq.34, pred[]{:T(512)S(6)} %eq.33, pred[]{:T(512)S(6)} %eq.32), kind=kLoop, calls=%fused_computation.8 | loop fusion | flops 81920 | bytes 327683 | tf_op jit(solution)/shard_map/jit(_where)/select_n | solution.py:344
  27.6 0.0 all-to-all-done.got
  27.6 5.6 %first.1 = (f32[5,16,16,256]{3,2,1,0:T(8,128)S(1)}, f32[256,256]{1,0:T(8,128)S(1)}, f32[5,16,256]{2,1,0:T(8,128)S(1)}, f32[5,16,256]{2,1,0:T(8,128)S(1)}, f32[5,...) custom-call(f32[150]{0:T(256)S(1)} %reshape.26.coef, ...), custom_call_target="tpu_custom_call" | custom-call | tf_op jit(solution)/shard_map/first/pallas_call | solution.py:413
  33.2 0.1 collective-permute-start.5
  33.3 3.9 %collective-permute-start.4 = (f32[5,16,256]{2,1,0:T(8,128)S(1)}, f32[5,16,256]{2,1,0:T(8,128)S(1)}, u32[]{:S(2)}, u32[]{:S(2)}) collective-permute-start(f32[5,16,256]{2,1,0:T(8,128)S(1)} %get-tuple-element.38), channel_id=1, source_target_pairs={{8,16},{16,8},{9,17},{17,9},{10,18},{18,10},{11,19},{19,11},{12,20... | collective-permute-start | bytes 245768 | tf_op jit(solution)/shard_map/ppermute | solution.py:334
  37.2 1.2 %collective-permute-start.7 = (f32[5,16,256]{2,1,0:T(8,128)S(1)}, f32[5,16,256]{2,1,0:T(8,128)S(1)}, u32[]{:S(2)}, u32[]{:S(2)}) collective-permute-start(f32[5,16,256]{2,1,0:T(8,128)S(1)} %get-tuple-element.33), channel_id=1, source_target_pairs={{0,1},{1,0},{2,3},{3,2},{4,5},{5,4},{6,7},{7,6},{8,9},{9,8},{10,11... | collective-permute-start | bytes 245768 | tf_op jit(solution)/shard_map/ppermute | solution.py:333
  38.4 2.1 %collective-permute-start.6 = (f32[5,16,256]{2,1,0:T(8,128)S(1)}, f32[5,16,256]{2,1,0:T(8,128)S(1)}, u32[]{:S(2)}, u32[]{:S(2)}) collective-permute-start(f32[5,16,256]{2,1,0:T(8,128)S(1)} %get-tuple-element.34), channel_id=1, source_target_pairs={{1,2},{2,1},{3,4},{4,3},{5,6},{6,5},{9,10},{10,9},{11,12},{12,11},... | collective-permute-start | bytes 245768 | tf_op jit(solution)/shard_map/ppermute | solution.py:334
  40.5 0.0 copy-start.4
  40.5 2.9 %late.1.target = f32[5,256,256]{2,1,0:T(8,128)S(1)} custom-call(f32[5,2048]{1,0:T(8,128)S(1)} %get-tuple-element.19.rows, bf16[256,2048]{1,0:T(8,128)(2,1)S(1)} %get-tuple-element.20.hot_xy, bf16[2048,256]{1,0:T(8,128)(2,1)S(1)} %get-tuple-element.21.hot_z), custom_call_target="tpu_custom_call" | custom-call | tf_op jit(solution)/shard_map/late/pallas_call | solution.py:438
  43.4 0.0 collective-permute-done.5
  43.4 0.0 collective-permute-done.4
  43.5 0.0 collective-permute-done.7
  43.5 1.0 %collective-permute-done.6 = f32[5,16,256]{2,1,0:T(8,128)S(1)} collective-permute-done((f32[5,16,256]{2,1,0:T(8,128)S(1)}, f32[5,16,256]{2,1,0:T(8,128)S(1)}, u32[]{:S(2)}, u32[]{:S(2)}) %collective-permute-start.6) | collective-permute-done | bytes 81952 | tf_op jit(solution)/shard_map/ppermute | solution.py:334
  44.5 0.0 copy-done.4
  44.5 2.7 %second.1 = f32[5,16,16,256]{3,2,1,0:T(8,128)} custom-call(f32[5,16,16,256]{3,2,1,0:T(8,128)S(1)} %get-tuple-element.17.state, bf16[2,240,256]{2,1,0:T(8,128)(2,1)S(1)} %copy-done.4, f32[5,16,16,256]{3,2,1,0:T(8,128)S(1)} %copy-done, f32[5,16,16,256]{3,2,1,0:T(8,128)S(1)} %copy-done.1, f32[16,16,256]{2,1,0:T(8,128)S(1)} %copy-done.2, ...), custom_call_target="tpu_custom_call" | custom-call | tf_op jit(solution)/shard_map/second/pallas_call | solution.py:446
  (7 shorter events, 0.1 us)
Async XLA Ops:
  0.7 14.0 %copy-start = (f32[5,16,16,256]{3,2,1,0:T(8,128)S(1)}, f32[5,16,16,256]{3,2,1,0:T(8,128)}, u32[]{:S(2)}) copy-start(f32[5,16,16,256]{3,2,1,0:T(8,128)} %q_now.5) | copy-start | bytes 3932164
  0.7 21.8 %copy-start.5 = (f32[3,2,5,5]{3,1,2,0:T(2,128)S(1)}, f32[3,2,5,5]{3,1,2,0:T(2,128)}, u32[]{:S(2)}) copy-start(f32[3,2,5,5]{3,1,2,0:T(2,128)} %param.12) | copy-start | bytes 1804
  0.7 21.9 %copy-start.2 = (f32[16,16,256]{2,1,0:T(8,128)S(1)}, f32[16,16,256]{2,1,0:T(8,128)}, u32[]{:S(2)}) copy-start(f32[16,16,256]{2,1,0:T(8,128)} %jac.5) | copy-start | bytes 786436
  8.3 14.3 %copy-start.1 = (f32[5,16,16,256]{3,2,1,0:T(8,128)S(1)}, f32[5,16,16,256]{3,2,1,0:T(8,128)}, u32[]{:S(2)}) copy-start(f32[5,16,16,256]{3,2,1,0:T(8,128)} %q_prev.3) | copy-start | bytes 3932164
  8.3 19.3 %all-to-all-start = ((f32[32,8,128]{2,1,0:T(8,128)}), f32[32,8,128]{2,1,0:T(8,128)S(1)}, u32[]{:S(2)}, u32[]{:S(2)}) async-start(f32[32,8,128]{2,1,0:T(8,128)} %donor.1), calls=%async_computation | async-start | bytes 262144 | tf_op jit(solution)/shard_map/all_to_all | solution.py:403
  14.7 11.2 %collective-permute-start.1 = (f32[5,16,256]{2,1,0:T(8,128)S(1)}, f32[5,16,256]{2,1,0:T(8,128)S(1)}, u32[]{:S(2)}, u32[]{:S(2)}) collective-permute-start(f32[5,16,256]{2,1,0:T(8,128)S(1)} %get-tuple-element.29), channel_id=1, source_target_pairs={{0,8},{8,0},{16,24},{24,16},{1,9},{9,1},{17,25},{25,17},{2,10},{10... | collective-permute-start | bytes 245768 | tf_op jit(solution)/shard_map/ppermute | solution.py:333
  15.2 10.8 %collective-permute-start = (f32[5,16,256]{2,1,0:T(8,128)S(1)}, f32[5,16,256]{2,1,0:T(8,128)S(1)}, u32[]{:S(2)}, u32[]{:S(2)}) collective-permute-start(f32[5,16,256]{2,1,0:T(8,128)S(1)} %get-tuple-element.30), channel_id=1, source_target_pairs={{8,16},{16,8},{9,17},{17,9},{10,18},{18,10},{11,19},{19,11},{12,20... | collective-permute-start | bytes 245768 | tf_op jit(solution)/shard_map/ppermute | solution.py:334
  19.1 6.9 %collective-permute-start.3 = (f32[5,16,256]{2,1,0:T(8,128)}, f32[5,16,256]{2,1,0:T(8,128)}, u32[]{:S(2)}, u32[]{:S(2)}) collective-permute-start(f32[5,16,256]{2,1,0:T(8,128)} %get-tuple-element.41), channel_id=1, source_target_pairs={{0,1},{1,0},{2,3},{3,2},{4,5},{5,4},{6,7},{7,6},{8,9},{9,8},{10,11... | collective-permute-start | bytes 245768 | tf_op jit(solution)/shard_map/ppermute | solution.py:333
  20.3 6.4 %collective-permute-start.2 = (f32[5,16,256]{2,1,0:T(8,128)}, f32[5,16,256]{2,1,0:T(8,128)}, u32[]{:S(2)}, u32[]{:S(2)}) collective-permute-start(f32[5,16,256]{2,1,0:T(8,128)} %get-tuple-element.42), channel_id=1, source_target_pairs={{1,2},{2,1},{3,4},{4,3},{5,6},{6,5},{9,10},{10,9},{11,12},{12,11},... | collective-permute-start | bytes 245768 | tf_op jit(solution)/shard_map/ppermute | solution.py:334
  25.9 0.8 %copy-start.3 = (bf16[2,240,256]{2,1,0:T(8,128)(2,1)}, bf16[2,240,256]{2,1,0:T(8,128)(2,1)S(1)}, u32[]{:S(2)}) copy-start(bf16[2,240,256]{2,1,0:T(8,128)(2,1)S(1)} %get-tuple-element.18.weights) | copy-start | bytes 737284
  33.2 10.2 %collective-permute-start.5 = (f32[5,16,256]{2,1,0:T(8,128)S(1)}, f32[5,16,256]{2,1,0:T(8,128)S(1)}, u32[]{:S(2)}, u32[]{:S(2)}) collective-permute-start(f32[5,16,256]{2,1,0:T(8,128)S(1)} %get-tuple-element.37), channel_id=1, source_target_pairs={{0,8},{8,0},{16,24},{24,16},{1,9},{9,1},{17,25},{25,17},{2,10},{10... | collective-permute-start | bytes 245768 | tf_op jit(solution)/shard_map/ppermute | solution.py:333
  33.3 10.2 %collective-permute-start.4 = (f32[5,16,256]{2,1,0:T(8,128)S(1)}, f32[5,16,256]{2,1,0:T(8,128)S(1)}, u32[]{:S(2)}, u32[]{:S(2)}) collective-permute-start(f32[5,16,256]{2,1,0:T(8,128)S(1)} %get-tuple-element.38), channel_id=1, source_target_pairs={{8,16},{16,8},{9,17},{17,9},{10,18},{18,10},{11,19},{19,11},{12,20... | collective-permute-start | bytes 245768 | tf_op jit(solution)/shard_map/ppermute | solution.py:334
  37.2 6.3 %collective-permute-start.7 = (f32[5,16,256]{2,1,0:T(8,128)S(1)}, f32[5,16,256]{2,1,0:T(8,128)S(1)}, u32[]{:S(2)}, u32[]{:S(2)}) collective-permute-start(f32[5,16,256]{2,1,0:T(8,128)S(1)} %get-tuple-element.33), channel_id=1, source_target_pairs={{0,1},{1,0},{2,3},{3,2},{4,5},{5,4},{6,7},{7,6},{8,9},{9,8},{10,11... | collective-permute-start | bytes 245768 | tf_op jit(solution)/shard_map/ppermute | solution.py:333
  38.4 6.1 %collective-permute-start.6 = (f32[5,16,256]{2,1,0:T(8,128)S(1)}, f32[5,16,256]{2,1,0:T(8,128)S(1)}, u32[]{:S(2)}, u32[]{:S(2)}) collective-permute-start(f32[5,16,256]{2,1,0:T(8,128)S(1)} %get-tuple-element.34), channel_id=1, source_target_pairs={{1,2},{2,1},{3,4},{4,3},{5,6},{6,5},{9,10},{10,9},{11,12},{12,11},... | collective-permute-start | bytes 245768 | tf_op jit(solution)/shard_map/ppermute | solution.py:334
  40.5 4.0 %copy-start.4 = (bf16[2,240,256]{2,1,0:T(8,128)(2,1)S(1)}, bf16[2,240,256]{2,1,0:T(8,128)(2,1)}, u32[]{:S(2)}) copy-start(bf16[2,240,256]{2,1,0:T(8,128)(2,1)} %copy-done.3) | copy-start | bytes 737284

commit v4 on v3

--- a/solution.py
+++ b/solution.py
@@ -16,6 +16,7 @@
 LANES = 256
 CHANNELS = 16
 MIB = 1 << 20
+DONOR_LIMIT = 44 * MIB
 
 
 def iota(shape, dim):
@@ -48,15 +49,15 @@
     return jnp.concatenate(pieces, axis=1)
 
 
-def donor_kernel(count, q_prev, q_now, base_in, frac_in, dest_in, cell_in, out, planes, lhs, spread, corner, place, values, base, frac, dest, cell, sems, *, size, devices, capacity):
+def donor_kernel(count, parity, q_prev, q_now, base_in, frac_in, dest_in, cell_in, jac_in, out, y_inner, y_outer, planes, jac, lhs, spread, corner, place, values, base, frac, dest, cell, sems, *, size, devices, capacity):
     nvars, size_x, size_y, size_z = size
     columns = size_x * size_y
     rows = base.shape[1]
-    small = [pltpu.make_async_copy(a, b, sems.at[2 + k]) for k, (a, b) in enumerate(((base_in, base), (frac_in, frac), (dest_in, dest), (cell_in, cell)))]
+    small = [pltpu.make_async_copy(a, b, sems.at[2 + k]) for k, (a, b) in enumerate(((base_in, base), (frac_in, frac), (dest_in, dest), (cell_in, cell), (jac_in, jac)))]
     copies = [pltpu.make_async_copy(ref, planes.at[k], sems.at[k]) for k, ref in enumerate((q_prev, q_now))]
     for copy in small + copies:
         copy.start()
-    for copy in small:
+    for copy in small[0:4]:
         copy.wait()
     start = base[...].astype(jnp.float32)
     in_y = jnp.floor((start + 0.5) * (1.0 / (size_z - 1)))
@@ -88,6 +89,16 @@
     values[2 * nvars + 1 : 2 * nvars + 2, :] = landing - land_xy * size_z
     for k in range(2):
         copies[k].wait()
+        if k == 1:
+            small[4].wait()
+            even = parity[1] == 0
+            for v in range(nvars + 1):
+                for x in range(size_x):
+                    line = planes.at[1, v] if v < nvars else jac
+                    low = line[x * size_y : x * size_y + 1, :]
+                    high = line[(x + 1) * size_y - 1 : (x + 1) * size_y, :]
+                    y_inner[v, x : x + 1, :] = jnp.where(even, high, low)
+                    y_outer[v, x : x + 1, :] = jnp.where(even, low, high)
         for v in range(nvars):
             at = pl.ds((k * nvars + v) * columns, columns)
             high, low = halves(planes[k, v])
@@ -152,14 +163,14 @@
             high[rows, :], low[rows, :] = halves(part)
 
 
-def fill_planes(state, around, planes, sides, size):
+def fill_planes(at_plane, around, planes, sides, size):
     nvars, size_x, size_y, size_z = size
     block = nvars * size_y
     for x in range(size_x + 2):
         for v in range(nvars):
             rows = slice(x * block + v * size_y, x * block + (v + 1) * size_y)
             if 0 < x <= size_x:
-                planes[0, rows, :], planes[1, rows, :] = halves(state[v, x - 1])
+                planes[0, rows, :], planes[1, rows, :] = halves(at_plane(v, x - 1))
             elif around is None:
                 planes[0, rows, :] = planes[1, rows, :] = jnp.zeros((size_y, size_z), jnp.bfloat16)
             else:
@@ -202,7 +213,7 @@
 def early_kernel(coef, q_now, q_prev, jac, base, weights, planes, buffer, sems, *, size):
     nvars, size_x, _, _ = size
     mixing_weights(coef, weights.at[0], weights.at[1], size)
-    fill_planes(q_now, None, planes, None, size)
+    fill_planes(lambda v, x: q_now[v, x], None, planes, None, size)
     copies = []
     for x in range(size_x):
         flux = flux_at(x, weights, planes, None, size)
@@ -216,18 +227,16 @@
         copy.wait()
 
 
-def crossing(coef, direction, low, high, nvars):
-    parts = []
-    for side, face in enumerate((low, high)):
-        mixed = []
-        for a in range(nvars):
-            total = None
-            for b in range(nvars):
-                term = coef[((direction * 2 + side) * nvars + a) * nvars + b] * face[b]
-                total = term if total is None else total + term
-            mixed.append(total if side else -total)
-        parts.append(mixed)
-    return parts
+def mixed_by(coef, direction, side, lines):
+    nvars = len(lines)
+    out = []
+    for a in range(nvars):
+        total = None
+        for b in range(nvars):
+            term = coef[((direction * 2 + side) * nvars + a) * nvars + b] * lines[b]
+            total = term if total is None else total + term
+        out.append(total)
+    return out
 
 
 def land(rows, hot_xy, hot_z, store, nvars):
@@ -244,7 +253,7 @@
             store(c, landed[at : at + columns] + landed[at + columns : at + 2 * columns])
 
 
-def first_kernel(coef, got, base_in, q_now, jac, x_low, x_high, y_low, y_high, state, hits, face_xl, face_xh, face_yl, face_yh, later, hot_xy, hot_z, rows, grid, base, sem, *, size, devices, capacity):
+def first_kernel(coef, parity, got, base_in, q_now, jac, line_inner, line_outer, state, hits, x_inner, x_outer, y_inner, y_outer, later, hot_xy, hot_z, rows, grid, base, sem, *, size, devices, capacity):
     nvars, size_x, size_y, size_z = size
     columns = size_x * size_y
     slots = devices * capacity
@@ -267,30 +276,40 @@
 
     hits[...] = dot(hot_xy[...], hot_z[...], ((1,), (0,)))
     land(rows, hot_xy, hot_z, keep, nvars)
-    from_x = crossing(coef, 0, x_low, x_high, nvars)
-    from_y = crossing(coef, 1, y_low, y_high, nvars)
+    even_x, even_y = parity[0] == 0, parity[1] == 0
+    y_low = [jnp.where(even_y, line_outer[v], line_inner[v]) for v in range(nvars)]
+    y_high = [jnp.where(even_y, line_inner[v], line_outer[v]) for v in range(nvars)]
+    from_low, from_high = mixed_by(coef, 1, 0, y_low), mixed_by(coef, 1, 1, y_high)
     row_at = iota((size_y, size_z), 0)
     fetch.wait()
+    faces = {}
     for x in range(size_x):
         at = slice(x * size_y, (x + 1) * size_y)
         landed = hits[at, :]
         scale = step_tau * jac[x]
         for v in range(nvars):
             change = penalty * (landed * q_now[v, x] - grid[v, at, :])
-            change = change + jnp.where(row_at == 0, from_y[0][v][x : x + 1], 0.0)
-            change = change + jnp.where(row_at == size_y - 1, from_y[1][v][x : x + 1], 0.0)
-            if x == 0:
-                change = change + from_x[0][v]
-            if x == size_x - 1:
-                change = change + from_x[1][v]
+            change = change - jnp.where(row_at == 0, from_low[v][x : x + 1], 0.0)
+            change = change + jnp.where(row_at == size_y - 1, from_high[v][x : x + 1], 0.0)
             new = base[v, x] - scale * change
             state[v, x] = new
-            face_yl[v, x : x + 1, :] = new[0:1]
-            face_yh[v, x : x + 1, :] = new[size_y - 1 : size_y]
-            if x == 0:
-                face_xl[v] = new
-            if x == size_x - 1:
-                face_xh[v] = new
+            low, high = new[0:1], new[size_y - 1 : size_y]
+            y_inner[v, x : x + 1, :] = jnp.where(even_y, high, low)
+            y_outer[v, x : x + 1, :] = jnp.where(even_y, low, high)
+            if x in (0, size_x - 1):
+                faces[x, v] = new
+    ends = [y_low[v] for v in range(nvars)] + [y_high[v] for v in range(nvars)]
+    for v in range(nvars):
+        for k, pair in enumerate(((faces[0, v], faces[size_x - 1, v]), (q_now[v, 0], q_now[v, size_x - 1]))):
+            x_inner[k * nvars + v] = jnp.where(even_x, pair[1], pair[0])
+            x_outer[k * nvars + v] = jnp.where(even_x, pair[0], pair[1])
+    x_inner[2 * nvars] = jnp.where(even_x, jac[size_x - 1], jac[0])
+    x_outer[2 * nvars] = jnp.where(even_x, jac[0], jac[size_x - 1])
+    x_inner[2 * nvars + 1] = x_outer[2 * nvars + 1] = jnp.zeros((size_y, size_z), jnp.float32)
+    for k, line in enumerate(ends):
+        low, high = line[0:1], line[size_x - 1 : size_x]
+        x_inner[2 * nvars + 1, k : k + 1, :] = jnp.where(even_x, high, low)
+        x_outer[2 * nvars + 1, k : k + 1, :] = jnp.where(even_x, low, high)
 
 
 def late_kernel(rows, hot_xy, hot_z, target):
@@ -300,9 +319,37 @@
     land(rows, hot_xy, hot_z, keep, rows.shape[0])
 
 
-def second_kernel(state, weights, q_now, q_prev, jac, target, hits, x_low, x_high, y_low, y_high, out, planes, sides, buffer, sems, *, size):
-    nvars, size_x, size_y, _ = size
-    fill_planes(state, (x_low, x_high, y_low, y_high), planes, sides, size)
+def second_kernel(coef, parity, state, weights, q_now, q_prev, jac, target, hits, x_inner, x_outer, y_inner, y_outer, line_inner, line_outer, out, planes, sides, edge, buffer, sems, *, size):
+    nvars, size_x, size_y, size_z = size
+    last = size_x - 1
+    even_x, even_y = parity[0] == 0, parity[1] == 0
+    x_low = [jnp.where(even_x, x_outer[k], x_inner[k]) for k in range(2 * nvars + 2)]
+    x_high = [jnp.where(even_x, x_inner[k], x_outer[k]) for k in range(2 * nvars + 2)]
+    own_low = mixed_by(coef, 0, 0, x_low[nvars : 2 * nvars])
+    own_high = mixed_by(coef, 0, 1, x_high[nvars : 2 * nvars])
+    ring_low = mixed_by(coef, 0, 1, [q_now[v, 0] for v in range(nvars)])
+    ring_high = mixed_by(coef, 0, 0, [q_now[v, last] for v in range(nvars)])
+    around = [[], [], [], []]
+    for v in range(nvars):
+        edge[0, v] = state[v, 0] + step_tau * jac[0] * own_low[v]
+        edge[1, v] = state[v, last] - step_tau * jac[last] * own_high[v]
+        around[0].append(x_low[v] - step_tau * x_low[2 * nvars] * ring_low[v])
+        around[1].append(x_high[v] + step_tau * x_high[2 * nvars] * ring_high[v])
+    row_at = iota((size_x, size_z), 0)
+    for side in range(2):
+        pick = (y_outer, y_inner, line_outer, line_inner) if side == 0 else (y_inner, y_outer, line_inner, line_outer)
+        scale = step_tau * jnp.where(even_y, pick[2][nvars], pick[3][nvars])
+        corner = slice(side * nvars, (side + 1) * nvars)
+        low = mixed_by(coef, 0, 0, [x_low[2 * nvars + 1][k : k + 1] for k in range(corner.start, corner.stop)])
+        high = mixed_by(coef, 0, 1, [x_high[2 * nvars + 1][k : k + 1] for k in range(corner.start, corner.stop)])
+        for v in range(nvars):
+            change = jnp.where(row_at == 0, low[v], 0.0) - jnp.where(row_at == last, high[v], 0.0)
+            around[2 + side].append(jnp.where(even_y, pick[0][v], pick[1][v]) + scale * change)
+
+    def at_plane(v, x):
+        return edge[0, v] if x == 0 else edge[1, v] if x == last else state[v, x]
+
+    fill_planes(at_plane, around, planes, sides, size)
     copies = []
     for x in range(size_x):
         at = slice(x * size_y, (x + 1) * size_y)
@@ -310,7 +357,7 @@
         landed = hits[at, :]
         scale = step_tau * jac[x]
         for v in range(nvars):
-            centre = state[v, x]
+            centre = at_plane(v, x)
             physical = (3.0 * centre - 4.0 * q_now[v, x] + q_prev[v, x]) / (2.0 * step_phys)
             coupling = penalty * (landed * centre - target[v, at, :])
             buffer[v, x] = centre - scale * (flux[v] + physical + coupling)
@@ -327,21 +374,12 @@
     return pairs
 
 
-def exchanged(low_face, high_face, axis):
-    here = lax.axis_index(axis)
-    even = here % 2 == 0
-    inner = lax.ppermute(jnp.where(even, high_face, low_face), axis, swap_pairs(axis, 0))
-    outer = lax.ppermute(jnp.where(even, low_face, high_face), axis, swap_pairs(axis, 1))
-    return jnp.where(even, outer, inner), jnp.where(even, inner, outer)
+def swapped(inner, outer, axis):
+    return lax.ppermute(inner, axis, swap_pairs(axis, 0)), lax.ppermute(outer, axis, swap_pairs(axis, 1))
 
 
 def params(limit):
     return pltpu.CompilerParams(vmem_limit_bytes=limit)
-
-
-def edges(halo, axis):
-    here, last = lax.axis_index(axis), lax.axis_size(axis) - 1
-    return jnp.where(here == 0, 0.0, halo[0]), jnp.where(here == last, 0.0, halo[1])
 
 
 def body(q_now, q_prev, jacobian, flux_split, donor_base, donor_frac, fringe_dest, receptor_cell, fringe_count):
@@ -362,22 +400,23 @@
     weights_shape = (2, 3 * block, 3 * block + CHANNELS)
     planes = pltpu.VMEM((2, (size_x + 2) * block, size_z), bf16)
     sides = pltpu.VMEM((size_x, CHANNELS, size_z), f32)
-    face_x, face_y = shape((nvars, size_y, size_z), f32), shape((nvars, size_x, size_z), f32)
-
-    def halos(low_x, high_x, low_y, high_y):
-        x_halo = exchanged(low_x, high_x, "gx")
-        y_halo = exchanged(low_y, high_y, "gy")
-        return *edges(x_halo, "gx"), *edges(y_halo, "gy")
-
+    face_y = shape((nvars, size_x, size_z), f32)
+
+    line, line_x = shape((nvars + 1, size_x, size_z), f32), shape((2 * nvars + 2, size_y, size_z), f32)
     coef = flux_split.reshape(-1)
-    around = halos(q_now[:, 0], q_now[:, size_x - 1], q_now[:, :, 0], q_now[:, :, size_y - 1])
-    sent = pl.pallas_call(
+    parity = jnp.stack([lax.axis_index("gx") % 2, lax.axis_index("gy") % 2]).astype(jnp.int32)
+
+    def there(x):
+        return pltpu.with_memory_space_constraint(x, pltpu.HBM)
+
+    sent, *lines = pl.pallas_call(
         functools.partial(donor_kernel, size=size, devices=devices, capacity=capacity),
-        out_shape=shape((devices, 8, 2 * capacity), f32),
-        in_specs=[smem] + [hbm] * 6,
-        out_specs=vmem,
+        out_shape=[shape((devices, 8, 2 * capacity), f32), line, line],
+        in_specs=[smem, smem] + [hbm] * 7,
+        out_specs=[vmem] * 3,
         scratch_shapes=[
             pltpu.VMEM((2, nvars, columns, size_z), f32),
+            pltpu.VMEM((columns, size_z), f32),
             pltpu.VMEM((2, 2 * nvars * columns, size_z), bf16),
             pltpu.VMEM((2, size_z, rows), bf16),
             pltpu.VMEM((columns, rows), f32),
@@ -387,20 +426,23 @@
             pltpu.VMEM((3, rows), f32),
             pltpu.VMEM((1, rows), jnp.int32),
             pltpu.VMEM((1, rows), jnp.int32),
-            pltpu.SemaphoreType.DMA((6,)),
+            pltpu.SemaphoreType.DMA((7,)),
         ],
-        compiler_params=params(60 * 1024 * 1024),
+        compiler_params=params(DONOR_LIMIT),
         name="donor",
     )(
         fringe_count,
-        q_prev.reshape(flat),
-        q_now.reshape(flat),
-        donor_base.reshape(1, rows),
-        donor_frac,
-        fringe_dest.reshape(1, rows),
-        receptor_cell.reshape(1, rows),
+        parity,
+        there(q_prev.reshape(flat)),
+        there(q_now.reshape(flat)),
+        there(donor_base.reshape(1, rows)),
+        there(donor_frac),
+        there(fringe_dest.reshape(1, rows)),
+        there(receptor_cell.reshape(1, rows)),
+        there(jacobian.reshape(columns, size_z)),
     )
     got = lax.all_to_all(sent, AXES, split_axis=0, concat_axis=0, tiled=True)
+    lines = swapped(*lines, "gy")
     base, weights = pl.pallas_call(
         functools.partial(early_kernel, size=size),
         out_shape=[pltpu.HBM(size, f32), shape(weights_shape, bf16)],
@@ -415,15 +457,15 @@
         out_shape=[
             shape(size, f32),
             shape((columns, size_z), f32),
-            face_x,
-            face_x,
+            line_x,
+            line_x,
             face_y,
             face_y,
             shape((nvars, slots), f32),
             shape((columns, slots), bf16),
             shape((slots, size_z), bf16),
         ],
-        in_specs=[smem, vmem, hbm] + [vmem] * 6,
+        in_specs=[smem, smem, vmem, hbm] + [vmem] * 4,
         out_specs=[vmem] * 9,
         scratch_shapes=[
             pltpu.VMEM((CHANNELS, slots), f32),
@@ -433,8 +475,8 @@
         ],
         compiler_params=params(20 * MIB),
         name="first",
-    )(coef, got, pltpu.with_memory_space_constraint(base, pltpu.HBM), q_now, jacobian, *around)
-    around = halos(*faces)
+    )(coef, parity, got, there(base), q_now, jacobian, *lines)
+    around = (*swapped(*faces[0:2], "gx"), *swapped(*faces[2:4], "gy"))
     target = pl.pallas_call(
         late_kernel,
         out_shape=shape(flat, f32),
@@ -446,12 +488,12 @@
     return pl.pallas_call(
         functools.partial(second_kernel, size=size),
         out_shape=shape(size, f32),
-        in_specs=[vmem] * 11,
+        in_specs=[smem, smem] + [vmem] * 13,
         out_specs=hbm,
-        scratch_shapes=[planes, sides, pltpu.VMEM(size, f32), pltpu.SemaphoreType.DMA((4,))],
+        scratch_shapes=[planes, sides, pltpu.VMEM((2, nvars, size_y, size_z), f32), pltpu.VMEM(size, f32), pltpu.SemaphoreType.DMA((4,))],
         compiler_params=params(20 * MIB),
         name="second",
-    )(state, weights, q_now, q_prev, jacobian, target, hits, *around)
+    )(coef, parity, state, weights, q_now, q_prev, jacobian, target, hits, *around, *lines)
 
 
 def solution(mesh):

time: 48 us -> 44.8 us (0.933)
  starting transfers between devices: 20.5 us -> 17.1 us
  Pallas kernels: 22 us -> 24 us
  other arithmetic: 1.72 us -> 0.08 us
    ppermute x8 -> x6, starting transfers between devices: 14.2 us -> 10.7 us  [the longest x3 7.09 us: swapped(): lax.ppermute(outer, axis, swap_pairs(axis, 1))]
    select_n x8 -> x0, other arithmetic: 1.72 us -> none  [the longest x4 0.99 us: edges(): jnp.where(here == last, 0.0, halo[1])]
    pallas_call x1, Pallas kernels: 2.69 us -> 3.61 us  [body(): pl.pallas_call(functools.partial(second_kernel, size=size), out_shape=sha...]
    pallas_call x1, Pallas kernels: 7.63 us -> 8.5 us  [body(): pl.pallas_call(functools.partial(donor_kernel, size=size, devices=devices...]
    ppermute x8 -> x6, waiting for transfers between devices: 1.74 us -> 2.07 us  [the longest x3 2.06 us: swapped(): lax.ppermute(outer, axis, swap_pairs(axis, 1))]
  transfers between devices with their start and end apart: 9 -> 7, of which waited for: 2 -> 2; matrix products, arithmetic and copies ran while one was open for 4% -> 0% of each run, Pallas kernels for 13% -> 14%
where the time goes in v4:
time: 44.8 us; the launch traced here: 44.3 us
  Pallas kernels  24 us (54%)
  starting transfers between devices  17.1 us (38%)
  waiting for transfers between devices  2.07 us (5%)
  between operations  0.95 us (2%)
    pallas_call x1, Pallas kernels, body(): pl.pallas_call(functools.partial(donor_kernel, size=size, devices=devices...  8.5 us
    ppermute x3, starting transfers between devices, swapped(): lax.ppermute(outer, axis, swap_pairs(axis, 1))  7.09 us
    all_to_all x1, starting transfers between devices, body(): got = lax.all_to_all(sent, AXES, split_axis=0, concat_axis=0, tiled=True)  6.33 us
    pallas_call x1, Pallas kernels, body(): pl.pallas_call(functools.partial(first_kernel, size=size, devices=devices...  5.72 us
    ppermute x3, starting transfers between devices, swapped(): lax.ppermute(inner, axis, swap_pairs(axis, 0))  3.65 us
    pallas_call x1, Pallas kernels, body(): pl.pallas_call(functools.partial(second_kernel, size=size), out_shape=sha...  3.61 us
    pallas_call x1, Pallas kernels, body(): pl.pallas_call(functools.partial(early_kernel, size=size), out_shape=[plt...  3.28 us
    pallas_call x1, Pallas kernels, body(): pl.pallas_call(late_kernel, out_shape=shape(flat, f32), in_specs=[vmem] *...  2.89 us
  transfers between devices with their start and end apart: 7, of which 2 were waited for; matrix products, arithmetic and copies ran while one was open for 0% of the time, Pallas kernels for 14%

profile of v4, /device:TPU:9, one launch (start us, length us, event | category | flops | bytes accessed | tf_op | source)
XLA Modules:
  0.0 44.3 jit_solution(10800877255094244796)
XLA Ops:
  0.7 0.1 pad_add_fusion.parity
  0.7 0.0 copy-start.3
  0.7 0.0 copy-start
  0.7 0.0 copy-start.1
  0.7 0.0 copy-start.2
  0.7 8.5 %donor.1 = (f32[32,8,128]{2,1,0:T(8,128)}, f32[6,16,256]{2,1,0:T(8,128)}, f32[6,16,256]{2,1,0:T(8,128)}) custom-call(s32[1]{0:T(128)S(6)} %copy.11.count, s32[2]{0:T(128)S(1)} %pad_add_fusion.parity, f32[5,256,256]{2,1,0:T(8,128)} %bitcast.9, f32[5,256,256]{2,1,0:T(8,128)} %bitcast.8, s32[1,1024]{1,0:T(1,128)} %bitcast.11, f32[3,1024]{1,0:T(4,128)} %frac_in.1, ...), custom_call_target="tpu_custom_call" | custom-call | tf_op jit(solution)/shard_map/donor/pallas_call | solution.py:412
  9.3 6.3 %all-to-all-start = ((f32[32,8,128]{2,1,0:T(8,128)}), f32[32,8,128]{2,1,0:T(8,128)S(1)}, u32[]{:S(2)}, u32[]{:S(2)}) async-start(f32[32,8,128]{2,1,0:T(8,128)} %get-tuple-element.19), calls=%async_computation | async-start | bytes 262144 | tf_op jit(solution)/shard_map/all_to_all | solution.py:444
  15.6 1.2 %collective-permute-start = (f32[6,16,256]{2,1,0:T(8,128)}, f32[6,16,256]{2,1,0:T(8,128)S(1)}, u32[]{:S(2)}, u32[]{:S(2)}) collective-permute-start(f32[6,16,256]{2,1,0:T(8,128)} %get-tuple-element.21), channel_id=1, source_target_pairs={{0,1},{1,0},{2,3},{3,2},{4,5},{5,4},{6,7},{7,6},{8,9},{9,8},{10,11... | collective-permute-start | bytes 294920 | tf_op jit(solution)/shard_map/ppermute | solution.py:378
  16.8 2.0 %collective-permute-start.1 = (f32[6,16,256]{2,1,0:T(8,128)}, f32[6,16,256]{2,1,0:T(8,128)S(1)}, u32[]{:S(2)}, u32[]{:S(2)}) collective-permute-start(f32[6,16,256]{2,1,0:T(8,128)} %get-tuple-element.22), channel_id=1, source_target_pairs={{1,2},{2,1},{3,4},{4,3},{5,6},{6,5},{9,10},{10,9},{11,12},{12,11},... | collective-permute-start | bytes 294920 | tf_op jit(solution)/shard_map/ppermute | solution.py:378
  18.8 0.0 copy-done.3
  18.9 0.1 reshape.21.coef
  19.0 0.0 copy-done
  19.0 0.0 copy-done.1
  19.0 0.0 copy-done.2
  19.0 3.3 %early.1 = (f32[5,16,16,256]{3,2,1,0:T(8,128)}, bf16[2,240,256]{2,1,0:T(8,128)(2,1)S(1)}) custom-call(f32[150]{0:T(256)S(1)} %reshape.21.coef, f32[5,16,16,256]{3,2,1,0:T(8,128)S(1)} %copy-done, f32[5,16,16,256]{3,2,1,0:T(8,128)S(1)} %copy-done.1, f32[16,16,256]{2,1,0:T(8,128)S(1)} %copy-done.2), custom_call_target="tpu_custom_call" | custom-call | tf_op jit(solution)/shard_map/early/pallas_call | solution.py:446
  22.3 0.0 collective-permute-done.line_inner
  22.3 1.0 %collective-permute-done.1.line_outer = f32[6,16,256]{2,1,0:T(8,128)S(1)} collective-permute-done((f32[6,16,256]{2,1,0:T(8,128)}, f32[6,16,256]{2,1,0:T(8,128)S(1)}, u32[]{:S(2)}, u32[]{:S(2)}) %collective-permute-start.1) | collective-permute-done | bytes 98336 | tf_op jit(solution)/shard_map/ppermute | solution.py:378
  23.3 0.0 all-to-all-done.got
  23.3 5.7 %first.1 = (f32[5,16,16,256]{3,2,1,0:T(8,128)S(1)}, f32[256,256]{1,0:T(8,128)S(1)}, f32[12,16,256]{2,1,0:T(8,128)S(1)}, f32[12,16,256]{2,1,0:T(8,128)S(1)}, f32[...) custom-call(f32[150]{0:T(256)S(1)} %reshape.21.coef, ...), custom_call_target="tpu_custom_call" | custom-call | tf_op jit(solution)/shard_map/first/pallas_call | solution.py:455
  29.0 1.9 %collective-permute-start.2 = (f32[12,16,256]{2,1,0:T(8,128)S(1)}, f32[12,16,256]{2,1,0:T(8,128)S(1)}, u32[]{:S(2)}, u32[]{:S(2)}) collective-permute-start(f32[12,16,256]{2,1,0:T(8,128)S(1)} %get-tuple-element.29), channel_id=1, source_target_pairs={{0,8},{8,0},{16,24},{24,16},{1,9},{9,1},{17,25},{25,17},{2,10},{10... | collective-permute-start | bytes 589832 | tf_op jit(solution)/shard_map/ppermute | solution.py:378
  30.9 3.0 %collective-permute-start.3 = (f32[12,16,256]{2,1,0:T(8,128)S(1)}, f32[12,16,256]{2,1,0:T(8,128)S(1)}, u32[]{:S(2)}, u32[]{:S(2)}) collective-permute-start(f32[12,16,256]{2,1,0:T(8,128)S(1)} %get-tuple-element.30), channel_id=1, source_target_pairs={{8,16},{16,8},{9,17},{17,9},{10,18},{18,10},{11,19},{19,11},{12,20... | collective-permute-start | bytes 589832 | tf_op jit(solution)/shard_map/ppermute | solution.py:378
  33.9 0.5 %collective-permute-start.4 = (f32[5,16,256]{2,1,0:T(8,128)S(1)}, f32[5,16,256]{2,1,0:T(8,128)S(1)}, u32[]{:S(2)}, u32[]{:S(2)}) collective-permute-start(f32[5,16,256]{2,1,0:T(8,128)S(1)} %get-tuple-element.31), channel_id=1, source_target_pairs={{0,1},{1,0},{2,3},{3,2},{4,5},{5,4},{6,7},{7,6},{8,9},{9,8},{10,11... | collective-permute-start | bytes 245768 | tf_op jit(solution)/shard_map/ppermute | solution.py:378
  34.4 2.1 %collective-permute-start.5 = (f32[5,16,256]{2,1,0:T(8,128)S(1)}, f32[5,16,256]{2,1,0:T(8,128)S(1)}, u32[]{:S(2)}, u32[]{:S(2)}) collective-permute-start(f32[5,16,256]{2,1,0:T(8,128)S(1)} %get-tuple-element.32), channel_id=1, source_target_pairs={{1,2},{2,1},{3,4},{4,3},{5,6},{6,5},{9,10},{10,9},{11,12},{12,11},... | collective-permute-start | bytes 245768 | tf_op jit(solution)/shard_map/ppermute | solution.py:378
  36.5 2.9 %late.1.target = f32[5,256,256]{2,1,0:T(8,128)S(1)} custom-call(f32[5,2048]{1,0:T(8,128)S(1)} %get-tuple-element.25.rows, bf16[256,2048]{1,0:T(8,128)(2,1)S(1)} %get-tuple-element.26.hot_xy, bf16[2048,256]{1,0:T(8,128)(2,1)S(1)} %get-tuple-element.27.hot_z), custom_call_target="tpu_custom_call" | custom-call | tf_op jit(solution)/shard_map/late/pallas_call | solution.py:480
  39.4 0.0 collective-permute-done.4.y_inner
  39.4 1.1 %collective-permute-done.5.y_outer = f32[5,16,256]{2,1,0:T(8,128)S(1)} collective-permute-done((f32[5,16,256]{2,1,0:T(8,128)S(1)}, f32[5,16,256]{2,1,0:T(8,128)S(1)}, u32[]{:S(2)}, u32[]{:S(2)}) %collective-permute-start.5) | collective-permute-done | bytes 81952 | tf_op jit(solution)/shard_map/ppermute | solution.py:378
  40.5 0.0 collective-permute-done.2.x_inner
  40.5 0.0 collective-permute-done.3.x_outer
  40.5 3.6 %second.1 = f32[5,16,16,256]{3,2,1,0:T(8,128)} custom-call(f32[150]{0:T(256)S(1)} %reshape.21.coef, s32[2]{0:T(128)S(1)} %pad_add_fusion.parity, f32[5,16,16,256]{3,2,1,0:T(8,128)S(1)} %get-tuple-element.23.state, bf16[2,240,256]{2,1,0:T(8,128)(2,1)S(1)} %get-tuple-element.24.weights, f32[5,16,16,256]{3,2,1,0:T(8,128)S(1)} %copy-done, ...), custom_call_target="tpu_custom_call" | custom-call | tf_op jit(solution)/shard_map/second/pallas_call | solution.py:488
  (1 shorter events, 0.0 us)
Async XLA Ops:
  0.7 18.1 %copy-start.3 = (f32[3,2,5,5]{3,1,2,0:T(2,128)S(1)}, f32[3,2,5,5]{3,1,2,0:T(2,128)}, u32[]{:S(2)}) copy-start(f32[3,2,5,5]{3,1,2,0:T(2,128)} %param.12) | copy-start | bytes 1804
  0.7 18.2 %copy-start = (f32[5,16,16,256]{3,2,1,0:T(8,128)S(1)}, f32[5,16,16,256]{3,2,1,0:T(8,128)}, u32[]{:S(2)}) copy-start(f32[5,16,16,256]{3,2,1,0:T(8,128)} %q_now.5) | copy-start | bytes 3932164
  0.7 18.2 %copy-start.1 = (f32[5,16,16,256]{3,2,1,0:T(8,128)S(1)}, f32[5,16,16,256]{3,2,1,0:T(8,128)}, u32[]{:S(2)}) copy-start(f32[5,16,16,256]{3,2,1,0:T(8,128)} %q_prev.3) | copy-start | bytes 3932164
  0.7 18.3 %copy-start.2 = (f32[16,16,256]{2,1,0:T(8,128)S(1)}, f32[16,16,256]{2,1,0:T(8,128)}, u32[]{:S(2)}) copy-start(f32[16,16,256]{2,1,0:T(8,128)} %jac.5) | copy-start | bytes 786436
  9.3 14.0 %all-to-all-start = ((f32[32,8,128]{2,1,0:T(8,128)}), f32[32,8,128]{2,1,0:T(8,128)S(1)}, u32[]{:S(2)}, u32[]{:S(2)}) async-start(f32[32,8,128]{2,1,0:T(8,128)} %get-tuple-element.19), calls=%async_computation | async-start | bytes 262144 | tf_op jit(solution)/shard_map/all_to_all | solution.py:444
  15.6 6.7 %collective-permute-start = (f32[6,16,256]{2,1,0:T(8,128)}, f32[6,16,256]{2,1,0:T(8,128)S(1)}, u32[]{:S(2)}, u32[]{:S(2)}) collective-permute-start(f32[6,16,256]{2,1,0:T(8,128)} %get-tuple-element.21), channel_id=1, source_target_pairs={{0,1},{1,0},{2,3},{3,2},{4,5},{5,4},{6,7},{7,6},{8,9},{9,8},{10,11... | collective-permute-start | bytes 294920 | tf_op jit(solution)/shard_map/ppermute | solution.py:378
  16.8 6.5 %collective-permute-start.1 = (f32[6,16,256]{2,1,0:T(8,128)}, f32[6,16,256]{2,1,0:T(8,128)S(1)}, u32[]{:S(2)}, u32[]{:S(2)}) collective-permute-start(f32[6,16,256]{2,1,0:T(8,128)} %get-tuple-element.22), channel_id=1, source_target_pairs={{1,2},{2,1},{3,4},{4,3},{5,6},{6,5},{9,10},{10,9},{11,12},{12,11},... | collective-permute-start | bytes 294920 | tf_op jit(solution)/shard_map/ppermute | solution.py:378
  29.0 11.5 %collective-permute-start.2 = (f32[12,16,256]{2,1,0:T(8,128)S(1)}, f32[12,16,256]{2,1,0:T(8,128)S(1)}, u32[]{:S(2)}, u32[]{:S(2)}) collective-permute-start(f32[12,16,256]{2,1,0:T(8,128)S(1)} %get-tuple-element.29), channel_id=1, source_target_pairs={{0,8},{8,0},{16,24},{24,16},{1,9},{9,1},{17,25},{25,17},{2,10},{10... | collective-permute-start | bytes 589832 | tf_op jit(solution)/shard_map/ppermute | solution.py:378
  30.9 9.6 %collective-permute-start.3 = (f32[12,16,256]{2,1,0:T(8,128)S(1)}, f32[12,16,256]{2,1,0:T(8,128)S(1)}, u32[]{:S(2)}, u32[]{:S(2)}) collective-permute-start(f32[12,16,256]{2,1,0:T(8,128)S(1)} %get-tuple-element.30), channel_id=1, source_target_pairs={{8,16},{16,8},{9,17},{17,9},{10,18},{18,10},{11,19},{19,11},{12,20... | collective-permute-start | bytes 589832 | tf_op jit(solution)/shard_map/ppermute | solution.py:378
  33.9 5.5 %collective-permute-start.4 = (f32[5,16,256]{2,1,0:T(8,128)S(1)}, f32[5,16,256]{2,1,0:T(8,128)S(1)}, u32[]{:S(2)}, u32[]{:S(2)}) collective-permute-start(f32[5,16,256]{2,1,0:T(8,128)S(1)} %get-tuple-element.31), channel_id=1, source_target_pairs={{0,1},{1,0},{2,3},{3,2},{4,5},{5,4},{6,7},{7,6},{8,9},{9,8},{10,11... | collective-permute-start | bytes 245768 | tf_op jit(solution)/shard_map/ppermute | solution.py:378
  34.4 6.1 %collective-permute-start.5 = (f32[5,16,256]{2,1,0:T(8,128)S(1)}, f32[5,16,256]{2,1,0:T(8,128)S(1)}, u32[]{:S(2)}, u32[]{:S(2)}) collective-permute-start(f32[5,16,256]{2,1,0:T(8,128)S(1)} %get-tuple-element.32), channel_id=1, source_target_pairs={{1,2},{2,1},{3,4},{4,3},{5,6},{6,5},{9,10},{10,9},{11,12},{12,11},... | collective-permute-start | bytes 245768 | tf_op jit(solution)/shard_map/ppermute | solution.py:378

commit v5 on v4

--- a/solution.py
+++ b/solution.py
@@ -49,7 +49,7 @@
     return jnp.concatenate(pieces, axis=1)
 
 
-def donor_kernel(count, parity, q_prev, q_now, base_in, frac_in, dest_in, cell_in, jac_in, out, y_inner, y_outer, planes, jac, lhs, spread, corner, place, values, base, frac, dest, cell, sems, *, size, devices, capacity):
+def donor_kernel(count, q_prev, q_now, base_in, frac_in, dest_in, cell_in, jac_in, out, y_inner, y_outer, planes, jac, lhs, spread, corner, place, values, base, frac, dest, cell, sems, *, size, devices, capacity):
     nvars, size_x, size_y, size_z = size
     columns = size_x * size_y
     rows = base.shape[1]
@@ -91,7 +91,7 @@
         copies[k].wait()
         if k == 1:
             small[4].wait()
-            even = parity[1] == 0
+            even = lax.axis_index("gy") % 2 == 0
             for v in range(nvars + 1):
                 for x in range(size_x):
                     line = planes.at[1, v] if v < nvars else jac
@@ -210,10 +210,15 @@
         copies[-1].start()
 
 
-def early_kernel(coef, q_now, q_prev, jac, base, weights, planes, buffer, sems, *, size):
-    nvars, size_x, _, _ = size
+def early_kernel(coef_in, q_now, q_prev, jac, base, weights, table, planes, coef, buffer, sems, *, size):
+    nvars, size_x, _, size_z = size
+    fetch = pltpu.make_async_copy(coef_in, coef, sems.at[4])
+    fetch.start()
+    fill_planes(lambda v, x: q_now[v, x], None, planes, None, size)
+    fetch.wait()
+    for k in range(table.shape[0]):
+        table[k : k + 1, :] = jnp.full((1, size_z), coef[k], jnp.float32)
     mixing_weights(coef, weights.at[0], weights.at[1], size)
-    fill_planes(lambda v, x: q_now[v, x], None, planes, None, size)
     copies = []
     for x in range(size_x):
         flux = flux_at(x, weights, planes, None, size)
@@ -227,13 +232,14 @@
         copy.wait()
 
 
-def mixed_by(coef, direction, side, lines):
+def mixed_by(table, direction, side, lines):
     nvars = len(lines)
     out = []
     for a in range(nvars):
         total = None
         for b in range(nvars):
-            term = coef[((direction * 2 + side) * nvars + a) * nvars + b] * lines[b]
+            k = ((direction * 2 + side) * nvars + a) * nvars + b
+            term = table[k : k + 1, :] * lines[b]
             total = term if total is None else total + term
         out.append(total)
     return out
@@ -253,12 +259,16 @@
             store(c, landed[at : at + columns] + landed[at + columns : at + 2 * columns])
 
 
-def first_kernel(coef, parity, got, base_in, q_now, jac, line_inner, line_outer, state, hits, x_inner, x_outer, y_inner, y_outer, later, hot_xy, hot_z, rows, grid, base, sem, *, size, devices, capacity):
+def first_kernel(table, got, base_in, q_now, jac, line_inner, line_outer, state, hits, x_inner, x_outer, y_inner, y_outer, later, hot_xy, hot_z, rows, grid, base, sems, *, size, devices, capacity):
     nvars, size_x, size_y, size_z = size
     columns = size_x * size_y
     slots = devices * capacity
-    fetch = pltpu.make_async_copy(base_in, base, sem)
-    fetch.start()
+    part = size_x // 4
+    fetches = []
+    for k in range(4):
+        some = pl.ds(k * part, part)
+        fetches.append(pltpu.make_async_copy(base_in.at[:, some], base.at[:, some], sems.at[k]))
+        fetches[-1].start()
     for d in range(devices):
         piece = got[d]
         lanes = slice(d * capacity, (d + 1) * capacity)
@@ -276,13 +286,14 @@
 
     hits[...] = dot(hot_xy[...], hot_z[...], ((1,), (0,)))
     land(rows, hot_xy, hot_z, keep, nvars)
-    even_x, even_y = parity[0] == 0, parity[1] == 0
+    even_x, even_y = lax.axis_index("gx") % 2 == 0, lax.axis_index("gy") % 2 == 0
     y_low = [jnp.where(even_y, line_outer[v], line_inner[v]) for v in range(nvars)]
     y_high = [jnp.where(even_y, line_inner[v], line_outer[v]) for v in range(nvars)]
-    from_low, from_high = mixed_by(coef, 1, 0, y_low), mixed_by(coef, 1, 1, y_high)
+    from_low, from_high = mixed_by(table, 1, 0, y_low), mixed_by(table, 1, 1, y_high)
     row_at = iota((size_y, size_z), 0)
-    fetch.wait()
     faces = {}
+    for fetch in fetches:
+        fetch.wait()
     for x in range(size_x):
         at = slice(x * size_y, (x + 1) * size_y)
         landed = hits[at, :]
@@ -319,16 +330,16 @@
     land(rows, hot_xy, hot_z, keep, rows.shape[0])
 
 
-def second_kernel(coef, parity, state, weights, q_now, q_prev, jac, target, hits, x_inner, x_outer, y_inner, y_outer, line_inner, line_outer, out, planes, sides, edge, buffer, sems, *, size):
+def second_kernel(table, state, weights, q_now, q_prev, jac, target, hits, x_inner, x_outer, y_inner, y_outer, line_inner, line_outer, out, planes, sides, edge, buffer, sems, *, size):
     nvars, size_x, size_y, size_z = size
     last = size_x - 1
-    even_x, even_y = parity[0] == 0, parity[1] == 0
+    even_x, even_y = lax.axis_index("gx") % 2 == 0, lax.axis_index("gy") % 2 == 0
     x_low = [jnp.where(even_x, x_outer[k], x_inner[k]) for k in range(2 * nvars + 2)]
     x_high = [jnp.where(even_x, x_inner[k], x_outer[k]) for k in range(2 * nvars + 2)]
-    own_low = mixed_by(coef, 0, 0, x_low[nvars : 2 * nvars])
-    own_high = mixed_by(coef, 0, 1, x_high[nvars : 2 * nvars])
-    ring_low = mixed_by(coef, 0, 1, [q_now[v, 0] for v in range(nvars)])
-    ring_high = mixed_by(coef, 0, 0, [q_now[v, last] for v in range(nvars)])
+    own_low = mixed_by(table, 0, 0, x_low[nvars : 2 * nvars])
+    own_high = mixed_by(table, 0, 1, x_high[nvars : 2 * nvars])
+    ring_low = mixed_by(table, 0, 1, [q_now[v, 0] for v in range(nvars)])
+    ring_high = mixed_by(table, 0, 0, [q_now[v, last] for v in range(nvars)])
     around = [[], [], [], []]
     for v in range(nvars):
         edge[0, v] = state[v, 0] + step_tau * jac[0] * own_low[v]
@@ -340,8 +351,8 @@
         pick = (y_outer, y_inner, line_outer, line_inner) if side == 0 else (y_inner, y_outer, line_inner, line_outer)
         scale = step_tau * jnp.where(even_y, pick[2][nvars], pick[3][nvars])
         corner = slice(side * nvars, (side + 1) * nvars)
-        low = mixed_by(coef, 0, 0, [x_low[2 * nvars + 1][k : k + 1] for k in range(corner.start, corner.stop)])
-        high = mixed_by(coef, 0, 1, [x_high[2 * nvars + 1][k : k + 1] for k in range(corner.start, corner.stop)])
+        low = mixed_by(table, 0, 0, [x_low[2 * nvars + 1][k : k + 1] for k in range(corner.start, corner.stop)])
+        high = mixed_by(table, 0, 1, [x_high[2 * nvars + 1][k : k + 1] for k in range(corner.start, corner.stop)])
         for v in range(nvars):
             change = jnp.where(row_at == 0, low[v], 0.0) - jnp.where(row_at == last, high[v], 0.0)
             around[2 + side].append(jnp.where(even_y, pick[0][v], pick[1][v]) + scale * change)
@@ -392,7 +403,6 @@
     capacity = 2 * rows // devices
     slots = devices * capacity
     f32, bf16 = jnp.float32, jnp.bfloat16
-    smem = pl.BlockSpec(memory_space=pltpu.SMEM)
     hbm = pl.BlockSpec(memory_space=pltpu.HBM)
     vmem = pl.BlockSpec(memory_space=pltpu.VMEM)
     flat = (nvars, columns, size_z)
@@ -402,17 +412,16 @@
     sides = pltpu.VMEM((size_x, CHANNELS, size_z), f32)
     face_y = shape((nvars, size_x, size_z), f32)
 
-    line, line_x = shape((nvars + 1, size_x, size_z), f32), shape((2 * nvars + 2, size_y, size_z), f32)
+    line, line_x = pltpu.VMEM((nvars + 1, size_x, size_z), f32), shape((2 * nvars + 2, size_y, size_z), f32)
     coef = flux_split.reshape(-1)
-    parity = jnp.stack([lax.axis_index("gx") % 2, lax.axis_index("gy") % 2]).astype(jnp.int32)
 
     def there(x):
         return pltpu.with_memory_space_constraint(x, pltpu.HBM)
 
     sent, *lines = pl.pallas_call(
         functools.partial(donor_kernel, size=size, devices=devices, capacity=capacity),
-        out_shape=[shape((devices, 8, 2 * capacity), f32), line, line],
-        in_specs=[smem, smem] + [hbm] * 7,
+        out_shape=[pltpu.VMEM((devices, 8, 2 * capacity), f32), line, line],
+        in_specs=[pl.BlockSpec(memory_space=pltpu.SMEM)] + [hbm] * 7,
         out_specs=[vmem] * 3,
         scratch_shapes=[
             pltpu.VMEM((2, nvars, columns, size_z), f32),
@@ -432,7 +441,6 @@
         name="donor",
     )(
         fringe_count,
-        parity,
         there(q_prev.reshape(flat)),
         there(q_now.reshape(flat)),
         there(donor_base.reshape(1, rows)),
@@ -443,15 +451,15 @@
     )
     got = lax.all_to_all(sent, AXES, split_axis=0, concat_axis=0, tiled=True)
     lines = swapped(*lines, "gy")
-    base, weights = pl.pallas_call(
+    base, weights, table = pl.pallas_call(
         functools.partial(early_kernel, size=size),
-        out_shape=[pltpu.HBM(size, f32), shape(weights_shape, bf16)],
-        in_specs=[smem] + [vmem] * 3,
-        out_specs=[hbm, vmem],
-        scratch_shapes=[planes, pltpu.VMEM(size, f32), pltpu.SemaphoreType.DMA((4,))],
+        out_shape=[pltpu.HBM(size, f32), shape(weights_shape, bf16), shape((4 * nvars * nvars, size_z), f32)],
+        in_specs=[hbm] + [vmem] * 3,
+        out_specs=[hbm, vmem, vmem],
+        scratch_shapes=[planes, pltpu.SMEM((6 * nvars * nvars,), f32), pltpu.VMEM(size, f32), pltpu.SemaphoreType.DMA((5,))],
         compiler_params=params(20 * MIB),
         name="early",
-    )(coef, q_now, q_prev, jacobian)
+    )(there(coef), q_now, q_prev, jacobian)
     state, hits, *faces, later, hot_xy, hot_z = pl.pallas_call(
         functools.partial(first_kernel, size=size, devices=devices, capacity=capacity),
         out_shape=[
@@ -465,17 +473,17 @@
             shape((columns, slots), bf16),
             shape((slots, size_z), bf16),
         ],
-        in_specs=[smem, smem, vmem, hbm] + [vmem] * 4,
+        in_specs=[vmem, vmem, hbm] + [vmem] * 4,
         out_specs=[vmem] * 9,
         scratch_shapes=[
             pltpu.VMEM((CHANNELS, slots), f32),
             pltpu.VMEM((nvars, columns, size_z), f32),
             pltpu.VMEM(size, f32),
-            pltpu.SemaphoreType.DMA,
+            pltpu.SemaphoreType.DMA((4,)),
         ],
         compiler_params=params(20 * MIB),
         name="first",
-    )(coef, parity, got, there(base), q_now, jacobian, *lines)
+    )(table, got, there(base), q_now, jacobian, *lines)
     around = (*swapped(*faces[0:2], "gx"), *swapped(*faces[2:4], "gy"))
     target = pl.pallas_call(
         late_kernel,
@@ -488,12 +496,12 @@
     return pl.pallas_call(
         functools.partial(second_kernel, size=size),
         out_shape=shape(size, f32),
-        in_specs=[smem, smem] + [vmem] * 13,
+        in_specs=[vmem] * 14,
         out_specs=hbm,
         scratch_shapes=[planes, sides, pltpu.VMEM((2, nvars, size_y, size_z), f32), pltpu.VMEM(size, f32), pltpu.SemaphoreType.DMA((4,))],
         compiler_params=params(20 * MIB),
         name="second",
-    )(coef, parity, state, weights, q_now, q_prev, jacobian, target, hits, *around, *lines)
+    )(table, state, weights, q_now, q_prev, jacobian, target, hits, *around, *lines)
 
 
 def solution(mesh):

time: 44.8 us -> 44.6 us (level)
  Pallas kernels: 24 us -> 22.7 us
  local copies, waits for them, and re-layouts: 0.12 us -> 1.4 us
  waiting for transfers between devices: 2.07 us -> 1.07 us
  starting transfers between devices: 17.1 us -> 18 us
    ppermute x3, waiting for transfers between devices: 2.06 us -> 1.06 us  [swapped(): lax.ppermute(outer, axis, swap_pairs(axis, 1))]
    ppermute x3, starting transfers between devices: 3.65 us -> 4.62 us  [swapped(): lax.ppermute(inner, axis, swap_pairs(axis, 0))]
    unnamed x9 -> x13, local copies, waits for them, and re-layouts: 0.02 us -> 0.71 us
    pallas_call x1, Pallas kernels: 8.5 us -> 7.81 us  [body(): pl.pallas_call(functools.partial(donor_kernel, size=size, devices=devices...]
    reshape x1, local copies, waits for them, and re-layouts: 0.1 us -> 0.68 us  [body(): coef = flux_split.reshape(-1)]
    pallas_call x1, Pallas kernels: 3.61 us -> 3.06 us  [body(): pl.pallas_call(functools.partial(second_kernel, size=size), out_shape=sha...]
  transfers between devices with their start and end apart: 7 -> 7, of which waited for: 2 -> 1; matrix products, arithmetic and copies ran while one was open for 0% -> 2% of each run, Pallas kernels for 14% -> 14%
where the time goes in v5:
time: 44.6 us; the launch traced here: 44.1 us
  Pallas kernels  22.7 us (51%)
  starting transfers between devices  18 us (40%)
  local copies, waits for them, and re-layouts  1.4 us (3%)
  waiting for transfers between devices  1.07 us (2%)
  between operations  0.96 us (2%)
    pallas_call x1, Pallas kernels, body(): pl.pallas_call(functools.partial(donor_kernel, size=size, devices=devices...  7.81 us
    ppermute x3, starting transfers between devices, swapped(): lax.ppermute(outer, axis, swap_pairs(axis, 1))  7.09 us
    all_to_all x1, starting transfers between devices, body(): got = lax.all_to_all(sent, AXES, split_axis=0, concat_axis=0, tiled=True)  6.33 us
    pallas_call x1, Pallas kernels, body(): pl.pallas_call(functools.partial(first_kernel, size=size, devices=devices...  5.43 us
    ppermute x3, starting transfers between devices, swapped(): lax.ppermute(inner, axis, swap_pairs(axis, 0))  4.62 us
    pallas_call x1, Pallas kernels, body(): pl.pallas_call(functools.partial(early_kernel, size=size), out_shape=[plt...  3.46 us
    pallas_call x1, Pallas kernels, body(): pl.pallas_call(functools.partial(second_kernel, size=size), out_shape=sha...  3.06 us
    pallas_call x1, Pallas kernels, body(): pl.pallas_call(late_kernel, out_shape=shape(flat, f32), in_specs=[vmem] *...  2.89 us
  transfers between devices with their start and end apart: 7, of which 1 were waited for; matrix products, arithmetic and copies ran while one was open for 2% of the time, Pallas kernels for 14%

profile of v5, /device:TPU:9, one launch (start us, length us, event | category | flops | bytes accessed | tf_op | source)
XLA Modules:
  0.0 44.1 jit_solution(6093867015554715181)
XLA Ops:
  0.7 0.0 copy-start.5
  0.7 0.0 copy-start
  0.7 0.0 copy-start.1
  0.7 0.0 copy-start.2
  0.7 7.8 %donor.1 = (f32[32,8,128]{2,1,0:T(8,128)}, f32[6,16,256]{2,1,0:T(8,128)S(1)}, f32[6,16,256]{2,1,0:T(8,128)S(1)}) custom-call(s32[1]{0:T(128)S(6)} %copy.11.count, f32[5,256,256]{2,1,0:T(8,128)} %bitcast.7, f32[5,256,256]{2,1,0:T(8,128)} %bitcast.6, s32[1,1024]{1,0:T(1,128)} %bitcast.9, f32[3,1024]{1,0:T(4,128)} %frac_in.1, s32[1,1024]{1,0:T(1,128)} %bitcast.10, ...), custom_call_target="tpu_custom_call" | custom-call | tf_op jit(solution)/shard_map/donor/pallas_call | solution.py:421
  8.5 6.3 %all-to-all-start = ((f32[32,8,128]{2,1,0:T(8,128)}), f32[32,8,128]{2,1,0:T(8,128)S(1)}, u32[]{:S(2)}, u32[]{:S(2)}) async-start(f32[32,8,128]{2,1,0:T(8,128)} %get-tuple-element.21), calls=%async_computation | async-start | bytes 262144 | tf_op jit(solution)/shard_map/all_to_all | solution.py:452
  14.8 1.2 %collective-permute-start = (f32[6,16,256]{2,1,0:T(8,128)S(1)}, f32[6,16,256]{2,1,0:T(8,128)S(1)}, u32[]{:S(2)}, u32[]{:S(2)}) collective-permute-start(f32[6,16,256]{2,1,0:T(8,128)S(1)} %get-tuple-element.23), channel_id=1, source_target_pairs={{0,1},{1,0},{2,3},{3,2},{4,5},{5,4},{6,7},{7,6},{8,9},{9,8},{10,11... | collective-permute-start | bytes 294920 | tf_op jit(solution)/shard_map/ppermute | solution.py:389
  16.1 2.0 %collective-permute-start.1 = (f32[6,16,256]{2,1,0:T(8,128)S(1)}, f32[6,16,256]{2,1,0:T(8,128)S(1)}, u32[]{:S(2)}, u32[]{:S(2)}) collective-permute-start(f32[6,16,256]{2,1,0:T(8,128)S(1)} %get-tuple-element.24), channel_id=1, source_target_pairs={{1,2},{2,1},{3,4},{4,3},{5,6},{6,5},{9,10},{10,9},{11,12},{12,11},... | collective-permute-start | bytes 294920 | tf_op jit(solution)/shard_map/ppermute | solution.py:389
  18.1 0.0 copy-done.5
  18.1 0.7 %reshape.21.coef_in = f32[150]{0:T(256)} reshape(f32[3,2,5,5]{3,2,1,0:T(8,128)S(1)} %copy.10) | data formatting | bytes 1200 | tf_op jit(solution)/shard_map/reshape | solution.py:416
  18.8 0.0 copy-done
  18.8 0.0 copy-done.1
  18.8 0.0 copy-done.2
  18.8 3.5 %early.1 = (f32[5,16,16,256]{3,2,1,0:T(8,128)}, bf16[2,240,256]{2,1,0:T(8,128)(2,1)S(1)}, f32[100,256]{1,0:T(8,128)S(1)}) custom-call(f32[150]{0:T(256)} %reshape.21.coef_in, f32[5,16,16,256]{3,2,1,0:T(8,128)S(1)} %copy-done, f32[5,16,16,256]{3,2,1,0:T(8,128)S(1)} %copy-done.1, f32[16,16,256]{2,1,0:T(8,128)S(1)} %copy-done.2), custom_call_target="tpu_custom_call" | custom-call | tf_op jit(solution)/shard_map/early/pallas_call | solution.py:454
  22.3 0.0 copy-start.3
  22.3 0.7 %copy-done.3 = bf16[2,240,256]{2,1,0:T(8,128)(2,1)} copy-done((bf16[2,240,256]{2,1,0:T(8,128)(2,1)}, bf16[2,240,256]{2,1,0:T(8,128)(2,1)S(1)}, u32[]{:S(2)}) %copy-start.3) | copy-done | bytes 245784
  23.0 0.0 collective-permute-done.line_inner
  23.0 0.0 collective-permute-done.1.line_outer
  23.0 0.0 all-to-all-done.got
  23.0 5.4 %first.1 = (f32[5,16,16,256]{3,2,1,0:T(8,128)S(1)}, f32[256,256]{1,0:T(8,128)S(1)}, f32[12,16,256]{2,1,0:T(8,128)S(1)}, f32[12,16,256]{2,1,0:T(8,128)S(1)}, f32[...) custom-call(f32[100,256]{1,0:T(8,128)S(1)} %get-tuple-element.20.tab, ...), custom_call_target="tpu_custom_call" | custom-call | tf_op jit(solution)/shard_map/first/pallas_call | solution.py:463
  28.4 1.2 %collective-permute-start.2 = (f32[12,16,256]{2,1,0:T(8,128)S(1)}, f32[12,16,256]{2,1,0:T(8,128)S(1)}, u32[]{:S(2)}, u32[]{:S(2)}) collective-permute-start(f32[12,16,256]{2,1,0:T(8,128)S(1)} %get-tuple-element.31), channel_id=1, source_target_pairs={{0,8},{8,0},{16,24},{24,16},{1,9},{9,1},{17,25},{25,17},{2,10},{10... | collective-permute-start | bytes 589832 | tf_op jit(solution)/shard_map/ppermute | solution.py:389
  29.7 3.0 %collective-permute-start.3 = (f32[12,16,256]{2,1,0:T(8,128)S(1)}, f32[12,16,256]{2,1,0:T(8,128)S(1)}, u32[]{:S(2)}, u32[]{:S(2)}) collective-permute-start(f32[12,16,256]{2,1,0:T(8,128)S(1)} %get-tuple-element.32), channel_id=1, source_target_pairs={{8,16},{16,8},{9,17},{17,9},{10,18},{18,10},{11,19},{19,11},{12,20... | collective-permute-start | bytes 589832 | tf_op jit(solution)/shard_map/ppermute | solution.py:389
  32.7 2.1 %collective-permute-start.4 = (f32[5,16,256]{2,1,0:T(8,128)S(1)}, f32[5,16,256]{2,1,0:T(8,128)S(1)}, u32[]{:S(2)}, u32[]{:S(2)}) collective-permute-start(f32[5,16,256]{2,1,0:T(8,128)S(1)} %get-tuple-element.33), channel_id=1, source_target_pairs={{0,1},{1,0},{2,3},{3,2},{4,5},{5,4},{6,7},{7,6},{8,9},{9,8},{10,11... | collective-permute-start | bytes 245768 | tf_op jit(solution)/shard_map/ppermute | solution.py:389
  34.8 2.1 %collective-permute-start.5 = (f32[5,16,256]{2,1,0:T(8,128)S(1)}, f32[5,16,256]{2,1,0:T(8,128)S(1)}, u32[]{:S(2)}, u32[]{:S(2)}) collective-permute-start(f32[5,16,256]{2,1,0:T(8,128)S(1)} %get-tuple-element.34), channel_id=1, source_target_pairs={{1,2},{2,1},{3,4},{4,3},{5,6},{6,5},{9,10},{10,9},{11,12},{12,11},... | collective-permute-start | bytes 245768 | tf_op jit(solution)/shard_map/ppermute | solution.py:389
  36.9 0.0 copy-start.4
  36.9 2.9 %late.1.target = f32[5,256,256]{2,1,0:T(8,128)S(1)} custom-call(f32[5,2048]{1,0:T(8,128)S(1)} %get-tuple-element.27.rows, bf16[256,2048]{1,0:T(8,128)(2,1)S(1)} %get-tuple-element.28.hot_xy, bf16[2048,256]{1,0:T(8,128)(2,1)S(1)} %get-tuple-element.29.hot_z), custom_call_target="tpu_custom_call" | custom-call | tf_op jit(solution)/shard_map/late/pallas_call | solution.py:488
  39.8 0.0 collective-permute-done.4.y_inner
  39.8 1.1 %collective-permute-done.5.y_outer = f32[5,16,256]{2,1,0:T(8,128)S(1)} collective-permute-done((f32[5,16,256]{2,1,0:T(8,128)S(1)}, f32[5,16,256]{2,1,0:T(8,128)S(1)}, u32[]{:S(2)}, u32[]{:S(2)}) %collective-permute-start.5) | collective-permute-done | bytes 81952 | tf_op jit(solution)/shard_map/ppermute | solution.py:389
  40.9 0.0 collective-permute-done.2.x_inner
  40.9 0.0 collective-permute-done.3.x_outer
  40.9 0.0 copy-done.4
  40.9 3.1 %second.1 = f32[5,16,16,256]{3,2,1,0:T(8,128)} custom-call(f32[100,256]{1,0:T(8,128)S(1)} %get-tuple-element.20.table, f32[5,16,16,256]{3,2,1,0:T(8,128)S(1)} %get-tuple-element.25.state, bf16[2,240,256]{2,1,0:T(8,128)(2,1)S(1)} %copy-done.4, f32[5,16,16,256]{3,2,1,0:T(8,128)S(1)} %copy-done, f32[5,16,16,256]{3,2,1,0:T(8,128)S(1)} %copy-done.1, ...), custom_call_target="tpu_custom_call" | custom-call | tf_op jit(solution)/shard_map/second/pallas_call | solution.py:496
  (1 shorter events, 0.0 us)
Async XLA Ops:
  0.7 17.5 %copy-start.5 = (f32[3,2,5,5]{3,1,2,0:T(2,128)S(1)}, f32[3,2,5,5]{3,1,2,0:T(2,128)}, u32[]{:S(2)}) copy-start(f32[3,2,5,5]{3,1,2,0:T(2,128)} %param.12) | copy-start | bytes 1804
  0.7 18.2 %copy-start = (f32[5,16,16,256]{3,2,1,0:T(8,128)S(1)}, f32[5,16,16,256]{3,2,1,0:T(8,128)}, u32[]{:S(2)}) copy-start(f32[5,16,16,256]{3,2,1,0:T(8,128)} %q_now.5) | copy-start | bytes 3932164
  0.7 18.2 %copy-start.1 = (f32[5,16,16,256]{3,2,1,0:T(8,128)S(1)}, f32[5,16,16,256]{3,2,1,0:T(8,128)}, u32[]{:S(2)}) copy-start(f32[5,16,16,256]{3,2,1,0:T(8,128)} %q_prev.3) | copy-start | bytes 3932164
  0.7 18.1 %copy-start.2 = (f32[16,16,256]{2,1,0:T(8,128)S(1)}, f32[16,16,256]{2,1,0:T(8,128)}, u32[]{:S(2)}) copy-start(f32[16,16,256]{2,1,0:T(8,128)} %jac.5) | copy-start | bytes 786436
  8.5 14.5 %all-to-all-start = ((f32[32,8,128]{2,1,0:T(8,128)}), f32[32,8,128]{2,1,0:T(8,128)S(1)}, u32[]{:S(2)}, u32[]{:S(2)}) async-start(f32[32,8,128]{2,1,0:T(8,128)} %get-tuple-element.21), calls=%async_computation | async-start | bytes 262144 | tf_op jit(solution)/shard_map/all_to_all | solution.py:452
  14.8 8.1 %collective-permute-start = (f32[6,16,256]{2,1,0:T(8,128)S(1)}, f32[6,16,256]{2,1,0:T(8,128)S(1)}, u32[]{:S(2)}, u32[]{:S(2)}) collective-permute-start(f32[6,16,256]{2,1,0:T(8,128)S(1)} %get-tuple-element.23), channel_id=1, source_target_pairs={{0,1},{1,0},{2,3},{3,2},{4,5},{5,4},{6,7},{7,6},{8,9},{9,8},{10,11... | collective-permute-start | bytes 294920 | tf_op jit(solution)/shard_map/ppermute | solution.py:389
  16.1 6.9 %collective-permute-start.1 = (f32[6,16,256]{2,1,0:T(8,128)S(1)}, f32[6,16,256]{2,1,0:T(8,128)S(1)}, u32[]{:S(2)}, u32[]{:S(2)}) collective-permute-start(f32[6,16,256]{2,1,0:T(8,128)S(1)} %get-tuple-element.24), channel_id=1, source_target_pairs={{1,2},{2,1},{3,4},{4,3},{5,6},{6,5},{9,10},{10,9},{11,12},{12,11},... | collective-permute-start | bytes 294920 | tf_op jit(solution)/shard_map/ppermute | solution.py:389
  22.3 0.7 %copy-start.3 = (bf16[2,240,256]{2,1,0:T(8,128)(2,1)}, bf16[2,240,256]{2,1,0:T(8,128)(2,1)S(1)}, u32[]{:S(2)}) copy-start(bf16[2,240,256]{2,1,0:T(8,128)(2,1)S(1)} %get-tuple-element.26.weights) | copy-start | bytes 737284
  28.4 12.4 %collective-permute-start.2 = (f32[12,16,256]{2,1,0:T(8,128)S(1)}, f32[12,16,256]{2,1,0:T(8,128)S(1)}, u32[]{:S(2)}, u32[]{:S(2)}) collective-permute-start(f32[12,16,256]{2,1,0:T(8,128)S(1)} %get-tuple-element.31), channel_id=1, source_target_pairs={{0,8},{8,0},{16,24},{24,16},{1,9},{9,1},{17,25},{25,17},{2,10},{10... | collective-permute-start | bytes 589832 | tf_op jit(solution)/shard_map/ppermute | solution.py:389
  29.7 11.2 %collective-permute-start.3 = (f32[12,16,256]{2,1,0:T(8,128)S(1)}, f32[12,16,256]{2,1,0:T(8,128)S(1)}, u32[]{:S(2)}, u32[]{:S(2)}) collective-permute-start(f32[12,16,256]{2,1,0:T(8,128)S(1)} %get-tuple-element.32), channel_id=1, source_target_pairs={{8,16},{16,8},{9,17},{17,9},{10,18},{18,10},{11,19},{19,11},{12,20... | collective-permute-start | bytes 589832 | tf_op jit(solution)/shard_map/ppermute | solution.py:389
  32.7 7.1 %collective-permute-start.4 = (f32[5,16,256]{2,1,0:T(8,128)S(1)}, f32[5,16,256]{2,1,0:T(8,128)S(1)}, u32[]{:S(2)}, u32[]{:S(2)}) collective-permute-start(f32[5,16,256]{2,1,0:T(8,128)S(1)} %get-tuple-element.33), channel_id=1, source_target_pairs={{0,1},{1,0},{2,3},{3,2},{4,5},{5,4},{6,7},{7,6},{8,9},{9,8},{10,11... | collective-permute-start | bytes 245768 | tf_op jit(solution)/shard_map/ppermute | solution.py:389
  34.8 6.1 %collective-permute-start.5 = (f32[5,16,256]{2,1,0:T(8,128)S(1)}, f32[5,16,256]{2,1,0:T(8,128)S(1)}, u32[]{:S(2)}, u32[]{:S(2)}) collective-permute-start(f32[5,16,256]{2,1,0:T(8,128)S(1)} %get-tuple-element.34), channel_id=1, source_target_pairs={{1,2},{2,1},{3,4},{4,3},{5,6},{6,5},{9,10},{10,9},{11,12},{12,11},... | collective-permute-start | bytes 245768 | tf_op jit(solution)/shard_map/ppermute | solution.py:389
  36.9 4.0 %copy-start.4 = (bf16[2,240,256]{2,1,0:T(8,128)(2,1)S(1)}, bf16[2,240,256]{2,1,0:T(8,128)(2,1)}, u32[]{:S(2)}) copy-start(bf16[2,240,256]{2,1,0:T(8,128)(2,1)} %copy-done.3) | copy-start | bytes 737284

commit v6 on v5

--- a/solution.py
+++ b/solution.py
@@ -53,8 +53,8 @@
     nvars, size_x, size_y, size_z = size
     columns = size_x * size_y
     rows = base.shape[1]
-    small = [pltpu.make_async_copy(a, b, sems.at[2 + k]) for k, (a, b) in enumerate(((base_in, base), (frac_in, frac), (dest_in, dest), (cell_in, cell), (jac_in, jac)))]
-    copies = [pltpu.make_async_copy(ref, planes.at[k], sems.at[k]) for k, ref in enumerate((q_prev, q_now))]
+    small = [pltpu.make_async_copy(a, b, sems.at[k]) for k, (a, b) in enumerate(((base_in, base), (frac_in, frac), (dest_in, dest), (cell_in, cell), (jac_in, jac)))]
+    copies = [pltpu.make_async_copy(ref.at[v], planes.at[k, v], sems.at[5 + k * nvars + v]) for k, ref in enumerate((q_prev, q_now)) for v in range(nvars)]
     for copy in small + copies:
         copy.start()
     for copy in small[0:4]:
@@ -88,8 +88,9 @@
     values[2 * nvars : 2 * nvars + 1, :] = land_xy + 1.0
     values[2 * nvars + 1 : 2 * nvars + 2, :] = landing - land_xy * size_z
     for k in range(2):
-        copies[k].wait()
         if k == 1:
+            for v in range(nvars):
+                copies[nvars + v].wait()
             small[4].wait()
             even = lax.axis_index("gy") % 2 == 0
             for v in range(nvars + 1):
@@ -100,6 +101,8 @@
                     y_inner[v, x : x + 1, :] = jnp.where(even, high, low)
                     y_outer[v, x : x + 1, :] = jnp.where(even, low, high)
         for v in range(nvars):
+            if k == 0:
+                copies[v].wait()
             at = pl.ds((k * nvars + v) * columns, columns)
             high, low = halves(planes[k, v])
             lhs[0, at, :] = high
@@ -210,7 +213,7 @@
         copies[-1].start()
 
 
-def early_kernel(coef_in, q_now, q_prev, jac, base, weights, table, planes, coef, buffer, sems, *, size):
+def early_kernel(coef_in, q_now, q_prev, jac, base, weights_out, table, planes, coef, buffer, weights, sems, *, size):
     nvars, size_x, _, size_z = size
     fetch = pltpu.make_async_copy(coef_in, coef, sems.at[4])
     fetch.start()
@@ -219,7 +222,8 @@
     for k in range(table.shape[0]):
         table[k : k + 1, :] = jnp.full((1, size_z), coef[k], jnp.float32)
     mixing_weights(coef, weights.at[0], weights.at[1], size)
-    copies = []
+    copies = [pltpu.make_async_copy(weights, weights_out, sems.at[5])]
+    copies[0].start()
     for x in range(size_x):
         flux = flux_at(x, weights, planes, None, size)
         scale = step_tau * jac[x]
@@ -263,12 +267,14 @@
     nvars, size_x, size_y, size_z = size
     columns = size_x * size_y
     slots = devices * capacity
-    part = size_x // 4
-    fetches = []
-    for k in range(4):
-        some = pl.ds(k * part, part)
-        fetches.append(pltpu.make_async_copy(base_in.at[:, some], base.at[:, some], sems.at[k]))
-        fetches[-1].start()
+
+    def fetch(x):
+        return pltpu.make_async_copy(base_in.at[:, pl.ds(x, 1)], base.at[:, pl.ds(x, 1)], sems.at[x])
+
+    @pl.loop(0, size_x)
+    def _(x):
+        fetch(x).start()
+
     for d in range(devices):
         piece = got[d]
         lanes = slice(d * capacity, (d + 1) * capacity)
@@ -287,13 +293,12 @@
     hits[...] = dot(hot_xy[...], hot_z[...], ((1,), (0,)))
     land(rows, hot_xy, hot_z, keep, nvars)
     even_x, even_y = lax.axis_index("gx") % 2 == 0, lax.axis_index("gy") % 2 == 0
-    y_low = [jnp.where(even_y, line_outer[v], line_inner[v]) for v in range(nvars)]
-    y_high = [jnp.where(even_y, line_inner[v], line_outer[v]) for v in range(nvars)]
+    y_low, y_high = zip(*(sides_of("gy", line_inner[v], line_outer[v]) for v in range(nvars)))
     from_low, from_high = mixed_by(table, 1, 0, y_low), mixed_by(table, 1, 1, y_high)
     row_at = iota((size_y, size_z), 0)
     faces = {}
-    for fetch in fetches:
-        fetch.wait()
+    for x in range(size_x):
+        fetch(x).wait()
     for x in range(size_x):
         at = slice(x * size_y, (x + 1) * size_y)
         landed = hits[at, :]
@@ -333,9 +338,7 @@
 def second_kernel(table, state, weights, q_now, q_prev, jac, target, hits, x_inner, x_outer, y_inner, y_outer, line_inner, line_outer, out, planes, sides, edge, buffer, sems, *, size):
     nvars, size_x, size_y, size_z = size
     last = size_x - 1
-    even_x, even_y = lax.axis_index("gx") % 2 == 0, lax.axis_index("gy") % 2 == 0
-    x_low = [jnp.where(even_x, x_outer[k], x_inner[k]) for k in range(2 * nvars + 2)]
-    x_high = [jnp.where(even_x, x_inner[k], x_outer[k]) for k in range(2 * nvars + 2)]
+    x_low, x_high = zip(*(sides_of("gx", x_inner[k], x_outer[k]) for k in range(2 * nvars + 2)))
     own_low = mixed_by(table, 0, 0, x_low[nvars : 2 * nvars])
     own_high = mixed_by(table, 0, 1, x_high[nvars : 2 * nvars])
     ring_low = mixed_by(table, 0, 1, [q_now[v, 0] for v in range(nvars)])
@@ -348,14 +351,13 @@
         around[1].append(x_high[v] + step_tau * x_high[2 * nvars] * ring_high[v])
     row_at = iota((size_x, size_z), 0)
     for side in range(2):
-        pick = (y_outer, y_inner, line_outer, line_inner) if side == 0 else (y_inner, y_outer, line_inner, line_outer)
-        scale = step_tau * jnp.where(even_y, pick[2][nvars], pick[3][nvars])
+        scale = step_tau * sides_of("gy", line_inner[nvars], line_outer[nvars])[side]
         corner = slice(side * nvars, (side + 1) * nvars)
         low = mixed_by(table, 0, 0, [x_low[2 * nvars + 1][k : k + 1] for k in range(corner.start, corner.stop)])
         high = mixed_by(table, 0, 1, [x_high[2 * nvars + 1][k : k + 1] for k in range(corner.start, corner.stop)])
         for v in range(nvars):
             change = jnp.where(row_at == 0, low[v], 0.0) - jnp.where(row_at == last, high[v], 0.0)
-            around[2 + side].append(jnp.where(even_y, pick[0][v], pick[1][v]) + scale * change)
+            around[2 + side].append(sides_of("gy", y_inner[v], y_outer[v])[side] + scale * change)
 
     def at_plane(v, x):
         return edge[0, v] if x == 0 else edge[1, v] if x == last else state[v, x]
@@ -377,16 +379,28 @@
         copy.wait()
 
 
-def swap_pairs(axis, odd):
-    count = lax.axis_size(axis)
-    pairs = []
-    for i in range(odd, count - 1, 2):
-        pairs += [(i, i + 1), (i + 1, i)]
-    return pairs
-
-
 def swapped(inner, outer, axis):
-    return lax.ppermute(inner, axis, swap_pairs(axis, 0)), lax.ppermute(outer, axis, swap_pairs(axis, 1))
+    count_x, count_y = lax.axis_size("gx"), lax.axis_size("gy")
+    inner_pairs, outer_pairs = [], []
+    for i in range(count_x):
+        for j in range(count_y):
+            at, count = (i, count_x) if axis == "gx" else (j, count_y)
+            for pairs, to in ((inner_pairs, at ^ 1), (outer_pairs, ((at + 1) ^ 1) - 1)):
+                x, y = (to, j) if axis == "gx" else (i, to)
+                if axis == "gx" and not 0 <= to < count:
+                    x = count - 1 - at
+                if axis == "gy" and not 0 <= to < count:
+                    x, y = i ^ 1, j
+                pairs.append((i * count_y + j, x * count_y + y))
+    return lax.ppermute(inner, AXES, inner_pairs), lax.ppermute(outer, AXES, outer_pairs)
+
+
+def sides_of(axis, inner, outer):
+    here, last = lax.axis_index(axis), lax.axis_size(axis) - 1
+    even = here % 2 == 0
+    inside = (here > 0) & (here < last)
+    masked = jnp.where(inside, outer, 0.0)
+    return jnp.where(even, masked, inner), jnp.where(even, inner, masked)
 
 
 def params(limit):
@@ -435,7 +449,7 @@
             pltpu.VMEM((3, rows), f32),
             pltpu.VMEM((1, rows), jnp.int32),
             pltpu.VMEM((1, rows), jnp.int32),
-            pltpu.SemaphoreType.DMA((7,)),
+            pltpu.SemaphoreType.DMA((5 + 2 * nvars,)),
         ],
         compiler_params=params(DONOR_LIMIT),
         name="donor",
@@ -453,13 +467,13 @@
     lines = swapped(*lines, "gy")
     base, weights, table = pl.pallas_call(
         functools.partial(early_kernel, size=size),
-        out_shape=[pltpu.HBM(size, f32), shape(weights_shape, bf16), shape((4 * nvars * nvars, size_z), f32)],
+        out_shape=[pltpu.HBM(size, f32), pltpu.HBM(weights_shape, bf16), shape((4 * nvars * nvars, size_z), f32)],
         in_specs=[hbm] + [vmem] * 3,
-        out_specs=[hbm, vmem, vmem],
-        scratch_shapes=[planes, pltpu.SMEM((6 * nvars * nvars,), f32), pltpu.VMEM(size, f32), pltpu.SemaphoreType.DMA((5,))],
+        out_specs=[hbm, hbm, vmem],
+        scratch_shapes=[planes, pltpu.SMEM((6 * nvars * nvars,), f32), pltpu.VMEM(size, f32), pltpu.VMEM(weights_shape, bf16), pltpu.SemaphoreType.DMA((6,))],
         compiler_params=params(20 * MIB),
         name="early",
-    )(there(coef), q_now, q_prev, jacobian)
+    )(coef, q_now, q_prev, jacobian)
     state, hits, *faces, later, hot_xy, hot_z = pl.pallas_call(
         functools.partial(first_kernel, size=size, devices=devices, capacity=capacity),
         out_shape=[
@@ -479,7 +493,7 @@
             pltpu.VMEM((CHANNELS, slots), f32),
             pltpu.VMEM((nvars, columns, size_z), f32),
             pltpu.VMEM(size, f32),
-            pltpu.SemaphoreType.DMA((4,)),
+            pltpu.SemaphoreType.DMA((size_x,)),
         ],
         compiler_params=params(20 * MIB),
         name="first",

time: 44.6 us -> 39 us (0.87)
  the two profiles are of different devices: /device:TPU:9 before, /device:TPU:0 now
where the time goes in v6:
time: 39 us; the launch traced here: 38.8 us
  Pallas kernels  21.5 us (55%)
  starting transfers between devices  12.8 us (33%)
  waiting for transfers between devices  3.33 us (9%)
  between operations  0.93 us (2%)
    pallas_call x1, Pallas kernels, body(): pl.pallas_call(functools.partial(donor_kernel, size=size, devices=devices...  7.85 us
    all_to_all x1, starting transfers between devices, body(): got = lax.all_to_all(sent, AXES, split_axis=0, concat_axis=0, tiled=True)  7.5 us
    pallas_call x1, Pallas kernels, body(): pl.pallas_call(functools.partial(first_kernel, size=size, devices=devices...  4.44 us
    ppermute x3, starting transfers between devices, swapped(): lax.ppermute(inner, AXES, inner_pairs)  4.33 us
    pallas_call x1, Pallas kernels, body(): pl.pallas_call(functools.partial(early_kernel, size=size), out_shape=[plt...  3.31 us
    pallas_call x1, Pallas kernels, body(): pl.pallas_call(functools.partial(second_kernel, size=size), out_shape=sha...  3.04 us
    pallas_call x1, Pallas kernels, body(): pl.pallas_call(late_kernel, out_shape=shape(flat, f32), in_specs=[vmem] *...  2.89 us
    ppermute x3, waiting for transfers between devices, swapped(): lax.ppermute(inner, AXES, inner_pairs)  2.77 us
  transfers between devices with their start and end apart: 7, of which 3 were waited for; matrix products, arithmetic and copies ran while one was open for 0% of the time, Pallas kernels for 16%

profile of v6, /device:TPU:0, one launch (start us, length us, event | category | flops | bytes accessed | tf_op | source)
XLA Modules:
  0.0 38.8 jit_solution(17370935589817095232)
XLA Ops:
  0.7 0.0 copy-start.4
  0.7 0.0 copy-start
  0.7 0.0 copy-start.1
  0.7 0.0 copy-start.2
  0.7 7.9 %donor.1 = (f32[32,8,128]{2,1,0:T(8,128)}, f32[6,16,256]{2,1,0:T(8,128)S(1)}, f32[6,16,256]{2,1,0:T(8,128)S(1)}) custom-call(s32[1]{0:T(128)S(6)} %copy.11.count, f32[5,256,256]{2,1,0:T(8,128)} %bitcast.7, f32[5,256,256]{2,1,0:T(8,128)} %bitcast.6, s32[1,1024]{1,0:T(1,128)} %bitcast.9, f32[3,1024]{1,0:T(4,128)} %frac_in.1, s32[1,1024]{1,0:T(1,128)} %bitcast.10, ...), custom_call_target="tpu_custom_call" | custom-call | tf_op jit(solution)/shard_map/donor/pallas_call | solution.py:435
  8.6 7.5 %all-to-all-start = ((f32[32,8,128]{2,1,0:T(8,128)}), f32[32,8,128]{2,1,0:T(8,128)S(1)}, u32[]{:S(2)}, u32[]{:S(2)}) async-start(f32[32,8,128]{2,1,0:T(8,128)} %get-tuple-element.21), calls=%async_computation | async-start | bytes 262144 | tf_op jit(solution)/shard_map/all_to_all | solution.py:466
  16.1 1.7 %collective-permute-start = (f32[6,16,256]{2,1,0:T(8,128)S(1)}, f32[6,16,256]{2,1,0:T(8,128)S(1)}, u32[]{:S(2)}, u32[]{:S(2)}) collective-permute-start(f32[6,16,256]{2,1,0:T(8,128)S(1)} %get-tuple-element.23), channel_id=1, source_target_pairs={{0,1},{1,0},{2,3},{3,2},{4,5},{5,4},{6,7},{7,6},{8,9},{9,8},{10,11... | collective-permute-start | bytes 294920 | tf_op jit(solution)/shard_map/ppermute | solution.py:395
  17.7 0.0 collective-permute-start.1
  17.7 0.0 copy-done.4
  17.7 0.1 reshape.21.coef_in
  17.8 0.0 copy-done
  17.8 0.0 copy-done.1
  17.9 0.0 copy-done.2
  17.9 3.3 %early.1 = (f32[5,16,16,256]{3,2,1,0:T(8,128)}, bf16[2,240,256]{2,1,0:T(8,128)(2,1)}, f32[100,256]{1,0:T(8,128)S(1)}) custom-call(f32[150]{0:T(256)S(1)} %reshape.21.coef_in, f32[5,16,16,256]{3,2,1,0:T(8,128)S(1)} %copy-done, f32[5,16,16,256]{3,2,1,0:T(8,128)S(1)} %copy-done.1, f32[16,16,256]{2,1,0:T(8,128)S(1)} %copy-done.2), custom_call_target="tpu_custom_call" | custom-call | tf_op jit(solution)/shard_map/early/pallas_call | solution.py:468
  21.2 2.0 %collective-permute-done.line_inner = f32[6,16,256]{2,1,0:T(8,128)S(1)} collective-permute-done((f32[6,16,256]{2,1,0:T(8,128)S(1)}, f32[6,16,256]{2,1,0:T(8,128)S(1)}, u32[]{:S(2)}, u32[]{:S(2)}) %collective-permute-start) | collective-permute-done | bytes 98336 | tf_op jit(solution)/shard_map/ppermute | solution.py:395
  23.1 0.0 collective-permute-done.1.line_outer
  23.1 0.5 %all-to-all-done.got = f32[32,8,128]{2,1,0:T(8,128)S(1)} async-done(((f32[32,8,128]{2,1,0:T(8,128)}), f32[32,8,128]{2,1,0:T(8,128)S(1)}, u32[]{:S(2)}, u32[]{:S(2)}) %all-to-all-start) | async-done | bytes 131104 | tf_op jit(solution)/shard_map/all_to_all | solution.py:466
  23.7 4.4 %first.1 = (f32[5,16,16,256]{3,2,1,0:T(8,128)S(1)}, f32[256,256]{1,0:T(8,128)S(1)}, f32[12,16,256]{2,1,0:T(8,128)S(1)}, f32[12,16,256]{2,1,0:T(8,128)S(1)}, f32[...) custom-call(f32[100,256]{1,0:T(8,128)S(1)} %get-tuple-element.20.tab, ...), custom_call_target="tpu_custom_call" | custom-call | tf_op jit(solution)/shard_map/first/pallas_call | solution.py:477
  28.1 0.2 collective-permute-start.2
  28.3 1.0 %collective-permute-start.3 = (f32[12,16,256]{2,1,0:T(8,128)S(1)}, f32[12,16,256]{2,1,0:T(8,128)S(1)}, u32[]{:S(2)}, u32[]{:S(2)}) collective-permute-start(f32[12,16,256]{2,1,0:T(8,128)S(1)} %get-tuple-element.32), channel_id=1, source_target_pairs={{0,24},{1,25},{2,26},{3,27},{4,28},{5,29},{6,30},{7,31},{8,16},{9,... | collective-permute-start | bytes 589832 | tf_op jit(solution)/shard_map/ppermute | solution.py:395
  29.3 2.5 %collective-permute-start.4 = (f32[5,16,256]{2,1,0:T(8,128)S(1)}, f32[5,16,256]{2,1,0:T(8,128)S(1)}, u32[]{:S(2)}, u32[]{:S(2)}) collective-permute-start(f32[5,16,256]{2,1,0:T(8,128)S(1)} %get-tuple-element.33), channel_id=1, source_target_pairs={{0,1},{1,0},{2,3},{3,2},{4,5},{5,4},{6,7},{7,6},{8,9},{9,8},{10,11... | collective-permute-start | bytes 245768 | tf_op jit(solution)/shard_map/ppermute | solution.py:395
  31.8 0.0 collective-permute-start.5
  31.8 0.0 copy-start.3
  31.8 2.9 %late.1.target = f32[5,256,256]{2,1,0:T(8,128)S(1)} custom-call(f32[5,2048]{1,0:T(8,128)S(1)} %get-tuple-element.27.rows, bf16[256,2048]{1,0:T(8,128)(2,1)S(1)} %get-tuple-element.28.hot_xy, bf16[2048,256]{1,0:T(8,128)(2,1)S(1)} %get-tuple-element.29.hot_z), custom_call_target="tpu_custom_call" | custom-call | tf_op jit(solution)/shard_map/late/pallas_call | solution.py:502
  34.7 0.8 %collective-permute-done.4.y_inner = f32[5,16,256]{2,1,0:T(8,128)S(1)} collective-permute-done((f32[5,16,256]{2,1,0:T(8,128)S(1)}, f32[5,16,256]{2,1,0:T(8,128)S(1)}, u32[]{:S(2)}, u32[]{:S(2)}) %collective-permute-start.4) | collective-permute-done | bytes 81952 | tf_op jit(solution)/shard_map/ppermute | solution.py:395
  35.5 0.0 collective-permute-done.5.y_outer
  35.5 0.0 collective-permute-done.2.x_inner
  35.5 0.0 collective-permute-done.3.x_outer
  35.5 0.0 copy-done.3
  35.6 3.0 %second.1 = f32[5,16,16,256]{3,2,1,0:T(8,128)} custom-call(f32[100,256]{1,0:T(8,128)S(1)} %get-tuple-element.20.table, f32[5,16,16,256]{3,2,1,0:T(8,128)S(1)} %get-tuple-element.25.state, bf16[2,240,256]{2,1,0:T(8,128)(2,1)S(1)} %copy-done.3, f32[5,16,16,256]{3,2,1,0:T(8,128)S(1)} %copy-done, f32[5,16,16,256]{3,2,1,0:T(8,128)S(1)} %copy-done.1, ...), custom_call_target="tpu_custom_call" | custom-call | tf_op jit(solution)/shard_map/second/pallas_call | solution.py:510
  (1 shorter events, 0.0 us)
Async XLA Ops:
  0.7 17.1 %copy-start.4 = (f32[3,2,5,5]{3,1,2,0:T(2,128)S(1)}, f32[3,2,5,5]{3,1,2,0:T(2,128)}, u32[]{:S(2)}) copy-start(f32[3,2,5,5]{3,1,2,0:T(2,128)} %param.12) | copy-start | bytes 1804
  0.7 17.2 %copy-start = (f32[5,16,16,256]{3,2,1,0:T(8,128)S(1)}, f32[5,16,16,256]{3,2,1,0:T(8,128)}, u32[]{:S(2)}) copy-start(f32[5,16,16,256]{3,2,1,0:T(8,128)} %q_now.5) | copy-start | bytes 3932164
  0.7 17.2 %copy-start.1 = (f32[5,16,16,256]{3,2,1,0:T(8,128)S(1)}, f32[5,16,16,256]{3,2,1,0:T(8,128)}, u32[]{:S(2)}) copy-start(f32[5,16,16,256]{3,2,1,0:T(8,128)} %q_prev.3) | copy-start | bytes 3932164
  0.7 17.2 %copy-start.2 = (f32[16,16,256]{2,1,0:T(8,128)S(1)}, f32[16,16,256]{2,1,0:T(8,128)}, u32[]{:S(2)}) copy-start(f32[16,16,256]{2,1,0:T(8,128)} %jac.5) | copy-start | bytes 786436
  8.6 15.1 %all-to-all-start = ((f32[32,8,128]{2,1,0:T(8,128)}), f32[32,8,128]{2,1,0:T(8,128)S(1)}, u32[]{:S(2)}, u32[]{:S(2)}) async-start(f32[32,8,128]{2,1,0:T(8,128)} %get-tuple-element.21), calls=%async_computation | async-start | bytes 262144 | tf_op jit(solution)/shard_map/all_to_all | solution.py:466
  16.1 7.1 %collective-permute-start = (f32[6,16,256]{2,1,0:T(8,128)S(1)}, f32[6,16,256]{2,1,0:T(8,128)S(1)}, u32[]{:S(2)}, u32[]{:S(2)}) collective-permute-start(f32[6,16,256]{2,1,0:T(8,128)S(1)} %get-tuple-element.23), channel_id=1, source_target_pairs={{0,1},{1,0},{2,3},{3,2},{4,5},{5,4},{6,7},{7,6},{8,9},{9,8},{10,11... | collective-permute-start | bytes 294920 | tf_op jit(solution)/shard_map/ppermute | solution.py:395
  17.7 5.4 %collective-permute-start.1 = (f32[6,16,256]{2,1,0:T(8,128)S(1)}, f32[6,16,256]{2,1,0:T(8,128)S(1)}, u32[]{:S(2)}, u32[]{:S(2)}) collective-permute-start(f32[6,16,256]{2,1,0:T(8,128)S(1)} %get-tuple-element.24), channel_id=1, source_target_pairs={{0,8},{1,2},{2,1},{3,4},{4,3},{5,6},{6,5},{7,15},{8,0},{9,10},{10,... | collective-permute-start | bytes 294920 | tf_op jit(solution)/shard_map/ppermute | solution.py:395
  28.1 7.4 %collective-permute-start.2 = (f32[12,16,256]{2,1,0:T(8,128)S(1)}, f32[12,16,256]{2,1,0:T(8,128)S(1)}, u32[]{:S(2)}, u32[]{:S(2)}) collective-permute-start(f32[12,16,256]{2,1,0:T(8,128)S(1)} %get-tuple-element.31), channel_id=1, source_target_pairs={{0,8},{1,9},{2,10},{3,11},{4,12},{5,13},{6,14},{7,15},{8,0},{9,1},... | collective-permute-start | bytes 589832 | tf_op jit(solution)/shard_map/ppermute | solution.py:395
  28.3 7.2 %collective-permute-start.3 = (f32[12,16,256]{2,1,0:T(8,128)S(1)}, f32[12,16,256]{2,1,0:T(8,128)S(1)}, u32[]{:S(2)}, u32[]{:S(2)}) collective-permute-start(f32[12,16,256]{2,1,0:T(8,128)S(1)} %get-tuple-element.32), channel_id=1, source_target_pairs={{0,24},{1,25},{2,26},{3,27},{4,28},{5,29},{6,30},{7,31},{8,16},{9,... | collective-permute-start | bytes 589832 | tf_op jit(solution)/shard_map/ppermute | solution.py:395
  29.3 6.2 %collective-permute-start.4 = (f32[5,16,256]{2,1,0:T(8,128)S(1)}, f32[5,16,256]{2,1,0:T(8,128)S(1)}, u32[]{:S(2)}, u32[]{:S(2)}) collective-permute-start(f32[5,16,256]{2,1,0:T(8,128)S(1)} %get-tuple-element.33), channel_id=1, source_target_pairs={{0,1},{1,0},{2,3},{3,2},{4,5},{5,4},{6,7},{7,6},{8,9},{9,8},{10,11... | collective-permute-start | bytes 245768 | tf_op jit(solution)/shard_map/ppermute | solution.py:395
  31.8 3.7 %collective-permute-start.5 = (f32[5,16,256]{2,1,0:T(8,128)S(1)}, f32[5,16,256]{2,1,0:T(8,128)S(1)}, u32[]{:S(2)}, u32[]{:S(2)}) collective-permute-start(f32[5,16,256]{2,1,0:T(8,128)S(1)} %get-tuple-element.34), channel_id=1, source_target_pairs={{0,8},{1,2},{2,1},{3,4},{4,3},{5,6},{6,5},{7,15},{8,0},{9,10},{10,... | collective-permute-start | bytes 245768 | tf_op jit(solution)/shard_map/ppermute | solution.py:395
  31.8 3.7 %copy-start.3 = (bf16[2,240,256]{2,1,0:T(8,128)(2,1)S(1)}, bf16[2,240,256]{2,1,0:T(8,128)(2,1)}, u32[]{:S(2)}) copy-start(bf16[2,240,256]{2,1,0:T(8,128)(2,1)} %get-tuple-element.26.weights) | copy-start | bytes 737284

commit v7 on v6

--- a/solution.py
+++ b/solution.py
@@ -17,6 +17,7 @@
 CHANNELS = 16
 MIB = 1 << 20
 DONOR_LIMIT = 44 * MIB
+PIECES = 8
 
 
 def iota(shape, dim):
@@ -49,15 +50,15 @@
     return jnp.concatenate(pieces, axis=1)
 
 
-def donor_kernel(count, q_prev, q_now, base_in, frac_in, dest_in, cell_in, jac_in, out, y_inner, y_outer, planes, jac, lhs, spread, corner, place, values, base, frac, dest, cell, sems, *, size, devices, capacity):
+def donor_kernel(count, q_prev, q_now, base_in, frac_in, dest_in, cell_in, out_there, y_inner, y_outer, out, planes, lhs, spread, corner, place, values, base, frac, dest, cell, sems, *, size, devices, capacity):
     nvars, size_x, size_y, size_z = size
     columns = size_x * size_y
     rows = base.shape[1]
-    small = [pltpu.make_async_copy(a, b, sems.at[k]) for k, (a, b) in enumerate(((base_in, base), (frac_in, frac), (dest_in, dest), (cell_in, cell), (jac_in, jac)))]
+    small = [pltpu.make_async_copy(a, b, sems.at[k]) for k, (a, b) in enumerate(((base_in, base), (frac_in, frac), (dest_in, dest), (cell_in, cell)))]
     copies = [pltpu.make_async_copy(ref.at[v], planes.at[k, v], sems.at[5 + k * nvars + v]) for k, ref in enumerate((q_prev, q_now)) for v in range(nvars)]
     for copy in small + copies:
         copy.start()
-    for copy in small[0:4]:
+    for copy in small:
         copy.wait()
     start = base[...].astype(jnp.float32)
     in_y = jnp.floor((start + 0.5) * (1.0 / (size_z - 1)))
@@ -91,11 +92,10 @@
         if k == 1:
             for v in range(nvars):
                 copies[nvars + v].wait()
-            small[4].wait()
             even = lax.axis_index("gy") % 2 == 0
-            for v in range(nvars + 1):
+            for v in range(nvars):
                 for x in range(size_x):
-                    line = planes.at[1, v] if v < nvars else jac
+                    line = planes.at[1, v]
                     low = line[x * size_y : x * size_y + 1, :]
                     high = line[(x + 1) * size_y - 1 : (x + 1) * size_y, :]
                     y_inner[v, x : x + 1, :] = jnp.where(even, high, low)
@@ -123,6 +123,7 @@
     middle = rest.astype(jnp.bfloat16)
     last = (rest - middle.astype(jnp.float32)).astype(jnp.bfloat16)
     three = jnp.concatenate([high, middle, last], axis=0)
+    leaving = []
     column = jnp.broadcast_to(place[:, 0:1], (rows, LANES))
     for n in range(devices * capacity // LANES):
         chosen = (column == (iota((rows, LANES), 1) + n * LANES).astype(jnp.float32)).astype(jnp.float32).astype(jnp.bfloat16)
@@ -132,6 +133,11 @@
             piece = moved[:, d * capacity : (d + 1) * capacity]
             to = n * (LANES // capacity) + d
             out[to] = jnp.concatenate([piece[0:8], piece[8:16]], axis=1)
+        some = pl.ds(n * (LANES // capacity), LANES // capacity)
+        leaving.append(pltpu.make_async_copy(out.at[some], out_there.at[some], sems.at[n]))
+        leaving[-1].start()
+    for copy in leaving:
+        copy.wait()
 
 
 def mixing_weights(coef, high, low, size):
@@ -206,7 +212,7 @@
 
 
 def sent_out(x, size_x, buffer, out, sems, copies):
-    part = size_x // 4
+    part = size_x // PIECES
     if (x + 1) % part == 0:
         some = pl.ds(x + 1 - part, part)
         copies.append(pltpu.make_async_copy(buffer.at[:, some], out.at[:, some], sems.at[x // part]))
@@ -215,14 +221,14 @@
 
 def early_kernel(coef_in, q_now, q_prev, jac, base, weights_out, table, planes, coef, buffer, weights, sems, *, size):
     nvars, size_x, _, size_z = size
-    fetch = pltpu.make_async_copy(coef_in, coef, sems.at[4])
+    fetch = pltpu.make_async_copy(coef_in, coef, sems.at[PIECES])
     fetch.start()
     fill_planes(lambda v, x: q_now[v, x], None, planes, None, size)
     fetch.wait()
     for k in range(table.shape[0]):
         table[k : k + 1, :] = jnp.full((1, size_z), coef[k], jnp.float32)
     mixing_weights(coef, weights.at[0], weights.at[1], size)
-    copies = [pltpu.make_async_copy(weights, weights_out, sems.at[5])]
+    copies = [pltpu.make_async_copy(weights, weights_out, sems.at[PIECES + 1])]
     copies[0].start()
     for x in range(size_x):
         flux = flux_at(x, weights, planes, None, size)
@@ -287,16 +293,17 @@
     hot_xy[...] = ((iota((columns, slots), 0) + 1).astype(jnp.float32) == land_xy).astype(jnp.float32).astype(jnp.bfloat16)
     later[...] = rows[nvars : 2 * nvars, :]
 
-    def keep(c, value):
-        grid[c] = value
-
     hits[...] = dot(hot_xy[...], hot_z[...], ((1,), (0,)))
-    land(rows, hot_xy, hot_z, keep, nvars)
     even_x, even_y = lax.axis_index("gx") % 2 == 0, lax.axis_index("gy") % 2 == 0
     y_low, y_high = zip(*(sides_of("gy", line_inner[v], line_outer[v]) for v in range(nvars)))
     from_low, from_high = mixed_by(table, 1, 0, y_low), mixed_by(table, 1, 1, y_high)
     row_at = iota((size_y, size_z), 0)
     faces = {}
+
+    def keep(c, value):
+        grid[c] = value
+
+    land(rows, hot_xy, hot_z, keep, nvars)
     for x in range(size_x):
         fetch(x).wait()
     for x in range(size_x):
@@ -310,10 +317,16 @@
             new = base[v, x] - scale * change
             state[v, x] = new
             low, high = new[0:1], new[size_y - 1 : size_y]
-            y_inner[v, x : x + 1, :] = jnp.where(even_y, high, low)
-            y_outer[v, x : x + 1, :] = jnp.where(even_y, low, high)
+            y_inner[v * size_x + x : v * size_x + x + 1, :] = jnp.where(even_y, high, low)
+            y_outer[v * size_x + x : v * size_x + x + 1, :] = jnp.where(even_y, low, high)
             if x in (0, size_x - 1):
                 faces[x, v] = new
+    tail = nvars * size_x
+    y_inner[tail:, :] = y_outer[tail:, :] = jnp.zeros((8, size_z), jnp.float32)
+    for k, x in enumerate((0, size_x - 1)):
+        low, high = jac[x][0:1], jac[x][size_y - 1 : size_y]
+        y_inner[tail + k : tail + k + 1, :] = jnp.where(even_y, high, low)
+        y_outer[tail + k : tail + k + 1, :] = jnp.where(even_y, low, high)
     ends = [y_low[v] for v in range(nvars)] + [y_high[v] for v in range(nvars)]
     for v in range(nvars):
         for k, pair in enumerate(((faces[0, v], faces[size_x - 1, v]), (q_now[v, 0], q_now[v, size_x - 1]))):
@@ -335,7 +348,7 @@
     land(rows, hot_xy, hot_z, keep, rows.shape[0])
 
 
-def second_kernel(table, state, weights, q_now, q_prev, jac, target, hits, x_inner, x_outer, y_inner, y_outer, line_inner, line_outer, out, planes, sides, edge, buffer, sems, *, size):
+def second_kernel(table, state, weights, q_now, q_prev, jac, target, hits, x_inner, x_outer, y_inner, y_outer, out, planes, sides, edge, buffer, sems, *, size):
     nvars, size_x, size_y, size_z = size
     last = size_x - 1
     x_low, x_high = zip(*(sides_of("gx", x_inner[k], x_outer[k]) for k in range(2 * nvars + 2)))
@@ -350,14 +363,16 @@
         around[0].append(x_low[v] - step_tau * x_low[2 * nvars] * ring_low[v])
         around[1].append(x_high[v] + step_tau * x_high[2 * nvars] * ring_high[v])
     row_at = iota((size_x, size_z), 0)
+    tail = nvars * size_x
     for side in range(2):
-        scale = step_tau * sides_of("gy", line_inner[nvars], line_outer[nvars])[side]
-        corner = slice(side * nvars, (side + 1) * nvars)
-        low = mixed_by(table, 0, 0, [x_low[2 * nvars + 1][k : k + 1] for k in range(corner.start, corner.stop)])
-        high = mixed_by(table, 0, 1, [x_high[2 * nvars + 1][k : k + 1] for k in range(corner.start, corner.stop)])
-        for v in range(nvars):
-            change = jnp.where(row_at == 0, low[v], 0.0) - jnp.where(row_at == last, high[v], 0.0)
-            around[2 + side].append(sides_of("gy", y_inner[v], y_outer[v])[side] + scale * change)
+        scale = sides_of("gy", y_inner[tail:, :], y_outer[tail:, :])[side]
+        corner = range(side * nvars, (side + 1) * nvars)
+        low = mixed_by(table, 0, 0, [x_low[2 * nvars + 1][k : k + 1] for k in corner])
+        high = mixed_by(table, 0, 1, [x_high[2 * nvars + 1][k : k + 1] for k in corner])
+        for v in range(nvars):
+            change = jnp.where(row_at == 0, scale[0:1] * low[v], 0.0) - jnp.where(row_at == last, scale[1:2] * high[v], 0.0)
+            face = slice(v * size_x, (v + 1) * size_x)
+            around[2 + side].append(sides_of("gy", y_inner[face, :], y_outer[face, :])[side] + step_tau * change)
 
     def at_plane(v, x):
         return edge[0, v] if x == 0 else edge[1, v] if x == last else state[v, x]
@@ -388,7 +403,7 @@
             for pairs, to in ((inner_pairs, at ^ 1), (outer_pairs, ((at + 1) ^ 1) - 1)):
                 x, y = (to, j) if axis == "gx" else (i, to)
                 if axis == "gx" and not 0 <= to < count:
-                    x = count - 1 - at
+                    x, y = i, j ^ 2
                 if axis == "gy" and not 0 <= to < count:
                     x, y = i ^ 1, j
                 pairs.append((i * count_y + j, x * count_y + y))
@@ -424,9 +439,9 @@
     weights_shape = (2, 3 * block, 3 * block + CHANNELS)
     planes = pltpu.VMEM((2, (size_x + 2) * block, size_z), bf16)
     sides = pltpu.VMEM((size_x, CHANNELS, size_z), f32)
-    face_y = shape((nvars, size_x, size_z), f32)
-
-    line, line_x = pltpu.VMEM((nvars + 1, size_x, size_z), f32), shape((2 * nvars + 2, size_y, size_z), f32)
+    face_y = shape((nvars * size_x + 8, size_z), f32)
+
+    line, line_x = pltpu.VMEM((nvars, size_x, size_z), f32), shape((2 * nvars + 2, size_y, size_z), f32)
     coef = flux_split.reshape(-1)
 
     def there(x):
@@ -434,12 +449,12 @@
 
     sent, *lines = pl.pallas_call(
         functools.partial(donor_kernel, size=size, devices=devices, capacity=capacity),
-        out_shape=[pltpu.VMEM((devices, 8, 2 * capacity), f32), line, line],
-        in_specs=[pl.BlockSpec(memory_space=pltpu.SMEM)] + [hbm] * 7,
-        out_specs=[vmem] * 3,
+        out_shape=[pltpu.HBM((devices, 8, 2 * capacity), f32), line, line],
+        in_specs=[pl.BlockSpec(memory_space=pltpu.SMEM)] + [hbm] * 6,
+        out_specs=[hbm, vmem, vmem],
         scratch_shapes=[
+            pltpu.VMEM((devices, 8, 2 * capacity), f32),
             pltpu.VMEM((2, nvars, columns, size_z), f32),
-            pltpu.VMEM((columns, size_z), f32),
             pltpu.VMEM((2, 2 * nvars * columns, size_z), bf16),
             pltpu.VMEM((2, size_z, rows), bf16),
             pltpu.VMEM((columns, rows), f32),
@@ -461,7 +476,6 @@
         there(donor_frac),
         there(fringe_dest.reshape(1, rows)),
         there(receptor_cell.reshape(1, rows)),
-        there(jacobian.reshape(columns, size_z)),
     )
     got = lax.all_to_all(sent, AXES, split_axis=0, concat_axis=0, tiled=True)
     lines = swapped(*lines, "gy")
@@ -470,7 +484,7 @@
         out_shape=[pltpu.HBM(size, f32), pltpu.HBM(weights_shape, bf16), shape((4 * nvars * nvars, size_z), f32)],
         in_specs=[hbm] + [vmem] * 3,
         out_specs=[hbm, hbm, vmem],
-        scratch_shapes=[planes, pltpu.SMEM((6 * nvars * nvars,), f32), pltpu.VMEM(size, f32), pltpu.VMEM(weights_shape, bf16), pltpu.SemaphoreType.DMA((6,))],
+        scratch_shapes=[planes, pltpu.SMEM((6 * nvars * nvars,), f32), pltpu.VMEM(size, f32), pltpu.VMEM(weights_shape, bf16), pltpu.SemaphoreType.DMA((PIECES + 2,))],
         compiler_params=params(20 * MIB),
         name="early",
     )(coef, q_now, q_prev, jacobian)
@@ -510,12 +524,12 @@
     return pl.pallas_call(
         functools.partial(second_kernel, size=size),
         out_shape=shape(size, f32),
-        in_specs=[vmem] * 14,
+        in_specs=[vmem] * 12,
         out_specs=hbm,
-        scratch_shapes=[planes, sides, pltpu.VMEM((2, nvars, size_y, size_z), f32), pltpu.VMEM(size, f32), pltpu.SemaphoreType.DMA((4,))],
+        scratch_shapes=[planes, sides, pltpu.VMEM((2, nvars, size_y, size_z), f32), pltpu.VMEM(size, f32), pltpu.SemaphoreType.DMA((PIECES,))],
         compiler_params=params(20 * MIB),
         name="second",
-    )(table, state, weights, q_now, q_prev, jacobian, target, hits, *around, *lines)
+    )(table, state, weights, q_now, q_prev, jacobian, target, hits, *around)
 
 
 def solution(mesh):

time: 39 us -> 38 us (0.974)
  the two profiles are of different devices: /device:TPU:0 before, /device:TPU:9 now
where the time goes in v7:
time: 38 us; the launch traced here: 37.8 us
  Pallas kernels  21.3 us (56%)
  starting transfers between devices  10.7 us (28%)
  waiting for transfers between devices  4.67 us (12%)
  between operations  0.92 us (2%)
    pallas_call x1, Pallas kernels, body(): pl.pallas_call(functools.partial(donor_kernel, size=size, devices=devices...  7.77 us
    all_to_all x1, starting transfers between devices, body(): got = lax.all_to_all(sent, AXES, split_axis=0, concat_axis=0, tiled=True)  6.34 us
    pallas_call x1, Pallas kernels, body(): pl.pallas_call(functools.partial(first_kernel, size=size, devices=devices...  4.59 us
    pallas_call x1, Pallas kernels, body(): pl.pallas_call(functools.partial(early_kernel, size=size), out_shape=[plt...  3.29 us
    ppermute x3, starting transfers between devices, swapped(): lax.ppermute(inner, AXES, inner_pairs)  2.93 us
    ppermute x3, waiting for transfers between devices, swapped(): lax.ppermute(inner, AXES, inner_pairs)  2.88 us
    pallas_call x1, Pallas kernels, body(): pl.pallas_call(late_kernel, out_shape=shape(flat, f32), in_specs=[vmem] *...  2.87 us
    pallas_call x1, Pallas kernels, body(): pl.pallas_call(functools.partial(second_kernel, size=size), out_shape=sha...  2.81 us
  transfers between devices with their start and end apart: 7, of which 3 were waited for; matrix products, arithmetic and copies ran while one was open for 0% of the time, Pallas kernels for 16%

profile of v7, /device:TPU:9, one launch (start us, length us, event | category | flops | bytes accessed | tf_op | source)
XLA Modules:
  0.0 37.8 jit_solution(8892867176562200451)
XLA Ops:
  0.7 0.0 copy-start.4
  0.7 0.0 copy-start
  0.7 0.0 copy-start.1
  0.7 0.0 copy-start.2
  0.7 7.8 %donor.1 = (f32[32,8,128]{2,1,0:T(8,128)}, f32[5,16,256]{2,1,0:T(8,128)S(1)}, f32[5,16,256]{2,1,0:T(8,128)S(1)}) custom-call(s32[1]{0:T(128)S(6)} %copy.11.count, f32[5,256,256]{2,1,0:T(8,128)} %bitcast.6, f32[5,256,256]{2,1,0:T(8,128)} %bitcast.5, s32[1,1024]{1,0:T(1,128)} %bitcast.7, f32[3,1024]{1,0:T(4,128)} %frac_in.1, s32[1,1024]{1,0:T(1,128)} %bitcast.8, ...), custom_call_target="tpu_custom_call" | custom-call | tf_op jit(solution)/shard_map/donor/pallas_call | solution.py:450
  8.5 6.3 %all-to-all-start = ((f32[32,8,128]{2,1,0:T(8,128)}), f32[32,8,128]{2,1,0:T(8,128)S(1)}, u32[]{:S(2)}, u32[]{:S(2)}) async-start(f32[32,8,128]{2,1,0:T(8,128)} %get-tuple-element.21), calls=%async_computation | async-start | bytes 262144 | tf_op jit(solution)/shard_map/all_to_all | solution.py:480
  14.8 1.2 %collective-permute-start = (f32[5,16,256]{2,1,0:T(8,128)S(1)}, f32[5,16,256]{2,1,0:T(8,128)S(1)}, u32[]{:S(2)}, u32[]{:S(2)}) collective-permute-start(f32[5,16,256]{2,1,0:T(8,128)S(1)} %get-tuple-element.23), channel_id=1, source_target_pairs={{0,1},{1,0},{2,3},{3,2},{4,5},{5,4},{6,7},{7,6},{8,9},{9,8},{10,11... | collective-permute-start | bytes 245768 | tf_op jit(solution)/shard_map/ppermute | solution.py:410
  16.1 0.1 collective-permute-start.1
  16.2 0.0 copy-done.4
  16.2 0.1 reshape.18.coef_in
  16.3 0.0 copy-done
  16.3 0.0 copy-done.1
  16.3 0.0 copy-done.2
  16.3 3.3 %early.1 = (f32[5,16,16,256]{3,2,1,0:T(8,128)}, bf16[2,240,256]{2,1,0:T(8,128)(2,1)}, f32[100,256]{1,0:T(8,128)S(1)}) custom-call(f32[150]{0:T(256)S(1)} %reshape.18.coef_in, f32[5,16,16,256]{3,2,1,0:T(8,128)S(1)} %copy-done, f32[5,16,16,256]{3,2,1,0:T(8,128)S(1)} %copy-done.1, f32[16,16,256]{2,1,0:T(8,128)S(1)} %copy-done.2), custom_call_target="tpu_custom_call" | custom-call | tf_op jit(solution)/shard_map/early/pallas_call | solution.py:482
  19.6 2.2 %collective-permute-done.line_inner = f32[5,16,256]{2,1,0:T(8,128)S(1)} collective-permute-done((f32[5,16,256]{2,1,0:T(8,128)S(1)}, f32[5,16,256]{2,1,0:T(8,128)S(1)}, u32[]{:S(2)}, u32[]{:S(2)}) %collective-permute-start) | collective-permute-done | bytes 81952 | tf_op jit(solution)/shard_map/ppermute | solution.py:410
  21.8 0.0 collective-permute-done.1.line_outer
  21.8 0.0 all-to-all-done.got
  21.8 4.6 %first.1 = (f32[5,16,16,256]{3,2,1,0:T(8,128)S(1)}, f32[256,256]{1,0:T(8,128)S(1)}, f32[12,16,256]{2,1,0:T(8,128)S(1)}, f32[12,16,256]{2,1,0:T(8,128)S(1)}, f32[...) custom-call(f32[100,256]{1,0:T(8,128)S(1)} %get-tuple-element.20.tab, ...), custom_call_target="tpu_custom_call" | custom-call | tf_op jit(solution)/shard_map/first/pallas_call | solution.py:491
  26.4 0.9 %collective-permute-start.2 = (f32[12,16,256]{2,1,0:T(8,128)S(1)}, f32[12,16,256]{2,1,0:T(8,128)S(1)}, u32[]{:S(2)}, u32[]{:S(2)}) collective-permute-start(f32[12,16,256]{2,1,0:T(8,128)S(1)} %get-tuple-element.31), channel_id=1, source_target_pairs={{0,8},{1,9},{2,10},{3,11},{4,12},{5,13},{6,14},{7,15},{8,0},{9,1},... | collective-permute-start | bytes 589832 | tf_op jit(solution)/shard_map/ppermute | solution.py:410
  27.3 1.1 %collective-permute-start.3 = (f32[12,16,256]{2,1,0:T(8,128)S(1)}, f32[12,16,256]{2,1,0:T(8,128)S(1)}, u32[]{:S(2)}, u32[]{:S(2)}) collective-permute-start(f32[12,16,256]{2,1,0:T(8,128)S(1)} %get-tuple-element.32), channel_id=1, source_target_pairs={{0,2},{1,3},{2,0},{3,1},{4,6},{5,7},{6,4},{7,5},{8,16},{9,17},{10,... | collective-permute-start | bytes 589832 | tf_op jit(solution)/shard_map/ppermute | solution.py:410
  28.5 0.8 %collective-permute-start.4 = (f32[88,256]{1,0:T(8,128)S(1)}, f32[88,256]{1,0:T(8,128)S(1)}, u32[]{:S(2)}, u32[]{:S(2)}) collective-permute-start(f32[88,256]{1,0:T(8,128)S(1)} %get-tuple-element.33), channel_id=1, source_target_pairs={{0,1},{1,0},{2,3},{3,2},{4,5},{5,4},{6,7},{7,6},{8,9},{9,8},{10,11... | collective-permute-start | bytes 270344 | tf_op jit(solution)/shard_map/ppermute | solution.py:410
  29.3 0.2 collective-permute-start.5
  29.5 0.0 copy-start.3
  29.5 2.9 %late.1.target = f32[5,256,256]{2,1,0:T(8,128)S(1)} custom-call(f32[5,2048]{1,0:T(8,128)S(1)} %get-tuple-element.27.rows, bf16[256,2048]{1,0:T(8,128)(2,1)S(1)} %get-tuple-element.28.hot_xy, bf16[2048,256]{1,0:T(8,128)(2,1)S(1)} %get-tuple-element.29.hot_z), custom_call_target="tpu_custom_call" | custom-call | tf_op jit(solution)/shard_map/late/pallas_call | solution.py:516
  32.3 0.7 %collective-permute-done.4.y_inner = f32[88,256]{1,0:T(8,128)S(1)} collective-permute-done((f32[88,256]{1,0:T(8,128)S(1)}, f32[88,256]{1,0:T(8,128)S(1)}, u32[]{:S(2)}, u32[]{:S(2)}) %collective-permute-start.4) | collective-permute-done | bytes 90144 | tf_op jit(solution)/shard_map/ppermute | solution.py:410
  33.0 1.8 %collective-permute-done.5.y_outer = f32[88,256]{1,0:T(8,128)S(1)} collective-permute-done((f32[88,256]{1,0:T(8,128)S(1)}, f32[88,256]{1,0:T(8,128)S(1)}, u32[]{:S(2)}, u32[]{:S(2)}) %collective-permute-start.5) | collective-permute-done | bytes 90144 | tf_op jit(solution)/shard_map/ppermute | solution.py:410
  34.8 0.0 collective-permute-done.2.x_inner
  34.8 0.0 collective-permute-done.3.x_outer
  34.8 0.0 copy-done.3
  34.8 2.8 %second.1 = f32[5,16,16,256]{3,2,1,0:T(8,128)} custom-call(f32[100,256]{1,0:T(8,128)S(1)} %get-tuple-element.20.table, f32[5,16,16,256]{3,2,1,0:T(8,128)S(1)} %get-tuple-element.25.state, bf16[2,240,256]{2,1,0:T(8,128)(2,1)S(1)} %copy-done.3, f32[5,16,16,256]{3,2,1,0:T(8,128)S(1)} %copy-done, f32[5,16,16,256]{3,2,1,0:T(8,128)S(1)} %copy-done.1, ...), custom_call_target="tpu_custom_call" | custom-call | tf_op jit(solution)/shard_map/second/pallas_call | solution.py:524
  (1 shorter events, 0.0 us)
Async XLA Ops:
  0.7 15.5 %copy-start.4 = (f32[3,2,5,5]{3,1,2,0:T(2,128)S(1)}, f32[3,2,5,5]{3,1,2,0:T(2,128)}, u32[]{:S(2)}) copy-start(f32[3,2,5,5]{3,1,2,0:T(2,128)} %param.12) | copy-start | bytes 1804
  0.7 15.6 %copy-start = (f32[5,16,16,256]{3,2,1,0:T(8,128)S(1)}, f32[5,16,16,256]{3,2,1,0:T(8,128)}, u32[]{:S(2)}) copy-start(f32[5,16,16,256]{3,2,1,0:T(8,128)} %q_now.5) | copy-start | bytes 3932164
  0.7 15.6 %copy-start.1 = (f32[5,16,16,256]{3,2,1,0:T(8,128)S(1)}, f32[5,16,16,256]{3,2,1,0:T(8,128)}, u32[]{:S(2)}) copy-start(f32[5,16,16,256]{3,2,1,0:T(8,128)} %q_prev.3) | copy-start | bytes 3932164
  0.7 15.6 %copy-start.2 = (f32[16,16,256]{2,1,0:T(8,128)S(1)}, f32[16,16,256]{2,1,0:T(8,128)}, u32[]{:S(2)}) copy-start(f32[16,16,256]{2,1,0:T(8,128)} %jac.5) | copy-start | bytes 786436
  8.5 13.4 %all-to-all-start = ((f32[32,8,128]{2,1,0:T(8,128)}), f32[32,8,128]{2,1,0:T(8,128)S(1)}, u32[]{:S(2)}, u32[]{:S(2)}) async-start(f32[32,8,128]{2,1,0:T(8,128)} %get-tuple-element.21), calls=%async_computation | async-start | bytes 262144 | tf_op jit(solution)/shard_map/all_to_all | solution.py:480
  14.8 7.0 %collective-permute-start = (f32[5,16,256]{2,1,0:T(8,128)S(1)}, f32[5,16,256]{2,1,0:T(8,128)S(1)}, u32[]{:S(2)}, u32[]{:S(2)}) collective-permute-start(f32[5,16,256]{2,1,0:T(8,128)S(1)} %get-tuple-element.23), channel_id=1, source_target_pairs={{0,1},{1,0},{2,3},{3,2},{4,5},{5,4},{6,7},{7,6},{8,9},{9,8},{10,11... | collective-permute-start | bytes 245768 | tf_op jit(solution)/shard_map/ppermute | solution.py:410
  16.1 5.8 %collective-permute-start.1 = (f32[5,16,256]{2,1,0:T(8,128)S(1)}, f32[5,16,256]{2,1,0:T(8,128)S(1)}, u32[]{:S(2)}, u32[]{:S(2)}) collective-permute-start(f32[5,16,256]{2,1,0:T(8,128)S(1)} %get-tuple-element.24), channel_id=1, source_target_pairs={{0,8},{1,2},{2,1},{3,4},{4,3},{5,6},{6,5},{7,15},{8,0},{9,10},{10,... | collective-permute-start | bytes 245768 | tf_op jit(solution)/shard_map/ppermute | solution.py:410
  26.4 8.4 %collective-permute-start.2 = (f32[12,16,256]{2,1,0:T(8,128)S(1)}, f32[12,16,256]{2,1,0:T(8,128)S(1)}, u32[]{:S(2)}, u32[]{:S(2)}) collective-permute-start(f32[12,16,256]{2,1,0:T(8,128)S(1)} %get-tuple-element.31), channel_id=1, source_target_pairs={{0,8},{1,9},{2,10},{3,11},{4,12},{5,13},{6,14},{7,15},{8,0},{9,1},... | collective-permute-start | bytes 589832 | tf_op jit(solution)/shard_map/ppermute | solution.py:410
  27.3 7.5 %collective-permute-start.3 = (f32[12,16,256]{2,1,0:T(8,128)S(1)}, f32[12,16,256]{2,1,0:T(8,128)S(1)}, u32[]{:S(2)}, u32[]{:S(2)}) collective-permute-start(f32[12,16,256]{2,1,0:T(8,128)S(1)} %get-tuple-element.32), channel_id=1, source_target_pairs={{0,2},{1,3},{2,0},{3,1},{4,6},{5,7},{6,4},{7,5},{8,16},{9,17},{10,... | collective-permute-start | bytes 589832 | tf_op jit(solution)/shard_map/ppermute | solution.py:410
  28.5 4.5 %collective-permute-start.4 = (f32[88,256]{1,0:T(8,128)S(1)}, f32[88,256]{1,0:T(8,128)S(1)}, u32[]{:S(2)}, u32[]{:S(2)}) collective-permute-start(f32[88,256]{1,0:T(8,128)S(1)} %get-tuple-element.33), channel_id=1, source_target_pairs={{0,1},{1,0},{2,3},{3,2},{4,5},{5,4},{6,7},{7,6},{8,9},{9,8},{10,11... | collective-permute-start | bytes 270344 | tf_op jit(solution)/shard_map/ppermute | solution.py:410
  29.3 5.5 %collective-permute-start.5 = (f32[88,256]{1,0:T(8,128)S(1)}, f32[88,256]{1,0:T(8,128)S(1)}, u32[]{:S(2)}, u32[]{:S(2)}) collective-permute-start(f32[88,256]{1,0:T(8,128)S(1)} %get-tuple-element.34), channel_id=1, source_target_pairs={{0,8},{1,2},{2,1},{3,4},{4,3},{5,6},{6,5},{7,15},{8,0},{9,10},{10,... | collective-permute-start | bytes 270344 | tf_op jit(solution)/shard_map/ppermute | solution.py:410
  29.5 5.3 %copy-start.3 = (bf16[2,240,256]{2,1,0:T(8,128)(2,1)S(1)}, bf16[2,240,256]{2,1,0:T(8,128)(2,1)}, u32[]{:S(2)}) copy-start(bf16[2,240,256]{2,1,0:T(8,128)(2,1)} %get-tuple-element.26.weights) | copy-start | bytes 737284

commit v8 on v7

--- a/solution.py
+++ b/solution.py
@@ -31,6 +31,10 @@
 def halves(x):
     high = x.astype(jnp.bfloat16)
     return high, (x - high.astype(jnp.float32)).astype(jnp.bfloat16)
+
+
+def eighth(x, power):
+    return (x * 2.0**power).astype(jnp.float8_e4m3fn)
 
 
 def ranks(dest, devices):
@@ -50,7 +54,7 @@
     return jnp.concatenate(pieces, axis=1)
 
 
-def donor_kernel(count, q_prev, q_now, base_in, frac_in, dest_in, cell_in, out_there, y_inner, y_outer, out, planes, lhs, spread, corner, place, values, base, frac, dest, cell, sems, *, size, devices, capacity):
+def donor_kernel(count, q_prev, q_now, base_in, frac_in, dest_in, cell_in, out_there, y_inner, y_outer, out, planes, lhs, lhs_low, spread, spread_low, corner, place, values, base, frac, dest, cell, sems, *, size, devices, capacity):
     nvars, size_x, size_y, size_z = size
     columns = size_x * size_y
     rows = base.shape[1]
@@ -72,9 +76,10 @@
         return jnp.where(at == 0.0, 1.0 - part, jnp.where(at == 1.0, part, 0.0))
 
     along_z = weights(base_z, frac_z, (size_z, rows))
-    high, low = halves(along_z)
-    spread[0] = high
-    spread[1] = low
+    spread[...] = along_z.astype(jnp.bfloat16)
+    rest = along_z - spread[...].astype(jnp.float32)
+    spread_low[0:size_z, :] = eighth(rest, 16)
+    spread_low[size_z : 2 * size_z, :] = eighth(along_z, 8)
     along_x = weights(base_x, frac_x, (size_x, rows))
     along_y = weights(base_y, frac_y, (size_y, rows))
     for x in range(size_x):
@@ -104,16 +109,16 @@
             if k == 0:
                 copies[v].wait()
             at = pl.ds((k * nvars + v) * columns, columns)
-            high, low = halves(planes[k, v])
-            lhs[0, at, :] = high
-            lhs[1, at, :] = low
+            plane = planes[k, v]
+            lhs[at, :] = plane.astype(jnp.bfloat16)
+            lhs_low[at, 0:size_z] = eighth(plane, 6)
+            lhs_low[at, size_z : 2 * size_z] = eighth(plane - plane.astype(jnp.bfloat16).astype(jnp.float32), 14)
     for n in range(rows // LANES):
         lanes = slice(n * LANES, (n + 1) * LANES)
         for k in range(2):
             at = slice(k * nvars * columns, (k + 1) * nvars * columns)
-            part = dot(lhs[0, at, :], spread[0, :, lanes], ((1,), (0,)))
-            part = part + dot(lhs[0, at, :], spread[1, :, lanes], ((1,), (0,)))
-            part = part + dot(lhs[1, at, :], spread[0, :, lanes], ((1,), (0,)))
+            part = dot(lhs[at, :], spread[:, lanes], ((1,), (0,)))
+            part = part + 2.0**-22 * dot(lhs_low[at, :], spread_low[:, lanes], ((1,), (0,)))
             for v in range(nvars):
                 picked = part[v * columns : (v + 1) * columns] * corner[:, lanes]
                 values[k * nvars + v : k * nvars + v + 1, lanes] = jnp.sum(picked, axis=0, keepdims=True)
@@ -455,8 +460,10 @@
         scratch_shapes=[
             pltpu.VMEM((devices, 8, 2 * capacity), f32),
             pltpu.VMEM((2, nvars, columns, size_z), f32),
-            pltpu.VMEM((2, 2 * nvars * columns, size_z), bf16),
-            pltpu.VMEM((2, size_z, rows), bf16),
+            pltpu.VMEM((2 * nvars * columns, size_z), bf16),
+            pltpu.VMEM((2 * nvars * columns, 2 * size_z), jnp.float8_e4m3fn),
+            pltpu.VMEM((size_z, rows), bf16),
+            pltpu.VMEM((2 * size_z, rows), jnp.float8_e4m3fn),
             pltpu.VMEM((columns, rows), f32),
             pltpu.VMEM((rows, 8), f32),
             pltpu.VMEM((CHANNELS, rows), f32),

time: 38 us -> 37.3 us (0.982)
  Pallas kernels: 21.3 us -> 20.5 us
    pallas_call x1, Pallas kernels: 7.77 us -> 6.98 us  [body(): pl.pallas_call(functools.partial(donor_kernel, size=size, devices=devices...]
  transfers between devices with their start and end apart: 7 -> 7, of which waited for: 3 -> 3; matrix products, arithmetic and copies ran while one was open for 0% -> 0% of each run, Pallas kernels for 16% -> 17%
where the time goes in v8:
time: 37.3 us; the launch traced here: 37 us
  Pallas kernels  20.5 us (55%)
  starting transfers between devices  10.7 us (29%)
  waiting for transfers between devices  4.67 us (13%)
  between operations  0.92 us (2%)
    pallas_call x1, Pallas kernels, body(): pl.pallas_call(functools.partial(donor_kernel, size=size, devices=devices...  6.98 us
    all_to_all x1, starting transfers between devices, body(): got = lax.all_to_all(sent, AXES, split_axis=0, concat_axis=0, tiled=True)  6.35 us
    pallas_call x1, Pallas kernels, body(): pl.pallas_call(functools.partial(first_kernel, size=size, devices=devices...  4.59 us
    pallas_call x1, Pallas kernels, body(): pl.pallas_call(functools.partial(early_kernel, size=size), out_shape=[plt...  3.29 us
    ppermute x3, starting transfers between devices, swapped(): lax.ppermute(inner, AXES, inner_pairs)  2.93 us
    ppermute x3, waiting for transfers between devices, swapped(): lax.ppermute(inner, AXES, inner_pairs)  2.88 us
    pallas_call x1, Pallas kernels, body(): pl.pallas_call(late_kernel, out_shape=shape(flat, f32), in_specs=[vmem] *...  2.87 us
    pallas_call x1, Pallas kernels, body(): pl.pallas_call(functools.partial(second_kernel, size=size), out_shape=sha...  2.81 us
  transfers between devices with their start and end apart: 7, of which 3 were waited for; matrix products, arithmetic and copies ran while one was open for 0% of the time, Pallas kernels for 17%

profile of v8, /device:TPU:9, one launch (start us, length us, event | category | flops | bytes accessed | tf_op | source)
XLA Modules:
  0.0 37.0 jit_solution(5579505119311833620)
XLA Ops:
  0.7 0.0 copy-start.4
  0.7 0.0 copy-start
  0.7 0.0 copy-start.1
  0.7 0.0 copy-start.2
  0.7 7.0 %donor.1 = (f32[32,8,128]{2,1,0:T(8,128)}, f32[5,16,256]{2,1,0:T(8,128)S(1)}, f32[5,16,256]{2,1,0:T(8,128)S(1)}) custom-call(s32[1]{0:T(128)S(6)} %copy.11.count, f32[5,256,256]{2,1,0:T(8,128)} %bitcast.6, f32[5,256,256]{2,1,0:T(8,128)} %bitcast.5, s32[1,1024]{1,0:T(1,128)} %bitcast.7, f32[3,1024]{1,0:T(4,128)} %frac_in.1, s32[1,1024]{1,0:T(1,128)} %bitcast.8, ...), custom_call_target="tpu_custom_call" | custom-call | tf_op jit(solution)/shard_map/donor/pallas_call | solution.py:455
  7.7 6.3 %all-to-all-start = ((f32[32,8,128]{2,1,0:T(8,128)}), f32[32,8,128]{2,1,0:T(8,128)S(1)}, u32[]{:S(2)}, u32[]{:S(2)}) async-start(f32[32,8,128]{2,1,0:T(8,128)} %get-tuple-element.21), calls=%async_computation | async-start | bytes 262144 | tf_op jit(solution)/shard_map/all_to_all | solution.py:487
  14.0 1.2 %collective-permute-start = (f32[5,16,256]{2,1,0:T(8,128)S(1)}, f32[5,16,256]{2,1,0:T(8,128)S(1)}, u32[]{:S(2)}, u32[]{:S(2)}) collective-permute-start(f32[5,16,256]{2,1,0:T(8,128)S(1)} %get-tuple-element.23), channel_id=1, source_target_pairs={{0,1},{1,0},{2,3},{3,2},{4,5},{5,4},{6,7},{7,6},{8,9},{9,8},{10,11... | collective-permute-start | bytes 245768 | tf_op jit(solution)/shard_map/ppermute | solution.py:415
  15.3 0.1 collective-permute-start.1
  15.4 0.0 copy-done.4
  15.4 0.1 reshape.18.coef_in
  15.5 0.0 copy-done
  15.5 0.0 copy-done.1
  15.5 0.0 copy-done.2
  15.5 3.3 %early.1 = (f32[5,16,16,256]{3,2,1,0:T(8,128)}, bf16[2,240,256]{2,1,0:T(8,128)(2,1)}, f32[100,256]{1,0:T(8,128)S(1)}) custom-call(f32[150]{0:T(256)S(1)} %reshape.18.coef_in, f32[5,16,16,256]{3,2,1,0:T(8,128)S(1)} %copy-done, f32[5,16,16,256]{3,2,1,0:T(8,128)S(1)} %copy-done.1, f32[16,16,256]{2,1,0:T(8,128)S(1)} %copy-done.2), custom_call_target="tpu_custom_call" | custom-call | tf_op jit(solution)/shard_map/early/pallas_call | solution.py:489
  18.8 2.2 %collective-permute-done.line_inner = f32[5,16,256]{2,1,0:T(8,128)S(1)} collective-permute-done((f32[5,16,256]{2,1,0:T(8,128)S(1)}, f32[5,16,256]{2,1,0:T(8,128)S(1)}, u32[]{:S(2)}, u32[]{:S(2)}) %collective-permute-start) | collective-permute-done | bytes 81952 | tf_op jit(solution)/shard_map/ppermute | solution.py:415
  21.0 0.0 collective-permute-done.1.line_outer
  21.1 0.0 all-to-all-done.got
  21.1 4.6 %first.1 = (f32[5,16,16,256]{3,2,1,0:T(8,128)S(1)}, f32[256,256]{1,0:T(8,128)S(1)}, f32[12,16,256]{2,1,0:T(8,128)S(1)}, f32[12,16,256]{2,1,0:T(8,128)S(1)}, f32[...) custom-call(f32[100,256]{1,0:T(8,128)S(1)} %get-tuple-element.20.tab, ...), custom_call_target="tpu_custom_call" | custom-call | tf_op jit(solution)/shard_map/first/pallas_call | solution.py:498
  25.6 0.9 %collective-permute-start.2 = (f32[12,16,256]{2,1,0:T(8,128)S(1)}, f32[12,16,256]{2,1,0:T(8,128)S(1)}, u32[]{:S(2)}, u32[]{:S(2)}) collective-permute-start(f32[12,16,256]{2,1,0:T(8,128)S(1)} %get-tuple-element.31), channel_id=1, source_target_pairs={{0,8},{1,9},{2,10},{3,11},{4,12},{5,13},{6,14},{7,15},{8,0},{9,1},... | collective-permute-start | bytes 589832 | tf_op jit(solution)/shard_map/ppermute | solution.py:415
  26.6 1.2 %collective-permute-start.3 = (f32[12,16,256]{2,1,0:T(8,128)S(1)}, f32[12,16,256]{2,1,0:T(8,128)S(1)}, u32[]{:S(2)}, u32[]{:S(2)}) collective-permute-start(f32[12,16,256]{2,1,0:T(8,128)S(1)} %get-tuple-element.32), channel_id=1, source_target_pairs={{0,2},{1,3},{2,0},{3,1},{4,6},{5,7},{6,4},{7,5},{8,16},{9,17},{10,... | collective-permute-start | bytes 589832 | tf_op jit(solution)/shard_map/ppermute | solution.py:415
  27.7 0.8 %collective-permute-start.4 = (f32[88,256]{1,0:T(8,128)S(1)}, f32[88,256]{1,0:T(8,128)S(1)}, u32[]{:S(2)}, u32[]{:S(2)}) collective-permute-start(f32[88,256]{1,0:T(8,128)S(1)} %get-tuple-element.33), channel_id=1, source_target_pairs={{0,1},{1,0},{2,3},{3,2},{4,5},{5,4},{6,7},{7,6},{8,9},{9,8},{10,11... | collective-permute-start | bytes 270344 | tf_op jit(solution)/shard_map/ppermute | solution.py:415
  28.5 0.2 collective-permute-start.5
  28.7 0.0 copy-start.3
  28.7 2.9 %late.1.target = f32[5,256,256]{2,1,0:T(8,128)S(1)} custom-call(f32[5,2048]{1,0:T(8,128)S(1)} %get-tuple-element.27.rows, bf16[256,2048]{1,0:T(8,128)(2,1)S(1)} %get-tuple-element.28.hot_xy, bf16[2048,256]{1,0:T(8,128)(2,1)S(1)} %get-tuple-element.29.hot_z), custom_call_target="tpu_custom_call" | custom-call | tf_op jit(solution)/shard_map/late/pallas_call | solution.py:523
  31.6 0.7 %collective-permute-done.4.y_inner = f32[88,256]{1,0:T(8,128)S(1)} collective-permute-done((f32[88,256]{1,0:T(8,128)S(1)}, f32[88,256]{1,0:T(8,128)S(1)}, u32[]{:S(2)}, u32[]{:S(2)}) %collective-permute-start.4) | collective-permute-done | bytes 90144 | tf_op jit(solution)/shard_map/ppermute | solution.py:415
  32.2 1.8 %collective-permute-done.5.y_outer = f32[88,256]{1,0:T(8,128)S(1)} collective-permute-done((f32[88,256]{1,0:T(8,128)S(1)}, f32[88,256]{1,0:T(8,128)S(1)}, u32[]{:S(2)}, u32[]{:S(2)}) %collective-permute-start.5) | collective-permute-done | bytes 90144 | tf_op jit(solution)/shard_map/ppermute | solution.py:415
  34.0 0.0 collective-permute-done.2.x_inner
  34.0 0.0 collective-permute-done.3.x_outer
  34.0 0.0 copy-done.3
  34.0 2.8 %second.1 = f32[5,16,16,256]{3,2,1,0:T(8,128)} custom-call(f32[100,256]{1,0:T(8,128)S(1)} %get-tuple-element.20.table, f32[5,16,16,256]{3,2,1,0:T(8,128)S(1)} %get-tuple-element.25.state, bf16[2,240,256]{2,1,0:T(8,128)(2,1)S(1)} %copy-done.3, f32[5,16,16,256]{3,2,1,0:T(8,128)S(1)} %copy-done, f32[5,16,16,256]{3,2,1,0:T(8,128)S(1)} %copy-done.1, ...), custom_call_target="tpu_custom_call" | custom-call | tf_op jit(solution)/shard_map/second/pallas_call | solution.py:531
  (1 shorter events, 0.0 us)
Async XLA Ops:
  0.7 14.7 %copy-start.4 = (f32[3,2,5,5]{3,1,2,0:T(2,128)S(1)}, f32[3,2,5,5]{3,1,2,0:T(2,128)}, u32[]{:S(2)}) copy-start(f32[3,2,5,5]{3,1,2,0:T(2,128)} %param.12) | copy-start | bytes 1804
  0.7 14.8 %copy-start = (f32[5,16,16,256]{3,2,1,0:T(8,128)S(1)}, f32[5,16,16,256]{3,2,1,0:T(8,128)}, u32[]{:S(2)}) copy-start(f32[5,16,16,256]{3,2,1,0:T(8,128)} %q_now.5) | copy-start | bytes 3932164
  0.7 14.8 %copy-start.1 = (f32[5,16,16,256]{3,2,1,0:T(8,128)S(1)}, f32[5,16,16,256]{3,2,1,0:T(8,128)}, u32[]{:S(2)}) copy-start(f32[5,16,16,256]{3,2,1,0:T(8,128)} %q_prev.3) | copy-start | bytes 3932164
  0.7 14.8 %copy-start.2 = (f32[16,16,256]{2,1,0:T(8,128)S(1)}, f32[16,16,256]{2,1,0:T(8,128)}, u32[]{:S(2)}) copy-start(f32[16,16,256]{2,1,0:T(8,128)} %jac.5) | copy-start | bytes 786436
  7.7 13.4 %all-to-all-start = ((f32[32,8,128]{2,1,0:T(8,128)}), f32[32,8,128]{2,1,0:T(8,128)S(1)}, u32[]{:S(2)}, u32[]{:S(2)}) async-start(f32[32,8,128]{2,1,0:T(8,128)} %get-tuple-element.21), calls=%async_computation | async-start | bytes 262144 | tf_op jit(solution)/shard_map/all_to_all | solution.py:487
  14.0 7.0 %collective-permute-start = (f32[5,16,256]{2,1,0:T(8,128)S(1)}, f32[5,16,256]{2,1,0:T(8,128)S(1)}, u32[]{:S(2)}, u32[]{:S(2)}) collective-permute-start(f32[5,16,256]{2,1,0:T(8,128)S(1)} %get-tuple-element.23), channel_id=1, source_target_pairs={{0,1},{1,0},{2,3},{3,2},{4,5},{5,4},{6,7},{7,6},{8,9},{9,8},{10,11... | collective-permute-start | bytes 245768 | tf_op jit(solution)/shard_map/ppermute | solution.py:415
  15.3 5.8 %collective-permute-start.1 = (f32[5,16,256]{2,1,0:T(8,128)S(1)}, f32[5,16,256]{2,1,0:T(8,128)S(1)}, u32[]{:S(2)}, u32[]{:S(2)}) collective-permute-start(f32[5,16,256]{2,1,0:T(8,128)S(1)} %get-tuple-element.24), channel_id=1, source_target_pairs={{0,8},{1,2},{2,1},{3,4},{4,3},{5,6},{6,5},{7,15},{8,0},{9,10},{10,... | collective-permute-start | bytes 245768 | tf_op jit(solution)/shard_map/ppermute | solution.py:415
  25.6 8.4 %collective-permute-start.2 = (f32[12,16,256]{2,1,0:T(8,128)S(1)}, f32[12,16,256]{2,1,0:T(8,128)S(1)}, u32[]{:S(2)}, u32[]{:S(2)}) collective-permute-start(f32[12,16,256]{2,1,0:T(8,128)S(1)} %get-tuple-element.31), channel_id=1, source_target_pairs={{0,8},{1,9},{2,10},{3,11},{4,12},{5,13},{6,14},{7,15},{8,0},{9,1},... | collective-permute-start | bytes 589832 | tf_op jit(solution)/shard_map/ppermute | solution.py:415
  26.6 7.5 %collective-permute-start.3 = (f32[12,16,256]{2,1,0:T(8,128)S(1)}, f32[12,16,256]{2,1,0:T(8,128)S(1)}, u32[]{:S(2)}, u32[]{:S(2)}) collective-permute-start(f32[12,16,256]{2,1,0:T(8,128)S(1)} %get-tuple-element.32), channel_id=1, source_target_pairs={{0,2},{1,3},{2,0},{3,1},{4,6},{5,7},{6,4},{7,5},{8,16},{9,17},{10,... | collective-permute-start | bytes 589832 | tf_op jit(solution)/shard_map/ppermute | solution.py:415
  27.7 4.5 %collective-permute-start.4 = (f32[88,256]{1,0:T(8,128)S(1)}, f32[88,256]{1,0:T(8,128)S(1)}, u32[]{:S(2)}, u32[]{:S(2)}) collective-permute-start(f32[88,256]{1,0:T(8,128)S(1)} %get-tuple-element.33), channel_id=1, source_target_pairs={{0,1},{1,0},{2,3},{3,2},{4,5},{5,4},{6,7},{7,6},{8,9},{9,8},{10,11... | collective-permute-start | bytes 270344 | tf_op jit(solution)/shard_map/ppermute | solution.py:415
  28.5 5.5 %collective-permute-start.5 = (f32[88,256]{1,0:T(8,128)S(1)}, f32[88,256]{1,0:T(8,128)S(1)}, u32[]{:S(2)}, u32[]{:S(2)}) collective-permute-start(f32[88,256]{1,0:T(8,128)S(1)} %get-tuple-element.34), channel_id=1, source_target_pairs={{0,8},{1,2},{2,1},{3,4},{4,3},{5,6},{6,5},{7,15},{8,0},{9,10},{10,... | collective-permute-start | bytes 270344 | tf_op jit(solution)/shard_map/ppermute | solution.py:415
  28.7 5.3 %copy-start.3 = (bf16[2,240,256]{2,1,0:T(8,128)(2,1)S(1)}, bf16[2,240,256]{2,1,0:T(8,128)(2,1)}, u32[]{:S(2)}) copy-start(bf16[2,240,256]{2,1,0:T(8,128)(2,1)} %get-tuple-element.26.weights) | copy-start | bytes 737284

commit v9 on v8

--- a/solution.py
+++ b/solution.py
@@ -274,7 +274,24 @@
             store(c, landed[at : at + columns] + landed[at + columns : at + 2 * columns])
 
 
-def first_kernel(table, got, base_in, q_now, jac, line_inner, line_outer, state, hits, x_inner, x_outer, y_inner, y_outer, later, hot_xy, hot_z, rows, grid, base, sems, *, size, devices, capacity):
+def land_split(rows, hot_xy, hot_z, hot_z_low, store, nvars):
+    columns = hot_xy.shape[0]
+    for first in range(0, nvars, 2):
+        some = range(first, min(first + 2, nvars))
+        high, low = [], []
+        for c in some:
+            whole = rows[c : c + 1, :]
+            part = whole.astype(jnp.bfloat16)
+            high.append(hot_xy[...] * part)
+            scaled = ((whole - part.astype(jnp.float32)) * 2.0**14).astype(jnp.bfloat16)
+            low.append((hot_xy[...] * scaled).astype(jnp.float8_e4m3fn))
+        landed = dot(jnp.concatenate(high, axis=0), hot_z[...], ((1,), (0,)))
+        landed = landed + 2.0**-14 * dot(jnp.concatenate(low, axis=0), hot_z_low[...], ((1,), (0,)))
+        for c in some:
+            store(c, landed[(c - first) * columns : (c - first + 1) * columns])
+
+
+def first_kernel(table, got, base_in, q_now, jac, line_inner, line_outer, state, hits, x_inner, x_outer, y_inner, y_outer, later, hot_xy, hot_z, hot_z_low, rows, grid, base, sems, *, size, devices, capacity):
     nvars, size_x, size_y, size_z = size
     columns = size_x * size_y
     slots = devices * capacity
@@ -294,6 +311,7 @@
     turned = jnp.transpose(rows[8:16, :])
     land_z = turned[:, 2 * nvars + 1 - 8 : 2 * nvars + 2 - 8]
     hot_z[...] = (iota((slots, size_z), 1).astype(jnp.float32) == land_z).astype(jnp.float32).astype(jnp.bfloat16)
+    hot_z_low[...] = (iota((slots, size_z), 1).astype(jnp.float32) == land_z).astype(jnp.float32).astype(jnp.float8_e4m3fn)
     land_xy = rows[2 * nvars : 2 * nvars + 1, :]
     hot_xy[...] = ((iota((columns, slots), 0) + 1).astype(jnp.float32) == land_xy).astype(jnp.float32).astype(jnp.bfloat16)
     later[...] = rows[nvars : 2 * nvars, :]
@@ -308,7 +326,7 @@
     def keep(c, value):
         grid[c] = value
 
-    land(rows, hot_xy, hot_z, keep, nvars)
+    land_split(rows, hot_xy, hot_z, hot_z_low, keep, nvars)
     for x in range(size_x):
         fetch(x).wait()
     for x in range(size_x):
@@ -511,6 +529,7 @@
         in_specs=[vmem, vmem, hbm] + [vmem] * 4,
         out_specs=[vmem] * 9,
         scratch_shapes=[
+            pltpu.VMEM((slots, size_z), jnp.float8_e4m3fn),
             pltpu.VMEM((CHANNELS, slots), f32),
             pltpu.VMEM((nvars, columns, size_z), f32),
             pltpu.VMEM(size, f32),

time: 37.3 us -> 36.6 us (0.981)
  Pallas kernels: 20.5 us -> 19.9 us
    pallas_call x1, Pallas kernels: 4.59 us -> 3.97 us  [body(): pl.pallas_call(functools.partial(first_kernel, size=size, devices=devices...]
where the time goes in v9:
time: 36.6 us; the launch traced here: 36.4 us
  Pallas kernels  19.9 us (54%)
  starting transfers between devices  10.7 us (29%)
  waiting for transfers between devices  4.67 us (13%)
  between operations  0.92 us (3%)
    pallas_call x1, Pallas kernels, body(): pl.pallas_call(functools.partial(donor_kernel, size=size, devices=devices...  6.98 us
    all_to_all x1, starting transfers between devices, body(): got = lax.all_to_all(sent, AXES, split_axis=0, concat_axis=0, tiled=True)  6.35 us
    pallas_call x1, Pallas kernels, body(): pl.pallas_call(functools.partial(first_kernel, size=size, devices=devices...  3.97 us
    pallas_call x1, Pallas kernels, body(): pl.pallas_call(functools.partial(early_kernel, size=size), out_shape=[plt...  3.29 us
    ppermute x3, starting transfers between devices, swapped(): lax.ppermute(inner, AXES, inner_pairs)  2.93 us
    ppermute x3, waiting for transfers between devices, swapped(): lax.ppermute(inner, AXES, inner_pairs)  2.88 us
    pallas_call x1, Pallas kernels, body(): pl.pallas_call(late_kernel, out_shape=shape(flat, f32), in_specs=[vmem] *...  2.87 us
    pallas_call x1, Pallas kernels, body(): pl.pallas_call(functools.partial(second_kernel, size=size), out_shape=sha...  2.81 us
  transfers between devices with their start and end apart: 7, of which 3 were waited for; matrix products, arithmetic and copies ran while one was open for 0% of the time, Pallas kernels for 17%

profile of v9, /device:TPU:9, one launch (start us, length us, event | category | flops | bytes accessed | tf_op | source)
XLA Modules:
  0.0 36.4 jit_solution(12131831672352470438)
XLA Ops:
  0.7 0.0 copy-start.4
  0.7 0.0 copy-start
  0.7 0.0 copy-start.1
  0.7 0.0 copy-start.2
  0.7 7.0 %donor.1 = (f32[32,8,128]{2,1,0:T(8,128)}, f32[5,16,256]{2,1,0:T(8,128)S(1)}, f32[5,16,256]{2,1,0:T(8,128)S(1)}) custom-call(s32[1]{0:T(128)S(6)} %copy.11.count, f32[5,256,256]{2,1,0:T(8,128)} %bitcast.6, f32[5,256,256]{2,1,0:T(8,128)} %bitcast.5, s32[1,1024]{1,0:T(1,128)} %bitcast.7, f32[3,1024]{1,0:T(4,128)} %frac_in.1, s32[1,1024]{1,0:T(1,128)} %bitcast.8, ...), custom_call_target="tpu_custom_call" | custom-call | tf_op jit(solution)/shard_map/donor/pallas_call | solution.py:473
  7.7 6.3 %all-to-all-start = ((f32[32,8,128]{2,1,0:T(8,128)}), f32[32,8,128]{2,1,0:T(8,128)S(1)}, u32[]{:S(2)}, u32[]{:S(2)}) async-start(f32[32,8,128]{2,1,0:T(8,128)} %get-tuple-element.21), calls=%async_computation | async-start | bytes 262144 | tf_op jit(solution)/shard_map/all_to_all | solution.py:505
  14.0 1.2 %collective-permute-start = (f32[5,16,256]{2,1,0:T(8,128)S(1)}, f32[5,16,256]{2,1,0:T(8,128)S(1)}, u32[]{:S(2)}, u32[]{:S(2)}) collective-permute-start(f32[5,16,256]{2,1,0:T(8,128)S(1)} %get-tuple-element.23), channel_id=1, source_target_pairs={{0,1},{1,0},{2,3},{3,2},{4,5},{5,4},{6,7},{7,6},{8,9},{9,8},{10,11... | collective-permute-start | bytes 245768 | tf_op jit(solution)/shard_map/ppermute | solution.py:433
  15.3 0.1 collective-permute-start.1
  15.4 0.0 copy-done.4
  15.4 0.1 reshape.18.coef_in
  15.5 0.0 copy-done
  15.5 0.0 copy-done.1
  15.5 0.0 copy-done.2
  15.5 3.3 %early.1 = (f32[5,16,16,256]{3,2,1,0:T(8,128)}, bf16[2,240,256]{2,1,0:T(8,128)(2,1)}, f32[100,256]{1,0:T(8,128)S(1)}) custom-call(f32[150]{0:T(256)S(1)} %reshape.18.coef_in, f32[5,16,16,256]{3,2,1,0:T(8,128)S(1)} %copy-done, f32[5,16,16,256]{3,2,1,0:T(8,128)S(1)} %copy-done.1, f32[16,16,256]{2,1,0:T(8,128)S(1)} %copy-done.2), custom_call_target="tpu_custom_call" | custom-call | tf_op jit(solution)/shard_map/early/pallas_call | solution.py:507
  18.8 2.2 %collective-permute-done.line_inner = f32[5,16,256]{2,1,0:T(8,128)S(1)} collective-permute-done((f32[5,16,256]{2,1,0:T(8,128)S(1)}, f32[5,16,256]{2,1,0:T(8,128)S(1)}, u32[]{:S(2)}, u32[]{:S(2)}) %collective-permute-start) | collective-permute-done | bytes 81952 | tf_op jit(solution)/shard_map/ppermute | solution.py:433
  21.0 0.0 collective-permute-done.1.line_outer
  21.1 0.0 all-to-all-done.got
  21.1 4.0 %first.1 = (f32[5,16,16,256]{3,2,1,0:T(8,128)S(1)}, f32[256,256]{1,0:T(8,128)S(1)}, f32[12,16,256]{2,1,0:T(8,128)S(1)}, f32[12,16,256]{2,1,0:T(8,128)S(1)}, f32[...) custom-call(f32[100,256]{1,0:T(8,128)S(1)} %get-tuple-element.20.tab, ...), custom_call_target="tpu_custom_call" | custom-call | tf_op jit(solution)/shard_map/first/pallas_call | solution.py:516
  25.0 0.9 %collective-permute-start.2 = (f32[12,16,256]{2,1,0:T(8,128)S(1)}, f32[12,16,256]{2,1,0:T(8,128)S(1)}, u32[]{:S(2)}, u32[]{:S(2)}) collective-permute-start(f32[12,16,256]{2,1,0:T(8,128)S(1)} %get-tuple-element.31), channel_id=1, source_target_pairs={{0,8},{1,9},{2,10},{3,11},{4,12},{5,13},{6,14},{7,15},{8,0},{9,1},... | collective-permute-start | bytes 589832 | tf_op jit(solution)/shard_map/ppermute | solution.py:433
  26.0 1.1 %collective-permute-start.3 = (f32[12,16,256]{2,1,0:T(8,128)S(1)}, f32[12,16,256]{2,1,0:T(8,128)S(1)}, u32[]{:S(2)}, u32[]{:S(2)}) collective-permute-start(f32[12,16,256]{2,1,0:T(8,128)S(1)} %get-tuple-element.32), channel_id=1, source_target_pairs={{0,2},{1,3},{2,0},{3,1},{4,6},{5,7},{6,4},{7,5},{8,16},{9,17},{10,... | collective-permute-start | bytes 589832 | tf_op jit(solution)/shard_map/ppermute | solution.py:433
  27.1 0.8 %collective-permute-start.4 = (f32[88,256]{1,0:T(8,128)S(1)}, f32[88,256]{1,0:T(8,128)S(1)}, u32[]{:S(2)}, u32[]{:S(2)}) collective-permute-start(f32[88,256]{1,0:T(8,128)S(1)} %get-tuple-element.33), channel_id=1, source_target_pairs={{0,1},{1,0},{2,3},{3,2},{4,5},{5,4},{6,7},{7,6},{8,9},{9,8},{10,11... | collective-permute-start | bytes 270344 | tf_op jit(solution)/shard_map/ppermute | solution.py:433
  27.9 0.2 collective-permute-start.5
  28.1 0.0 copy-start.3
  28.1 2.9 %late.1.target = f32[5,256,256]{2,1,0:T(8,128)S(1)} custom-call(f32[5,2048]{1,0:T(8,128)S(1)} %get-tuple-element.27.rows, bf16[256,2048]{1,0:T(8,128)(2,1)S(1)} %get-tuple-element.28.hot_xy, bf16[2048,256]{1,0:T(8,128)(2,1)S(1)} %get-tuple-element.29.hot_z), custom_call_target="tpu_custom_call" | custom-call | tf_op jit(solution)/shard_map/late/pallas_call | solution.py:542
  30.9 0.7 %collective-permute-done.4.y_inner = f32[88,256]{1,0:T(8,128)S(1)} collective-permute-done((f32[88,256]{1,0:T(8,128)S(1)}, f32[88,256]{1,0:T(8,128)S(1)}, u32[]{:S(2)}, u32[]{:S(2)}) %collective-permute-start.4) | collective-permute-done | bytes 90144 | tf_op jit(solution)/shard_map/ppermute | solution.py:433
  31.6 1.8 %collective-permute-done.5.y_outer = f32[88,256]{1,0:T(8,128)S(1)} collective-permute-done((f32[88,256]{1,0:T(8,128)S(1)}, f32[88,256]{1,0:T(8,128)S(1)}, u32[]{:S(2)}, u32[]{:S(2)}) %collective-permute-start.5) | collective-permute-done | bytes 90144 | tf_op jit(solution)/shard_map/ppermute | solution.py:433
  33.4 0.0 collective-permute-done.2.x_inner
  33.4 0.0 collective-permute-done.3.x_outer
  33.4 0.0 copy-done.3
  33.4 2.8 %second.1 = f32[5,16,16,256]{3,2,1,0:T(8,128)} custom-call(f32[100,256]{1,0:T(8,128)S(1)} %get-tuple-element.20.table, f32[5,16,16,256]{3,2,1,0:T(8,128)S(1)} %get-tuple-element.25.state, bf16[2,240,256]{2,1,0:T(8,128)(2,1)S(1)} %copy-done.3, f32[5,16,16,256]{3,2,1,0:T(8,128)S(1)} %copy-done, f32[5,16,16,256]{3,2,1,0:T(8,128)S(1)} %copy-done.1, ...), custom_call_target="tpu_custom_call" | custom-call | tf_op jit(solution)/shard_map/second/pallas_call | solution.py:550
  (1 shorter events, 0.0 us)
Async XLA Ops:
  0.7 14.7 %copy-start.4 = (f32[3,2,5,5]{3,1,2,0:T(2,128)S(1)}, f32[3,2,5,5]{3,1,2,0:T(2,128)}, u32[]{:S(2)}) copy-start(f32[3,2,5,5]{3,1,2,0:T(2,128)} %param.12) | copy-start | bytes 1804
  0.7 14.8 %copy-start = (f32[5,16,16,256]{3,2,1,0:T(8,128)S(1)}, f32[5,16,16,256]{3,2,1,0:T(8,128)}, u32[]{:S(2)}) copy-start(f32[5,16,16,256]{3,2,1,0:T(8,128)} %q_now.5) | copy-start | bytes 3932164
  0.7 14.8 %copy-start.1 = (f32[5,16,16,256]{3,2,1,0:T(8,128)S(1)}, f32[5,16,16,256]{3,2,1,0:T(8,128)}, u32[]{:S(2)}) copy-start(f32[5,16,16,256]{3,2,1,0:T(8,128)} %q_prev.3) | copy-start | bytes 3932164
  0.7 14.8 %copy-start.2 = (f32[16,16,256]{2,1,0:T(8,128)S(1)}, f32[16,16,256]{2,1,0:T(8,128)}, u32[]{:S(2)}) copy-start(f32[16,16,256]{2,1,0:T(8,128)} %jac.5) | copy-start | bytes 786436
  7.7 13.4 %all-to-all-start = ((f32[32,8,128]{2,1,0:T(8,128)}), f32[32,8,128]{2,1,0:T(8,128)S(1)}, u32[]{:S(2)}, u32[]{:S(2)}) async-start(f32[32,8,128]{2,1,0:T(8,128)} %get-tuple-element.21), calls=%async_computation | async-start | bytes 262144 | tf_op jit(solution)/shard_map/all_to_all | solution.py:505
  14.0 7.0 %collective-permute-start = (f32[5,16,256]{2,1,0:T(8,128)S(1)}, f32[5,16,256]{2,1,0:T(8,128)S(1)}, u32[]{:S(2)}, u32[]{:S(2)}) collective-permute-start(f32[5,16,256]{2,1,0:T(8,128)S(1)} %get-tuple-element.23), channel_id=1, source_target_pairs={{0,1},{1,0},{2,3},{3,2},{4,5},{5,4},{6,7},{7,6},{8,9},{9,8},{10,11... | collective-permute-start | bytes 245768 | tf_op jit(solution)/shard_map/ppermute | solution.py:433
  15.3 5.8 %collective-permute-start.1 = (f32[5,16,256]{2,1,0:T(8,128)S(1)}, f32[5,16,256]{2,1,0:T(8,128)S(1)}, u32[]{:S(2)}, u32[]{:S(2)}) collective-permute-start(f32[5,16,256]{2,1,0:T(8,128)S(1)} %get-tuple-element.24), channel_id=1, source_target_pairs={{0,8},{1,2},{2,1},{3,4},{4,3},{5,6},{6,5},{7,15},{8,0},{9,10},{10,... | collective-permute-start | bytes 245768 | tf_op jit(solution)/shard_map/ppermute | solution.py:433
  25.0 8.4 %collective-permute-start.2 = (f32[12,16,256]{2,1,0:T(8,128)S(1)}, f32[12,16,256]{2,1,0:T(8,128)S(1)}, u32[]{:S(2)}, u32[]{:S(2)}) collective-permute-start(f32[12,16,256]{2,1,0:T(8,128)S(1)} %get-tuple-element.31), channel_id=1, source_target_pairs={{0,8},{1,9},{2,10},{3,11},{4,12},{5,13},{6,14},{7,15},{8,0},{9,1},... | collective-permute-start | bytes 589832 | tf_op jit(solution)/shard_map/ppermute | solution.py:433
  26.0 7.5 %collective-permute-start.3 = (f32[12,16,256]{2,1,0:T(8,128)S(1)}, f32[12,16,256]{2,1,0:T(8,128)S(1)}, u32[]{:S(2)}, u32[]{:S(2)}) collective-permute-start(f32[12,16,256]{2,1,0:T(8,128)S(1)} %get-tuple-element.32), channel_id=1, source_target_pairs={{0,2},{1,3},{2,0},{3,1},{4,6},{5,7},{6,4},{7,5},{8,16},{9,17},{10,... | collective-permute-start | bytes 589832 | tf_op jit(solution)/shard_map/ppermute | solution.py:433
  27.1 4.5 %collective-permute-start.4 = (f32[88,256]{1,0:T(8,128)S(1)}, f32[88,256]{1,0:T(8,128)S(1)}, u32[]{:S(2)}, u32[]{:S(2)}) collective-permute-start(f32[88,256]{1,0:T(8,128)S(1)} %get-tuple-element.33), channel_id=1, source_target_pairs={{0,1},{1,0},{2,3},{3,2},{4,5},{5,4},{6,7},{7,6},{8,9},{9,8},{10,11... | collective-permute-start | bytes 270344 | tf_op jit(solution)/shard_map/ppermute | solution.py:433
  27.9 5.5 %collective-permute-start.5 = (f32[88,256]{1,0:T(8,128)S(1)}, f32[88,256]{1,0:T(8,128)S(1)}, u32[]{:S(2)}, u32[]{:S(2)}) collective-permute-start(f32[88,256]{1,0:T(8,128)S(1)} %get-tuple-element.34), channel_id=1, source_target_pairs={{0,8},{1,2},{2,1},{3,4},{4,3},{5,6},{6,5},{7,15},{8,0},{9,10},{10,... | collective-permute-start | bytes 270344 | tf_op jit(solution)/shard_map/ppermute | solution.py:433
  28.1 5.3 %copy-start.3 = (bf16[2,240,256]{2,1,0:T(8,128)(2,1)S(1)}, bf16[2,240,256]{2,1,0:T(8,128)(2,1)}, u32[]{:S(2)}) copy-start(bf16[2,240,256]{2,1,0:T(8,128)(2,1)} %get-tuple-element.26.weights) | copy-start | bytes 737284

commit v10 on v9

--- a/solution.py
+++ b/solution.py
@@ -339,11 +339,13 @@
             change = change + jnp.where(row_at == size_y - 1, from_high[v][x : x + 1], 0.0)
             new = base[v, x] - scale * change
             state[v, x] = new
-            low, high = new[0:1], new[size_y - 1 : size_y]
-            y_inner[v * size_x + x : v * size_x + x + 1, :] = jnp.where(even_y, high, low)
-            y_outer[v * size_x + x : v * size_x + x + 1, :] = jnp.where(even_y, low, high)
             if x in (0, size_x - 1):
                 faces[x, v] = new
+    toward = jnp.where(even_y, size_y - 1, 0)
+    for v in range(nvars):
+        for x in range(size_x):
+            y_inner[v * size_x + x : v * size_x + x + 1, :] = state[v, x, pl.ds(toward, 1), :]
+            y_outer[v * size_x + x : v * size_x + x + 1, :] = state[v, x, pl.ds(size_y - 1 - toward, 1), :]
     tail = nvars * size_x
     y_inner[tail:, :] = y_outer[tail:, :] = jnp.zeros((8, size_z), jnp.float32)
     for k, x in enumerate((0, size_x - 1)):

time: 36.6 us -> 36.6 us (level)
  no operation moved by 1% of the time
where the time goes in v10:
time: 36.6 us; the launch traced here: 36.4 us
  Pallas kernels  19.9 us (54%)
  starting transfers between devices  10.7 us (29%)
  waiting for transfers between devices  4.67 us (13%)
  between operations  0.92 us (3%)
    pallas_call x1, Pallas kernels, body(): pl.pallas_call(functools.partial(donor_kernel, size=size, devices=devices...  6.98 us
    all_to_all x1, starting transfers between devices, body(): got = lax.all_to_all(sent, AXES, split_axis=0, concat_axis=0, tiled=True)  6.35 us
    pallas_call x1, Pallas kernels, body(): pl.pallas_call(functools.partial(first_kernel, size=size, devices=devices...  3.94 us
    pallas_call x1, Pallas kernels, body(): pl.pallas_call(functools.partial(early_kernel, size=size), out_shape=[plt...  3.29 us
    ppermute x3, starting transfers between devices, swapped(): lax.ppermute(inner, AXES, inner_pairs)  2.94 us
    ppermute x3, waiting for transfers between devices, swapped(): lax.ppermute(inner, AXES, inner_pairs)  2.88 us
    pallas_call x1, Pallas kernels, body(): pl.pallas_call(late_kernel, out_shape=shape(flat, f32), in_specs=[vmem] *...  2.87 us
    pallas_call x1, Pallas kernels, body(): pl.pallas_call(functools.partial(second_kernel, size=size), out_shape=sha...  2.82 us
  transfers between devices with their start and end apart: 7, of which 3 were waited for; matrix products, arithmetic and copies ran while one was open for 0% of the time, Pallas kernels for 17%

profile of v10, /device:TPU:9, one launch (start us, length us, event | category | flops | bytes accessed | tf_op | source)
XLA Modules:
  0.0 36.4 jit_solution(1595418934996521918)
XLA Ops:
  0.7 0.0 copy-start.4
  0.7 0.0 copy-start
  0.7 0.0 copy-start.1
  0.7 0.0 copy-start.2
  0.7 7.0 %donor.1 = (f32[32,8,128]{2,1,0:T(8,128)}, f32[5,16,256]{2,1,0:T(8,128)S(1)}, f32[5,16,256]{2,1,0:T(8,128)S(1)}) custom-call(s32[1]{0:T(128)S(6)} %copy.11.count, f32[5,256,256]{2,1,0:T(8,128)} %bitcast.6, f32[5,256,256]{2,1,0:T(8,128)} %bitcast.5, s32[1,1024]{1,0:T(1,128)} %bitcast.7, f32[3,1024]{1,0:T(4,128)} %frac_in.1, s32[1,1024]{1,0:T(1,128)} %bitcast.8, ...), custom_call_target="tpu_custom_call" | custom-call | tf_op jit(solution)/shard_map/donor/pallas_call | solution.py:475
  7.7 6.3 %all-to-all-start = ((f32[32,8,128]{2,1,0:T(8,128)}), f32[32,8,128]{2,1,0:T(8,128)S(1)}, u32[]{:S(2)}, u32[]{:S(2)}) async-start(f32[32,8,128]{2,1,0:T(8,128)} %get-tuple-element.21), calls=%async_computation | async-start | bytes 262144 | tf_op jit(solution)/shard_map/all_to_all | solution.py:507
  14.0 1.2 %collective-permute-start = (f32[5,16,256]{2,1,0:T(8,128)S(1)}, f32[5,16,256]{2,1,0:T(8,128)S(1)}, u32[]{:S(2)}, u32[]{:S(2)}) collective-permute-start(f32[5,16,256]{2,1,0:T(8,128)S(1)} %get-tuple-element.23), channel_id=1, source_target_pairs={{0,1},{1,0},{2,3},{3,2},{4,5},{5,4},{6,7},{7,6},{8,9},{9,8},{10,11... | collective-permute-start | bytes 245768 | tf_op jit(solution)/shard_map/ppermute | solution.py:435
  15.3 0.1 collective-permute-start.1
  15.4 0.0 copy-done.4
  15.4 0.1 reshape.18.coef_in
  15.5 0.0 copy-done
  15.5 0.0 copy-done.1
  15.5 0.0 copy-done.2
  15.5 3.3 %early.1 = (f32[5,16,16,256]{3,2,1,0:T(8,128)}, bf16[2,240,256]{2,1,0:T(8,128)(2,1)}, f32[100,256]{1,0:T(8,128)S(1)}) custom-call(f32[150]{0:T(256)S(1)} %reshape.18.coef_in, f32[5,16,16,256]{3,2,1,0:T(8,128)S(1)} %copy-done, f32[5,16,16,256]{3,2,1,0:T(8,128)S(1)} %copy-done.1, f32[16,16,256]{2,1,0:T(8,128)S(1)} %copy-done.2), custom_call_target="tpu_custom_call" | custom-call | tf_op jit(solution)/shard_map/early/pallas_call | solution.py:509
  18.8 2.2 %collective-permute-done.line_inner = f32[5,16,256]{2,1,0:T(8,128)S(1)} collective-permute-done((f32[5,16,256]{2,1,0:T(8,128)S(1)}, f32[5,16,256]{2,1,0:T(8,128)S(1)}, u32[]{:S(2)}, u32[]{:S(2)}) %collective-permute-start) | collective-permute-done | bytes 81952 | tf_op jit(solution)/shard_map/ppermute | solution.py:435
  21.0 0.0 collective-permute-done.1.line_outer
  21.1 0.0 all-to-all-done.got
  21.1 3.9 %first.1 = (f32[5,16,16,256]{3,2,1,0:T(8,128)S(1)}, f32[256,256]{1,0:T(8,128)S(1)}, f32[12,16,256]{2,1,0:T(8,128)S(1)}, f32[12,16,256]{2,1,0:T(8,128)S(1)}, f32[...) custom-call(f32[100,256]{1,0:T(8,128)S(1)} %get-tuple-element.20.tab, ...), custom_call_target="tpu_custom_call" | custom-call | tf_op jit(solution)/shard_map/first/pallas_call | solution.py:518
  25.0 0.9 %collective-permute-start.2 = (f32[12,16,256]{2,1,0:T(8,128)S(1)}, f32[12,16,256]{2,1,0:T(8,128)S(1)}, u32[]{:S(2)}, u32[]{:S(2)}) collective-permute-start(f32[12,16,256]{2,1,0:T(8,128)S(1)} %get-tuple-element.31), channel_id=1, source_target_pairs={{0,8},{1,9},{2,10},{3,11},{4,12},{5,13},{6,14},{7,15},{8,0},{9,1},... | collective-permute-start | bytes 589832 | tf_op jit(solution)/shard_map/ppermute | solution.py:435
  25.9 1.1 %collective-permute-start.3 = (f32[12,16,256]{2,1,0:T(8,128)S(1)}, f32[12,16,256]{2,1,0:T(8,128)S(1)}, u32[]{:S(2)}, u32[]{:S(2)}) collective-permute-start(f32[12,16,256]{2,1,0:T(8,128)S(1)} %get-tuple-element.32), channel_id=1, source_target_pairs={{0,2},{1,3},{2,0},{3,1},{4,6},{5,7},{6,4},{7,5},{8,16},{9,17},{10,... | collective-permute-start | bytes 589832 | tf_op jit(solution)/shard_map/ppermute | solution.py:435
  27.1 0.8 %collective-permute-start.4 = (f32[88,256]{1,0:T(8,128)S(1)}, f32[88,256]{1,0:T(8,128)S(1)}, u32[]{:S(2)}, u32[]{:S(2)}) collective-permute-start(f32[88,256]{1,0:T(8,128)S(1)} %get-tuple-element.33), channel_id=1, source_target_pairs={{0,1},{1,0},{2,3},{3,2},{4,5},{5,4},{6,7},{7,6},{8,9},{9,8},{10,11... | collective-permute-start | bytes 270344 | tf_op jit(solution)/shard_map/ppermute | solution.py:435
  27.8 0.2 collective-permute-start.5
  28.0 0.0 copy-start.3
  28.0 2.9 %late.1.target = f32[5,256,256]{2,1,0:T(8,128)S(1)} custom-call(f32[5,2048]{1,0:T(8,128)S(1)} %get-tuple-element.27.rows, bf16[256,2048]{1,0:T(8,128)(2,1)S(1)} %get-tuple-element.28.hot_xy, bf16[2048,256]{1,0:T(8,128)(2,1)S(1)} %get-tuple-element.29.hot_z), custom_call_target="tpu_custom_call" | custom-call | tf_op jit(solution)/shard_map/late/pallas_call | solution.py:544
  30.9 0.7 %collective-permute-done.4.y_inner = f32[88,256]{1,0:T(8,128)S(1)} collective-permute-done((f32[88,256]{1,0:T(8,128)S(1)}, f32[88,256]{1,0:T(8,128)S(1)}, u32[]{:S(2)}, u32[]{:S(2)}) %collective-permute-start.4) | collective-permute-done | bytes 90144 | tf_op jit(solution)/shard_map/ppermute | solution.py:435
  31.6 1.8 %collective-permute-done.5.y_outer = f32[88,256]{1,0:T(8,128)S(1)} collective-permute-done((f32[88,256]{1,0:T(8,128)S(1)}, f32[88,256]{1,0:T(8,128)S(1)}, u32[]{:S(2)}, u32[]{:S(2)}) %collective-permute-start.5) | collective-permute-done | bytes 90144 | tf_op jit(solution)/shard_map/ppermute | solution.py:435
  33.4 0.0 collective-permute-done.2.x_inner
  33.4 0.0 collective-permute-done.3.x_outer
  33.4 0.0 copy-done.3
  33.4 2.8 %second.1 = f32[5,16,16,256]{3,2,1,0:T(8,128)} custom-call(f32[100,256]{1,0:T(8,128)S(1)} %get-tuple-element.20.table, f32[5,16,16,256]{3,2,1,0:T(8,128)S(1)} %get-tuple-element.25.state, bf16[2,240,256]{2,1,0:T(8,128)(2,1)S(1)} %copy-done.3, f32[5,16,16,256]{3,2,1,0:T(8,128)S(1)} %copy-done, f32[5,16,16,256]{3,2,1,0:T(8,128)S(1)} %copy-done.1, ...), custom_call_target="tpu_custom_call" | custom-call | tf_op jit(solution)/shard_map/second/pallas_call | solution.py:552
  (1 shorter events, 0.0 us)
Async XLA Ops:
  0.7 14.7 %copy-start.4 = (f32[3,2,5,5]{3,1,2,0:T(2,128)S(1)}, f32[3,2,5,5]{3,1,2,0:T(2,128)}, u32[]{:S(2)}) copy-start(f32[3,2,5,5]{3,1,2,0:T(2,128)} %param.12) | copy-start | bytes 1804
  0.7 14.8 %copy-start = (f32[5,16,16,256]{3,2,1,0:T(8,128)S(1)}, f32[5,16,16,256]{3,2,1,0:T(8,128)}, u32[]{:S(2)}) copy-start(f32[5,16,16,256]{3,2,1,0:T(8,128)} %q_now.5) | copy-start | bytes 3932164
  0.7 14.8 %copy-start.1 = (f32[5,16,16,256]{3,2,1,0:T(8,128)S(1)}, f32[5,16,16,256]{3,2,1,0:T(8,128)}, u32[]{:S(2)}) copy-start(f32[5,16,16,256]{3,2,1,0:T(8,128)} %q_prev.3) | copy-start | bytes 3932164
  0.7 14.8 %copy-start.2 = (f32[16,16,256]{2,1,0:T(8,128)S(1)}, f32[16,16,256]{2,1,0:T(8,128)}, u32[]{:S(2)}) copy-start(f32[16,16,256]{2,1,0:T(8,128)} %jac.5) | copy-start | bytes 786436
  7.7 13.4 %all-to-all-start = ((f32[32,8,128]{2,1,0:T(8,128)}), f32[32,8,128]{2,1,0:T(8,128)S(1)}, u32[]{:S(2)}, u32[]{:S(2)}) async-start(f32[32,8,128]{2,1,0:T(8,128)} %get-tuple-element.21), calls=%async_computation | async-start | bytes 262144 | tf_op jit(solution)/shard_map/all_to_all | solution.py:507
  14.0 7.0 %collective-permute-start = (f32[5,16,256]{2,1,0:T(8,128)S(1)}, f32[5,16,256]{2,1,0:T(8,128)S(1)}, u32[]{:S(2)}, u32[]{:S(2)}) collective-permute-start(f32[5,16,256]{2,1,0:T(8,128)S(1)} %get-tuple-element.23), channel_id=1, source_target_pairs={{0,1},{1,0},{2,3},{3,2},{4,5},{5,4},{6,7},{7,6},{8,9},{9,8},{10,11... | collective-permute-start | bytes 245768 | tf_op jit(solution)/shard_map/ppermute | solution.py:435
  15.3 5.8 %collective-permute-start.1 = (f32[5,16,256]{2,1,0:T(8,128)S(1)}, f32[5,16,256]{2,1,0:T(8,128)S(1)}, u32[]{:S(2)}, u32[]{:S(2)}) collective-permute-start(f32[5,16,256]{2,1,0:T(8,128)S(1)} %get-tuple-element.24), channel_id=1, source_target_pairs={{0,8},{1,2},{2,1},{3,4},{4,3},{5,6},{6,5},{7,15},{8,0},{9,10},{10,... | collective-permute-start | bytes 245768 | tf_op jit(solution)/shard_map/ppermute | solution.py:435
  25.0 8.4 %collective-permute-start.2 = (f32[12,16,256]{2,1,0:T(8,128)S(1)}, f32[12,16,256]{2,1,0:T(8,128)S(1)}, u32[]{:S(2)}, u32[]{:S(2)}) collective-permute-start(f32[12,16,256]{2,1,0:T(8,128)S(1)} %get-tuple-element.31), channel_id=1, source_target_pairs={{0,8},{1,9},{2,10},{3,11},{4,12},{5,13},{6,14},{7,15},{8,0},{9,1},... | collective-permute-start | bytes 589832 | tf_op jit(solution)/shard_map/ppermute | solution.py:435
  25.9 7.5 %collective-permute-start.3 = (f32[12,16,256]{2,1,0:T(8,128)S(1)}, f32[12,16,256]{2,1,0:T(8,128)S(1)}, u32[]{:S(2)}, u32[]{:S(2)}) collective-permute-start(f32[12,16,256]{2,1,0:T(8,128)S(1)} %get-tuple-element.32), channel_id=1, source_target_pairs={{0,2},{1,3},{2,0},{3,1},{4,6},{5,7},{6,4},{7,5},{8,16},{9,17},{10,... | collective-permute-start | bytes 589832 | tf_op jit(solution)/shard_map/ppermute | solution.py:435
  27.1 4.5 %collective-permute-start.4 = (f32[88,256]{1,0:T(8,128)S(1)}, f32[88,256]{1,0:T(8,128)S(1)}, u32[]{:S(2)}, u32[]{:S(2)}) collective-permute-start(f32[88,256]{1,0:T(8,128)S(1)} %get-tuple-element.33), channel_id=1, source_target_pairs={{0,1},{1,0},{2,3},{3,2},{4,5},{5,4},{6,7},{7,6},{8,9},{9,8},{10,11... | collective-permute-start | bytes 270344 | tf_op jit(solution)/shard_map/ppermute | solution.py:435
  27.8 5.5 %collective-permute-start.5 = (f32[88,256]{1,0:T(8,128)S(1)}, f32[88,256]{1,0:T(8,128)S(1)}, u32[]{:S(2)}, u32[]{:S(2)}) collective-permute-start(f32[88,256]{1,0:T(8,128)S(1)} %get-tuple-element.34), channel_id=1, source_target_pairs={{0,8},{1,2},{2,1},{3,4},{4,3},{5,6},{6,5},{7,15},{8,0},{9,10},{10,... | collective-permute-start | bytes 270344 | tf_op jit(solution)/shard_map/ppermute | solution.py:435
  28.0 5.3 %copy-start.3 = (bf16[2,240,256]{2,1,0:T(8,128)(2,1)S(1)}, bf16[2,240,256]{2,1,0:T(8,128)(2,1)}, u32[]{:S(2)}) copy-start(bf16[2,240,256]{2,1,0:T(8,128)(2,1)} %get-tuple-element.26.weights) | copy-start | bytes 737284
